TPU v7x, 128 devices: a whole 4x4x4 slice. The times are simulated.
128 devices in a mesh: sp: 4 (over x), fsdp: 32 (over z, y, core).
Axes of the slice: x: 4, y: 4, z: 4, core: 2. Of those that a mesh axis runs over, the one named last changes fastest.
Arguments:
- x: bfloat16 [32, 2048, 2048], P('fsdp', 'sp')
- grad_y: bfloat16 [32, 2048, 2048], P('fsdp', 'sp')
- w_q: bfloat16 [2048, 2048], P('fsdp')
- w_k: bfloat16 [2048, 2048], P('fsdp')
- w_v: bfloat16 [2048, 2048], P('fsdp')
- w_o: bfloat16 [2048, 2048], P('fsdp')
- q_norm_w: float32 [2048], P('fsdp')
- k_norm_w: float32 [2048], P('fsdp')
- post_norm_w: float32 [2048], P('fsdp')
Outputs:
- output 1: bfloat16 [32, 2048, 2048], P('fsdp', 'sp')
- output 2: bfloat16 [32, 2048, 2048], P('fsdp', 'sp')
- output 3: float32 [2048, 2048], P('fsdp')
- output 4: float32 [2048, 2048], P('fsdp')
- output 5: float32 [2048, 2048], P('fsdp')
- output 6: float32 [2048, 2048], P('fsdp')
- output 7: float32 [2048], P('fsdp')
- output 8: float32 [2048], P('fsdp')
- output 9: float32 [2048], P('fsdp')
All inputs are finite; a program needn't handle non-finite values.
Results may differ from a plain program's by a relative error of at most 0.0131566.
Values are sent between devices in bfloat16 or wider.
A program may use at most 1 GiB of HBM per device.

v0:
```python
import functools
import math

import jax
import jax.numpy as jnp
import numpy as np
from jax import lax
from jax.experimental import pallas as pl
from jax.experimental.pallas import tpu as pltpu
from jax.sharding import Mesh, PartitionSpec as P

HEAD_DIM = 128
RMS_EPSILON = 1e-6
ROPE_THETA = 500000.0
SM_SCALE = HEAD_DIM ** -0.5
LOG2_SCALE = SM_SCALE * math.log2(math.e)
NT = (((1,), (1,)), ((), ()))
NN = (((1,), (0,)), ((), ()))
FS = ('z', 'y', 'core')
MESH = pl.DeviceIdType.MESH
BLK = 512
TILE = 128
WIDTH = 2048
SEQ = 2048
RING = (1, 2, 3)
GROUP = 32
HALF = 768
QKV = 1536
NSP = 4
QUAD = range(NSP)
ROWS = 64
F32 = jnp.float32
BF16 = jnp.bfloat16
TN = (((0,), (0,)), ((), ()))
VMEM_LIMIT = 62 * 2 ** 20
SUB = 8
WIDE = 256
PART = 16
SIDES = (1, 3)
HALF_HEAD = 64
STEPS = 64
MIB = 2 ** 20
PAIR = range(2)
TRIO = range(3)


def repeat(count, body):
    lax.fori_loop(0, count, body, 0)


def parity(value):
    return lax.rem(value, 2)


def before(d):
    return d - 1


def plus(total, part):
    return part if total is None else total + part


def other_core(core):
    return 1 - core


def row_sum(values):
    return jnp.sum(values, axis=0, keepdims=True)


def my_coords():
    return lax.axis_index('sp'), lax.axis_index('z'), lax.axis_index('y'), lax.axis_index('core')


def fsdp_index():
    sp, z, y, core = my_coords()
    return z * SUB + y * 2 + core


def fsdp_peer(step):
    sp = lax.axis_index('sp')
    f = lax.rem(fsdp_index() + step, GROUP)
    return f, (sp, f // SUB, mod4(f // 2), parity(f))


def mod4(value):
    return lax.rem(value, NSP)


def ring_sp(d):
    sp, z, y, core = my_coords()
    return mod4(sp + d), z, y, core


def ring_z(d):
    sp, z, y, core = my_coords()
    return sp, mod4(z + d), y, core


def ring_y(d):
    sp, z, y, core = my_coords()
    return sp, z, mod4(y + d), core


def partner():
    sp, z, y, core = my_coords()
    return sp, z, y, other_core(core)


def loop(count, body):
    def step(i, carry):
        body(i)
        return carry

    lax.fori_loop(0, count, step, 0)


def step_offset(t):
    return jnp.where(t == 0, 2, jnp.where(t == 1, 1, jnp.where(t == 2, 3, 0)))


def local_gains(gt_ref, grow):
    lane = lax.broadcasted_iota(jnp.int32, (1, TILE), 1) < HALF_HEAD
    first = lax.axis_index('sp') * SUB
    for h in QUAD:
        for m in PAIR:
            grow[m:m + 1, h * TILE:(h + 1) * TILE] = jnp.where(lane, gt_ref[first + 2 * h, m:m + 1, :], gt_ref[first + 2 * h + 1, m:m + 1, :])


def inv_columns(inv_ref, invc):
    for m in PAIR:
        for i in QUAD:
            invc[m, i] = jnp.broadcast_to(inv_ref[m * NSP + i:m * NSP + i + 1, :], (TILE, BLK)).T


def remote(src, dst, send, recv, peer):
    return pltpu.make_async_remote_copy(src_ref=src, dst_ref=dst, send_sem=send, recv_sem=recv, device_id=peer, device_id_type=MESH)


def greet_all():
    barrier = pltpu.get_barrier_semaphore()
    for step in range(1, GROUP):
        pl.semaphore_signal(barrier, device_id=fsdp_peer(step)[1], device_id_type=MESH)
    for d in RING:
        pl.semaphore_signal(barrier, device_id=ring_sp(d), device_id_type=MESH)
    pl.semaphore_wait(barrier, 34)


def fill_rope(ca_ref, sa_ref, cb_ref, sb_ref, cos_scr, sin_scr):
    half = lax.broadcasted_iota(jnp.int32, (ROWS, HEAD_DIM), 1) < HALF_HEAD

    def fill(a, carry):
        rows = pl.ds(pl.multiple_of(a * ROWS, ROWS), ROWS)
        ca, sa, cb, sb = ca_ref[pl.ds(a, 1), :], sa_ref[pl.ds(a, 1), :], cb_ref[:, :], sb_ref[:, :]
        cos_scr[rows, :] = ca * cb - sa * sb
        sine = sa * cb + ca * sb
        sin_scr[rows, :] = jnp.where(half, -sine, sine)
        return carry

    repeat(GROUP, fill)


def drain(sized, *sems):
    for sem in sems:
        pltpu.make_async_copy(sized, sized, sem).wait()


def gather_stages(buf, g, sems):
    sp, z, y, core = my_coords()
    a1_send, a1_recv, b1_send, b1_recv, near_send, near_recv, far_send, far_recv, c_send, c_recv = sems
    low, high = pl.ds(0, GROUP), pl.ds(GROUP, GROUP)
    ways = tuple(enumerate(SIDES))

    def first(d):
        own_low, own_high = buf.at[z, y, core, low], buf.at[z, y, core, high]
        return (remote(own_low, own_low, a1_send.at[g, before(d)], a1_recv.at[g, before(d)], ring_z(d)),
                remote(own_high, own_high, b1_send.at[g, before(d)], b1_recv.at[g, before(d)], ring_y(d)))

    def send_near(e):
        along_y, along_z = buf.at[mod4(z + NSP - e), y, core, low], buf.at[z, mod4(y + NSP - e), core, high]
        for i, d in ways:
            remote(along_y, along_y, near_send.at[g, i], near_recv.at[g, i], ring_y(d)).start()
            remote(along_z, along_z, near_send.at[g, 2 + i], near_recv.at[g, 2 + i], ring_z(d)).start()

    def across(e):
        piece = buf.at[mod4(z + NSP - e), :, core]
        return remote(piece, piece, c_send.at[g, e], c_recv.at[g, e], partner())

    def begin():
        for d in RING:
            for copy in first(d):
                copy.start()
        send_near(0)

    def pass_on():
        for e in RING:
            for copy in first(e):
                copy.wait()
            send_near(e)

    def relay():
        for i, d in ways:
            drain(buf.at[:, y, core, low], near_send.at[g, i], near_recv.at[g, i])
            piece = buf.at[:, mod4(y + NSP - d), core, pl.ds(i * PART, PART)]
            remote(piece, piece, far_send.at[g, i], far_recv.at[g, i], ring_y(d)).start()
            drain(buf.at[z, :, core, high], near_send.at[g, 2 + i], near_recv.at[g, 2 + i])
            piece = buf.at[mod4(z + NSP - d), :, core, pl.ds(GROUP + i * PART, PART)]
            remote(piece, piece, far_send.at[g, 2 + i], far_recv.at[g, 2 + i], ring_z(d)).start()

    def share():
        for i, d in ways:
            drain(buf.at[:, y, core, pl.ds(0, PART)], far_send.at[g, i], far_recv.at[g, i])
            drain(buf.at[z, :, core, pl.ds(0, PART)], far_send.at[g, 2 + i], far_recv.at[g, 2 + i])
        for e in QUAD:
            across(e).start()

    def finish():
        for e in QUAD:
            across(e).wait()

    return begin, pass_on, relay, share, finish


def gather_sems(groups):
    return dma_sems((groups, 3), (groups, 3), (groups, NSP), (groups, NSP), (groups, NSP))


def norm_and_grad(acc, x, grad_y, gain, y_out, grad_out, post):
    post[:, :] = jnp.zeros_like(post)

    def chunk(r):
        rows = pl.ds(pl.multiple_of(r * ROWS, ROWS), ROWS)
        a = jnp.concatenate([acc[n, rows, :].astype(BF16).astype(F32) for n in QUAD], axis=1)
        inv = lax.rsqrt(jnp.sum(a * a, axis=1, keepdims=True) / WIDTH + RMS_EPSILON)
        a_hat = a * inv
        grad = grad_y[rows, :].astype(F32)
        y_out[rows, :] = (x[rows, :].astype(F32) + a_hat * gain).astype(BF16)
        post[:, :] += jnp.sum((grad * a_hat).reshape(ROWS // SUB, SUB, WIDTH), axis=0)
        grad = grad * gain
        grad_out[rows, :] = (inv * (grad - a_hat * (jnp.sum(grad * a_hat, axis=1, keepdims=True) / WIDTH))).astype(BF16)

    loop(BLK // ROWS, chunk)


def fwd_kernel(x_hbm, gy_hbm, wq_hbm, wk_hbm, wv_hbm, wo_hbm, tile_ref, ca_ref, sa_ref, cb_ref, sb_ref,
               xf_hbm, q0_hbm, k0_hbm, qr_hbm, kr_hbm, v_hbm, o_hbm, ot_hbm, lse_hbm, y_hbm, ga_hbm, ds_hbm, wl_hbm, wa_hbm, wb_hbm, wc_hbm,
               inv_hbm, gt_hbm, post_hbm,
               inv_ref, gt_ref, post_ref, xf, wl, wo, q0, k0, v, qr, kr, o, ot, lse, s_scr, vt_scr, cos_scr, sin_scr, st, st_in, grow, gpost, invc,
               ld_sem, out_sem, own_send, own_recv, fw_send, fw_recv, t_send, t_recv, u_send, u_recv, o_send, o_recv, *w_sems):
    sp, z, y, core = my_coords()
    me = fsdp_index()
    right, left = ring_sp(1), ring_sp(3)
    far = mod4(sp + 2)
    w_rows = (wq_hbm, wk_hbm, wv_hbm)

    def own_cols(d):
        return pl.ds(pl.multiple_of(mod4(sp + d) * BLK, BLK), BLK)

    loads = []
    for g, buf in enumerate((wl, wa_hbm, wb_hbm, wc_hbm)):
        for m, w_hbm in enumerate(w_rows):
            loads.append(pltpu.make_async_copy(w_hbm.at[:, own_cols(g)], buf.at[z, y, core, :, pl.ds(m * BLK, BLK)], ld_sem.at[g * 3 + m]))
    loads.append(pltpu.make_async_copy(wo_hbm, wo.at[z, y, core], ld_sem.at[12]))
    loads.append(pltpu.make_async_copy(x_hbm, xf.at[sp], ld_sem.at[13]))
    for load in loads:
        load.start()
    greet_all()

    def chunk(c):
        return pl.ds(pl.multiple_of(c * TILE, TILE), TILE)

    def own_x(side, c):
        return remote(x_hbm.at[chunk(c)], xf.at[sp, chunk(c)], own_send.at[side, c], own_recv.at[side, c], (right, left)[side])

    for right_c, left_c in zip((0, 2, 1, 3), (1, 3, 0, 2)):
        own_x(0, right_c).start()
        own_x(1, left_c).start()

    tile_sends = []
    for step in range(1, GROUP):
        tile_sends.append(remote(tile_ref, gt_ref.at[me], t_send.at[0], t_recv.at[0], fsdp_peer(step)[1]))
    for load in loads[:3]:
        load.wait()
    stages = [gather_stages(buf, g, w_sems) for g, buf in enumerate((wl, wo, wa_hbm, wb_hbm, wc_hbm))]

    def begin(g):
        stages[g][0]()

    def pass_on(g):
        stages[g][1]()

    def relay(g):
        stages[g][2]()

    def share(g):
        stages[g][3]()

    def gathered(g):
        stages[g][NSP]()

    begin(0)
    for copy in tile_sends:
        copy.start()
    gt_ref[me] = tile_ref[:, :]
    fill_rope(ca_ref, sa_ref, cb_ref, sb_ref, cos_scr, sin_scr)
    pass_on(0)

    def forward(side, i):
        block = mod4(sp + (3, 1)[side])
        piece = xf.at[block, chunk(2 * i + side)]
        return remote(piece, piece, fw_send.at[side, i], fw_recv.at[side, i], (right, left)[side])

    def forward_x(i):
        for side in PAIR:
            own_x(side, 2 * i + side).wait()
            forward(side, i).start()

    forward_x(0)
    relay(0)
    for load in loads[3:]:
        load.wait()
    for g in RING + (NSP,):
        begin(g)
    share(0)
    forward_x(1)
    pass_on(1)
    gathered(0)
    st[:, :] = jnp.zeros_like(st)

    def project(block, i):
        rows = pl.ds(pl.multiple_of(i * WIDE, WIDE), WIDE)
        tokens = xf[block, rows, :]
        for n, dst in enumerate((q0, k0, v)):
            weight = wl[:, :, :, :, n * BLK:(n + 1) * BLK].reshape(WIDTH, BLK)
            out = jnp.dot(tokens, weight, preferred_element_type=F32).astype(BF16)
            dst[block, rows, :] = out
            if n < 2:
                wide = out.astype(F32)
                wide = wide * wide
                part = (wide[:, :TILE] + wide[:, TILE:WIDE]) + (wide[:, WIDE:3 * TILE] + wide[:, 3 * TILE:])
                mine = lax.broadcasted_iota(jnp.int32, (SUB, WIDE), 0) == n * NSP + block
                st[:, rows] = jnp.where(mine, row_sum(part.T), st[:, rows])

    def near(step):
        k, i = step // 2, parity(step)
        for side in PAIR:
            @pl.when(k == 2 - side)
            def _():
                own_x(side, 2 * i + 1 - side).wait()

        project(mod4(sp + k + lax.select(k == 2, 1, 0)), i)

    def distant(i):
        for side in PAIR:
            forward(side, i).wait()
        project(far, i)

    loop(6, near)
    relay(1)
    for g in (2, 3, NSP):
        pass_on(g)
    loop(2, distant)
    stats = [remote(st, st_in.at[before(d)], u_send.at[before(d)], u_recv.at[before(d)], ring_sp(d)) for d in RING]
    for copy in stats:
        copy.start()
    stores = [pltpu.make_async_copy(src, dst, out_sem.at[i]) for i, (src, dst) in enumerate(((xf, xf_hbm), (q0, q0_hbm), (k0, k0_hbm), (v, v_hbm), (wl, wl_hbm)))]
    for copy in stores:
        copy.start()
    relay(2)
    share(1)
    drain(gt_ref.at[pl.ds(1, GROUP - 1)], t_send.at[0], t_recv.at[0])
    local_gains(gt_ref, grow)
    lane = lax.broadcasted_iota(jnp.int32, (1, TILE), 1) < HALF_HEAD
    for i in range(WIDTH // TILE):
        gpost[:, i * TILE:(i + 1) * TILE] = jnp.broadcast_to(jnp.where(lane, gt_ref[2 * i, 2:3, :], gt_ref[2 * i + 1, 2:3, :]), (SUB, TILE))
    for copy in stats:
        copy.wait()
    total = (st[:, :] + st_in[0]) + (st_in[1] + st_in[2])
    inv_ref[:, :] = lax.rsqrt(total / WIDTH + RMS_EPSILON)

    inv_columns(inv_ref, invc)
    row = lax.broadcasted_iota(jnp.int32, (BLK, BLK), 0)
    col = lax.broadcasted_iota(jnp.int32, (BLK, BLK), 1)

    def send_o(h, d):
        lanes = pl.ds(pl.multiple_of(h * TILE, TILE), TILE)
        return remote(o.at[mod4(sp + d), :, lanes], ot.at[sp, :, lanes], o_send.at[h, before(d)], o_recv.at[h, before(d)], ring_sp(d))

    def head(h, carry):
        lanes = pl.ds(pl.multiple_of(h * TILE, TILE), TILE)
        for i in QUAD:
            rows = slice(i * BLK, (i + 1) * BLK)
            for m, (src, dst) in enumerate(((q0, qr), (k0, kr))):
                u = src[i, :, lanes].astype(F32) * invc[m, i] * grow[m:m + 1, lanes]
                dst[i, :, lanes] = (u * cos_scr[rows, :] + pltpu.roll(u, HALF_HEAD, 1) * sin_scr[rows, :]).astype(BF16)
        vt_scr[:, :] = v[:, :, lanes].reshape(SEQ, TILE).T
        for i in QUAD:
            q_i = qr[i, :, lanes]
            buf = i % 2
            top = None
            for j in range(i + 1):
                s = lax.dot_general(kr[j, :, lanes], q_i, NT, preferred_element_type=F32)
                if j == i:
                    s = jnp.where(row <= col, s, -1e30)
                s_scr[buf, j] = s
                part = jnp.max(s.reshape(STEPS, SUB, BLK), axis=0)
                top = part if top is None else jnp.maximum(top, part)
            m = jnp.max(top, axis=0, keepdims=True) * LOG2_SCALE
            tot = None
            for j in range(i + 1):
                e = jnp.exp2(s_scr[buf, j] * LOG2_SCALE - m)
                s_scr[buf, j] = e
                part = jnp.sum(e.reshape(STEPS, SUB, BLK), axis=0)
                tot = plus(tot, part)
            l = row_sum(tot)
            r = 1.0 / l
            acc = None
            for j in range(i + 1):
                p = (s_scr[buf, j] * r).astype(BF16)
                part = lax.dot_general(vt_scr[:, j * BLK:(j + 1) * BLK], p, NN, preferred_element_type=F32)
                acc = plus(acc, part)
            o[i, :, lanes] = acc.T.astype(BF16)
            lse[h, :, i * BLK:(i + 1) * BLK] = jnp.broadcast_to(m + jnp.log2(l), (SUB, BLK))
        for d in RING:
            send_o(h, d).start()
        return carry

    repeat(NSP, head)
    for copy in stores:
        copy.wait()
    ot[sp] = o[sp]
    relay(3)
    relay(NSP)
    share(2)
    last = [pltpu.make_async_copy(o, o_hbm, out_sem.at[0]), pltpu.make_async_copy(lse, lse_hbm, out_sem.at[1]),
            pltpu.make_async_copy(qr, qr_hbm, out_sem.at[6]), pltpu.make_async_copy(kr, kr_hbm, out_sem.at[7])]
    grad_in = pltpu.make_async_copy(gy_hbm, xf.at[mod4(sp + 1)], ld_sem.at[0])
    for copy in last + [grad_in]:
        copy.start()
    gathered(1)
    acc = s_scr.at[0]

    def project_out(h):
        for d in RING:
            send_o(h, d).wait()
        lanes = pl.ds(pl.multiple_of(h * TILE, TILE), TILE)
        mine = jnp.concatenate([ot[s, :, lanes] for s in QUAD], axis=1)
        for n in QUAD:
            part = jnp.dot(mine, wo[:, h, :, :, n * BLK:(n + 1) * BLK].reshape(BLK, BLK), preferred_element_type=F32)

            @pl.when(h == 0)
            def _():
                acc[n] = part

            @pl.when(h > 0)
            def _():
                acc[n] += part

    loop(NSP, project_out)
    share(3)
    share(NSP)
    grad_in.wait()
    last.append(pltpu.make_async_copy(ot, ot_hbm, out_sem.at[2]))
    last[-1].start()
    y_out, grad_a = xf.at[far], xf.at[mod4(sp + 3)]
    norm_and_grad(acc, xf.at[sp], xf.at[mod4(sp + 1)], gpost[0:1, :], y_out, grad_a, post_ref)
    for i, (src, dst) in enumerate(((y_out, y_hbm), (grad_a, ga_hbm), (inv_ref, inv_hbm), (gt_ref, gt_hbm), (post_ref, post_hbm))):
        last.append(pltpu.make_async_copy(src, dst, out_sem.at[SUB + i]))
        last[-1].start()

    def grad_attn(h):
        out = lax.dot_general(grad_a[:, :], wo[:, h].reshape(BLK, WIDTH), NT, preferred_element_type=F32).astype(BF16)
        for s in QUAD:
            v[s, :, pl.ds(pl.multiple_of(h * TILE, TILE), TILE)] = out[:, s * TILE:(s + 1) * TILE]

    loop(NSP, grad_attn)
    gathered(2)
    gathered(3)
    last.append(pltpu.make_async_copy(v, ds_hbm, out_sem.at[5]))
    last[-1].start()
    gathered(NSP)
    for copy in last:
        copy.wait()


def dma_sems(*shapes):
    return [pltpu.SemaphoreType.DMA(shape) for shape in shapes for _ in PAIR]


def forward_pass(x, grad_y, wq_rows, wk_rows, wv_rows, wo_rows, gain_tile, tables):
    hbm = pl.BlockSpec(memory_space=pl.ANY)
    vmem = pl.BlockSpec(memory_space=pltpu.VMEM)
    quad = (NSP, BLK, BLK)
    wide = jax.ShapeDtypeStruct(quad, BF16)
    tokens = jax.ShapeDtypeStruct((BLK, WIDTH), BF16)
    blocks = (NSP, NSP, 2, ROWS)
    weight = jax.ShapeDtypeStruct(blocks + (QKV,), BF16)
    return pl.pallas_call(
        fwd_kernel,
        out_shape=[jax.ShapeDtypeStruct((NSP, BLK, WIDTH), BF16)] + [wide] * 7 + [jax.ShapeDtypeStruct((NSP, SUB, SEQ), F32), tokens, tokens, wide] + [weight] * NSP + [
            jax.ShapeDtypeStruct((SUB, BLK), F32), jax.ShapeDtypeStruct((GROUP, SUB, TILE), F32), jax.ShapeDtypeStruct((SUB, WIDTH), F32)],
        in_specs=[hbm] * 6 + [vmem] * 5, out_specs=[hbm] * 19,
        scratch_shapes=[pltpu.VMEM((SUB, BLK), F32), pltpu.VMEM((GROUP, SUB, TILE), F32), pltpu.VMEM((SUB, WIDTH), F32), pltpu.VMEM((NSP, BLK, WIDTH), BF16), pltpu.VMEM(blocks + (QKV,), BF16), pltpu.VMEM(blocks + (WIDTH,), BF16)] + [pltpu.VMEM(quad, BF16)] * 7 + [
            pltpu.VMEM((NSP, SUB, SEQ), F32), pltpu.VMEM((2,) + quad, F32), pltpu.VMEM((TILE, SEQ), BF16),
            pltpu.VMEM((SEQ, TILE), F32), pltpu.VMEM((SEQ, TILE), F32), pltpu.VMEM((SUB, BLK), F32), pltpu.VMEM((3, SUB, BLK), F32), pltpu.VMEM((SUB, BLK), F32),
            pltpu.VMEM((SUB, WIDTH), F32), pltpu.VMEM((2, NSP, BLK, TILE), F32),
            pltpu.SemaphoreType.DMA((14,)), pltpu.SemaphoreType.DMA((13,))] + dma_sems((2, NSP), (2, 2), (1,), (3,), (NSP, 3)) + gather_sems(5),
        compiler_params=pltpu.CompilerParams(collective_id=1, has_side_effects=True, vmem_limit_bytes=VMEM_LIMIT),
        cost_estimate=pl.CostEstimate(flops=80_000_000_000, bytes_accessed=40 * MIB, transcendentals=0),
        name='forward')(x, grad_y, wq_rows, wk_rows, wv_rows, wo_rows, gain_tile, *tables)


def mid_kernel(ot_hbm, ga_hbm, ds_hbm, qr_hbm, kr_hbm, v_hbm, o_hbm, q0_hbm, k0_hbm, lse_hbm, inv_ref, gt_ref, post_ref,
               ca_ref, sa_ref, cb_ref, sb_ref, d_hbm, as_hbm, bs_hbm, dvt_hbm, tile_hbm,
               tile_ref, ot, ga, gap, ott, do, qa, ka, va, oa, q0, k0, otp, big, chip, half_y, half_z, full_y, full_z, invc, cos_scr, sin_scr,
               dk_scr, dv_scr, kt_scr, lse, grow, gacc, st, st_in,
               in_sem, out_sem, do_send, do_recv, c_send, c_recv, a1_send, a1_recv, b1_send, b1_recv, a2_send, a2_recv, b2_send, b2_recv,
               u_send, u_recv, v_send, v_recv):
    sp, z, y, core = my_coords()

    def block_cols(n):
        return pl.ds(n * BLK, BLK)

    def lanes_of(h):
        return pl.ds(pl.multiple_of(h * TILE, TILE), TILE)

    def group(pairs, sem):
        copies = [pltpu.make_async_copy(src, dst, sem.at[i]) for i, (src, dst) in enumerate(pairs)]
        for copy in copies:
            copy.start()
        return copies

    load_ot = group([(ot_hbm, ot), (ga_hbm, ga)], in_sem.at[0])

    barrier = pltpu.get_barrier_semaphore()
    greeted = [ring(d) for ring in (ring_sp, ring_z, ring_y) for d in RING] + [partner()]
    for peer in greeted:
        pl.semaphore_signal(barrier, device_id=peer, device_id_type=MESH)
    pl.semaphore_wait(barrier, len(greeted))

    def send_do(h, d):
        return remote(ds_hbm.at[mod4(sp + d), :, lanes_of(h)], do.at[sp, :, lanes_of(h)], do_send.at[h, d], do_recv.at[h, d], ring_sp(d))

    send_grad = remote(ga_hbm, gap, c_send.at[NSP], c_recv.at[NSP], partner())
    send_grad.start()
    for h in QUAD:
        for d in RING:
            send_do(h, d).start()
    load_qk = group([(ds_hbm.at[sp], do.at[sp]), (qr_hbm, qa), (kr_hbm, ka), (v_hbm, va), (o_hbm, oa), (lse_hbm, lse), (q0_hbm, q0), (k0_hbm, k0)], in_sem.at[2])
    for copy in load_ot:
        copy.wait()

    def core_rows(i, c):
        return pl.ds(pl.multiple_of(i * TILE + c * ROWS, ROWS), ROWS)

    def send_core(i):
        return remote(ott.at[:, core_rows(i, other_core(core))], otp.at[:, i], c_send.at[i], c_recv.at[i], partner())

    for s in QUAD:
        ott[s] = ot[s].T
    for i in QUAD:
        send_core(i).start()
    local_gains(gt_ref, grow)
    fill_rope(ca_ref, sa_ref, cb_ref, sb_ref, cos_scr, sin_scr)
    inv_columns(inv_ref, invc)
    gacc[:, :, :] = jnp.zeros_like(gacc)

    def step_z(t):
        return mod4(z + step_offset(t))

    low, high = pl.ds(0, 2), pl.ds(2, 2)
    ways = tuple(enumerate(SIDES))

    def half_a(t, i, d):
        return remote(chip.at[t, i, mod4(y + 2)], half_y.at[t, i], a1_send.at[t, i], a1_recv.at[t, i], ring_y(d))

    def half_b(k, i, d):
        return remote(chip.at[0, 2 + i, k], half_z.at[k, i], b1_send.at[k, i], b1_recv.at[k, i], ring_z(d))

    def sum_a(t, i, d):
        return remote(chip.at[t, low, mod4(y + d)], full_y.at[i, t], a2_send.at[t, i], a2_recv.at[t, i], ring_y(d))

    def sum_b(k, i, d):
        return remote(chip.at[1 + i, high, k], full_z.at[i, k], b2_send.at[k, i], b2_recv.at[k, i], ring_z(d))

    def pass_on(t):
        for i, d in ways:
            half_a(t, i, d).wait()
            chip[t, i, mod4(y + d)] += half_y[t, i]
            half_b(t, i, d).wait()
            chip[1 + i, 2 + i, t] += half_z[t, i]
        for i, d in ways:
            sum_a(t, i, d).start()
            sum_b(t, i, d).start()

    send_grad.wait()
    for i in QUAD:
        send_core(i).wait()

    def wgrad(t):
        block = step_z(t)
        mine = jnp.concatenate([ott[block, core_rows(i, core), :] for i in QUAD], axis=0)
        other = otp[block].reshape(NSP * ROWS, BLK)
        for n in QUAD:
            cols = slice(n * BLK, (n + 1) * BLK)
            part = jnp.dot(mine, ga[:, cols], preferred_element_type=F32) + jnp.dot(other, gap[:, cols], preferred_element_type=F32)
            chip[t, n] = part.reshape(NSP, ROWS, BLK)
        for i, d in ways:
            half_a(t, i, d).start()

        @pl.when(t == 0)
        def _():
            for k in QUAD:
                for i, d in ways:
                    half_b(k, i, d).start()

    loop(NSP, wgrad)
    for copy in load_qk:
        copy.wait()

    row = lax.broadcasted_iota(jnp.int32, (BLK, BLK), 0)
    col = lax.broadcasted_iota(jnp.int32, (BLK, BLK), 1)

    def unrotate(grad, i, m, lanes, kept):
        rows = slice(i * BLK, (i + 1) * BLK)
        grad = grad * cos_scr[rows, :] - pltpu.roll(grad, HALF_HEAD, 1) * sin_scr[rows, :]
        hat = kept[i, :, lanes].astype(F32) * invc[m, i]
        gacc[m, :, lanes] += jnp.sum((grad * hat).reshape(STEPS, SUB, TILE), axis=0)
        big[m, i, :, lanes] = grad * grow[m:m + 1, lanes]

    def send_dv(h, d):
        return remote(va.at[mod4(sp + d), :, lanes_of(h)], dvt_hbm.at[sp, :, lanes_of(h)], v_send.at[h, d], v_recv.at[h, d], ring_sp(d))

    def head(h):
        lanes = lanes_of(h)
        for d in RING:
            send_do(h, d).wait()

        @pl.when(h > 0)
        def _():
            for d in RING:
                send_dv(h - 1, d).start()

        kt_scr[:, :] = ka[:, :, lanes].reshape(SEQ, TILE).T
        for i in QUAD:
            q_i, do_i = qa[i, :, lanes], do[i, :, lanes]
            delta = row_sum((do_i.astype(F32) * oa[i, :, lanes].astype(F32)).T)
            top = lse[h, 0:1, i * BLK:(i + 1) * BLK]
            dqt = None
            for j in range(i + 1):
                s = lax.dot_general(ka[j, :, lanes], q_i, NT, preferred_element_type=F32)
                p = jnp.exp2(s * LOG2_SCALE - top)
                if j == i:
                    p = jnp.where(row <= col, p, 0.0)
                dp = lax.dot_general(va[j, :, lanes], do_i, NT, preferred_element_type=F32)
                grad_s = (p * (dp - delta)).astype(BF16)
                dv = jnp.dot(p.astype(BF16), do_i, preferred_element_type=F32)
                dk = jnp.dot(grad_s, q_i, preferred_element_type=F32)
                part = jnp.dot(kt_scr[:, j * BLK:(j + 1) * BLK], grad_s, preferred_element_type=F32)
                dqt = plus(dqt, part)
                if j == i:
                    dv_scr[j] = dv
                    dk_scr[j] = dk
                else:
                    dv_scr[j] += dv
                    dk_scr[j] += dk
            unrotate((dqt * SM_SCALE).T, i, 0, lanes, q0)
        for i in QUAD:
            unrotate(dk_scr[i] * SM_SCALE, i, 1, lanes, k0)
            va[i, :, lanes] = dv_scr[i].astype(BF16)
        pass_on(h)

    loop(NSP, head)
    kept = (q0, k0)
    for m, ref in enumerate(kept):
        for i in QUAD:
            part = None
            for h in QUAD:
                lanes = slice(h * TILE, (h + 1) * TILE)
                term = big[m, i, :, lanes] * ref[i, :, lanes].astype(F32)
                part = plus(part, term)
            st[m * NSP + i:m * NSP + i + 1, :] = row_sum((part * invc[m, i]).T)
    stats = [remote(st, st_in.at[before(d)], u_send.at[d], u_recv.at[d], ring_sp(d)) for d in RING]
    for copy in stats:
        copy.start()
    for d in RING:
        send_dv(NSP - 1, d).start()
    store_v = group([(va, d_hbm.at[:, :, block_cols(2)]), (va.at[sp], dvt_hbm.at[sp])], out_sem.at[1])

    tile_ref[:, :, :] = jnp.zeros_like(tile_ref)
    for i in range(WIDTH // TILE):
        total = row_sum(post_ref[:, i * TILE:(i + 1) * TILE])
        tile_ref[2 * i, 2:3, :] = total
        tile_ref[2 * i + 1, 2:3, :] = total
    for m in PAIR:
        for h in QUAD:
            total = row_sum(gacc[m, :, h * TILE:(h + 1) * TILE])
            for c in PAIR:
                tile_ref[sp * SUB + 2 * h + c, m:m + 1, :] = total

    store_v += group([(tile_ref, tile_hbm)], out_sem.at[3])
    for copy in stats:
        copy.wait()
    st[:, :] = ((st[:, :] + st_in[0]) + (st_in[1] + st_in[2])) / WIDTH
    for m, ref in enumerate(kept):
        for i in QUAD:
            proj = jnp.broadcast_to(st[m * NSP + i:m * NSP + i + 1, :], (TILE, BLK)).T
            for h in QUAD:
                lanes = slice(h * TILE, (h + 1) * TILE)
                hat = ref[i, :, lanes].astype(F32) * invc[m, i]
                ref[i, :, lanes] = (invc[m, i] * (big[m, i, :, lanes] - hat * proj)).astype(BF16)
    store_d = group([(ref, d_hbm.at[:, :, block_cols(m)]) for m, ref in enumerate(kept)], out_sem.at[2])

    for t in QUAD:
        for i, d in ways:
            sum_a(t, i, d).wait()
            sum_b(t, i, d).wait()
        chip[t, low, y] += full_y[0, t] + full_y[1, t]
        chip[NSP - 1, high, t] += full_z[0, t] + full_z[1, t]
    store_w = group([(chip.at[t, low, y], as_hbm.at[t]) for t in QUAD] + [(chip.at[NSP - 1, high], bs_hbm)], out_sem.at[0])
    for h in QUAD:
        for d in RING:
            send_dv(h, d).wait()
    for copy in store_v + store_d + store_w:
        copy.wait()


def mid(o_tok, grad_a, grad_o, heads, lse, inv, gains, post, tables):
    hbm = pl.BlockSpec(memory_space=pl.ANY)
    vmem = pl.BlockSpec(memory_space=pltpu.VMEM)
    quad = (NSP, BLK, BLK)
    tokens = (BLK, WIDTH)
    pair = (2, ROWS, BLK)
    sems = dma_sems((NSP, NSP), (NSP + 1,), (NSP, 2), (NSP, 2), (NSP, 2), (NSP, 2), (NSP,), (NSP, NSP))
    half = [pltpu.VMEM(shape, BF16) for shape in (quad, tokens, tokens) + (quad,) * SUB + ((NSP, NSP, ROWS, BLK),)]
    scratch = half + [pltpu.VMEM(shape, F32) for shape in (
        (2,) + quad, (NSP, NSP, NSP, ROWS, BLK), (NSP,) + pair, (NSP,) + pair, (2, NSP) + pair, (2, NSP) + pair,
        (2, NSP, BLK, TILE), (SEQ, TILE), (SEQ, TILE), (NSP, BLK, TILE), (NSP, BLK, TILE))] + [pltpu.VMEM((TILE, SEQ), BF16)] + [
        pltpu.VMEM(shape, F32) for shape in ((NSP, SUB, SEQ), (SUB, BLK), (2, SUB, BLK), (SUB, BLK), (3, SUB, BLK))]
    return pl.pallas_call(
        mid_kernel,
        out_shape=[jax.ShapeDtypeStruct((NSP, BLK, QKV), BF16),
                   jax.ShapeDtypeStruct((NSP,) + pair, F32), jax.ShapeDtypeStruct((2, NSP, ROWS, BLK), F32), jax.ShapeDtypeStruct(quad, BF16),
                   jax.ShapeDtypeStruct(gains.shape, F32)],
        in_specs=[hbm] * 10 + [vmem] * 7, out_specs=[hbm] * 5,
        scratch_shapes=[pltpu.VMEM(gains.shape, F32)] + scratch + [pltpu.SemaphoreType.DMA(shape) for shape in ((3, SUB), (NSP, 5))] + sems,
        compiler_params=pltpu.CompilerParams(collective_id=2, has_side_effects=True, vmem_limit_bytes=VMEM_LIMIT),
        cost_estimate=pl.CostEstimate(flops=60_000_000_000, bytes_accessed=WIDTH * WIDTH * SUB, transcendentals=0),
        name='middle')(o_tok, grad_a, grad_o, *heads, lse, inv, gains, post, *tables)


def tail_kernel(d_hbm, x_hbm, wl_hbm, wa_hbm, wb_hbm, wc_hbm, gy_hbm, as_hbm, bs_hbm, dvt_hbm, tile_ref,
                gx_hbm, gq_hbm, gk_hbm, gv_hbm, gwo_hbm, gain_hbm, gain_ref,
                d_loc, x_col, part, chip, half_y, half_z, full_y, full_z, sum_b, recv_a2, recv_b2, d_tok, w_buf, acc, gy_buf, gw_buf, gtile, gpart, gacross,
                o_a, o_b, o_ra, o_rb, fin, rc, fout,
                ld_sem, x_sem, w_sem, out_sem, d_send, d_recv, c_send, c_recv, a1_send, a1_recv, b1_send, b1_recv,
                a2_send, a2_recv, b2_send, b2_recv, g_send, g_recv, t_send, t_recv, u_send, u_recv,
                oa_send, oa_recv, ob_send, ob_recv, s_send, s_recv, f_send, f_recv, f1_send, f1_recv, f2_send, f2_recv):
    sp, z, y, core = my_coords()
    me = fsdp_index()

    load_o = [pltpu.make_async_copy(as_hbm, o_a, ld_sem.at[2]), pltpu.make_async_copy(bs_hbm, o_b, ld_sem.at[3])]
    load_d = pltpu.make_async_copy(d_hbm, d_loc, ld_sem.at[0])
    load_gy = pltpu.make_async_copy(gy_hbm, gy_buf, ld_sem.at[1])
    load_v = [pltpu.make_async_copy(dvt_hbm.at[mod4(sp + NSP - d)], d_tok.at[before(d), :, pl.ds(2 * BLK, BLK)], ld_sem.at[3 + d]) for d in RING]
    for load in load_o + [load_d]:
        load.start()

    def step_z(t):
        return mod4(z + step_offset(t))

    def load_x(t):
        return pltpu.make_async_copy(x_hbm.at[:, pl.ds(pl.multiple_of(step_z(t) * BLK, BLK), BLK)], x_col.at[parity(t)], x_sem.at[parity(t)])

    load_x(0).start()

    def source(k):
        return jnp.where(k == 0, 0, jnp.where(k == 1, 1, jnp.where(k == 2, 3, 2)))

    def which(j):
        return lax.rem(j + 2, 3)

    w_order = (wl_hbm, wc_hbm, wa_hbm, wb_hbm)

    def load_w(j, src=wl_hbm):
        return pltpu.make_async_copy(src.at[:, pl.ds(pl.multiple_of(which(j) * BLK, BLK), BLK)], w_buf.at[lax.rem(j, 3)], w_sem.at[lax.rem(j, 3)])

    def start_w(j):
        for k, src in enumerate(w_order):
            @pl.when(j // 3 == k)
            def _():
                load_w(j, src).start()

    greet_all()
    tile_sends = []
    for step in range(1, GROUP):
        f, peer = fsdp_peer(step)
        tile_sends.append(remote(tile_ref.at[f], gtile.at[me], t_send.at[0], t_recv.at[0], peer))
        tile_sends[-1].start()
    gtile[me] = tile_ref[me]

    def send_d(d, m):
        return remote(d_hbm.at[mod4(sp + d), :, pl.ds(m * BLK, BLK)], d_tok.at[before(d), :, pl.ds(m * BLK, BLK)],
                       d_send.at[before(d), m], d_recv.at[before(d), m], ring_sp(d))

    for load in load_v + [load_gy]:
        load.start()
    start_w(0)
    start_w(1)
    for load in load_o:
        load.wait()
    low, high = pl.ds(0, 2), pl.ds(2, 2)
    o_sends = [remote(o_a.at[t], o_ra.at[t], oa_send.at[t], oa_recv.at[t], ring_z(d)) for t, d in enumerate((2, 1, 3))]
    o_sends += [remote(o_b.at[:, mod4(y + d)], o_rb.at[before(d)], ob_send.at[d], ob_recv.at[d], ring_y(d)) for d in RING]
    for copy in o_sends:
        copy.start()
    for m in PAIR:
        for d in SIDES:
            send_d(d, m).start()

    load_d.wait()

    def send_core(t):
        return remote(part.at[parity(t), :, other_core(core)], chip.at[t], c_send.at[t], c_recv.at[t], partner())

    quarter = HALF // 2
    ways = tuple(enumerate(SIDES))

    def half_a(t, i, d):
        return remote(chip.at[t, mod4(y + 2), :, pl.ds(i * quarter, quarter)], half_y.at[t, i], a1_send.at[t, i], a1_recv.at[t, i], ring_y(d))

    def half_b(i, d):
        return remote(chip.at[0, :, :, pl.ds(HALF + i * quarter, quarter)], half_z.at[i], b1_send.at[i], b1_recv.at[i], ring_z(d))

    def full_a(t, i, d):
        return remote(chip.at[t, mod4(y + d), :, pl.ds(0, HALF)], full_y.at[i, t], f1_send.at[t, i], f1_recv.at[t, i], ring_y(d))

    def full_b(i, d):
        return remote(chip.at[1 + i, :, :, pl.ds(HALF, HALF)], full_z.at[i], f2_send.at[i], f2_recv.at[i], ring_z(d))

    def pass_a(t):
        for i, d in ways:
            half_a(t, i, d).wait()
            chip[t, mod4(y + d), :, i * quarter:(i + 1) * quarter] += half_y[t, i]
            full_a(t, i, d).start()

    def pass_b():
        for i, d in ways:
            half_b(i, d).wait()
            chip[1 + i, :, :, HALF + i * quarter:HALF + (i + 1) * quarter] += half_z[i]
            full_b(i, d).start()

    def finish(t):
        send_core(t).wait()
        chip[t] += part[parity(t), :, core]
        for i, d in ways:
            half_a(t, i, d).start()

        @pl.when(t == 0)
        def _():
            for i, d in ways:
                half_b(i, d).start()

    def wgrad_step(t, carry):
        load_x(t).wait()

        @pl.when(t < 3)
        def _():
            load_x(t + 1).start()

        for n in TRIO:
            prod = lax.dot_general(x_col[parity(t)], d_loc[:, :, n * BLK:(n + 1) * BLK].reshape(WIDTH, BLK),
                                   (((0,), (0,)), ((), ())), preferred_element_type=F32)
            part[parity(t), :, :, :, n * BLK:(n + 1) * BLK] = prod.reshape(NSP, 2, ROWS, BLK)
        send_core(t).start()

        @pl.when(t > 0)
        def _():
            finish(t - 1)
        return carry

    repeat(NSP, wgrad_step)
    finish(3)
    pass_a(0)
    pass_a(1)
    pass_b()
    pass_a(2)
    for copy in o_sends:
        copy.wait()
    fin[low] = (o_a[NSP - 1] + o_ra[0]) + (o_ra[1] + o_ra[2])
    fin[high] = (o_b[:, y] + o_rb[0]) + (o_rb[1] + o_rb[2])
    scatter = [remote(fin.at[mod4(sp + d)], rc.at[before(d)], s_send.at[d], s_recv.at[d], ring_sp(d)) for d in RING]
    for copy in scatter:
        copy.start()
    for m in PAIR:
        send_d(2, m).start()
    for load in load_v + [load_gy]:
        load.wait()
    acc[...] = gy_buf[...].astype(F32)

    def gx_step(k, m, block):
        j = 3 * k + m
        load_w(j).wait()

        @pl.when(j < 10)
        def _():
            start_w(j + 2)

        def columns(n):
            cols = pl.ds(pl.multiple_of(n * 2 * BLK, 2 * BLK), 2 * BLK)
            acc[:, cols] += lax.dot_general(block, w_buf[lax.rem(j, 3), cols, :], NT, preferred_element_type=F32)

        loop(2, columns)

    def own_steps(i, carry):
        gx_step(0, i, d_loc[sp, :, pl.ds(pl.multiple_of(which(i) * BLK, BLK), BLK)])
        return carry

    repeat(3, own_steps)

    def remote_steps(k):
        d = source(k)

        def step(i, carry):
            @pl.when(i > 0)
            def _():
                send_d(d, i - 1).wait()

            gx_step(k, i, d_tok[before(d), :, pl.ds(pl.multiple_of(which(i) * BLK, BLK), BLK)])
            return carry
        repeat(3, step)

    def send_a2(t):
        return remote(chip.at[t, y, :, pl.ds(0, HALF)], recv_a2.at[t], a2_send.at[t], a2_recv.at[t], (sp, step_z(t), y, core))

    def send_b2(d):
        return remote(sum_b.at[mod4(y + d)], recv_b2.at[before(d)], b2_send.at[before(d)], b2_recv.at[before(d)], ring_y(d))

    def sum_a(t):
        for i, d in ways:
            full_a(t, i, d).wait()
        chip[t, y, :, :HALF] += full_y[0, t] + full_y[1, t]

    def send_gw(cols, part, d):
        return remote(gw_buf.at[sp, :, cols], gw_buf.at[sp, :, cols], g_send.at[part, d], g_recv.at[part, d], ring_sp(d))

    pass_a(3)
    sum_a(0)
    send_a2(0).start()
    remote_steps(1)
    sum_a(1)
    send_a2(1).start()
    remote_steps(2)
    sum_a(2)
    send_a2(2).start()
    for copy in scatter:
        copy.wait()
    fout[sp] = (fin[sp] + rc[0]) + (rc[1] + rc[2])
    spread = [remote(fout.at[sp], fout.at[sp], f_send.at[d], f_recv.at[d], ring_sp(d)) for d in RING]
    for copy in spread:
        copy.start()
    for i, d in ways:
        full_b(i, d).wait()
    for i in QUAD:
        sum_b[i] = chip[3, i, :, HALF:] + (full_z[0, i] + full_z[1, i])
    for d in RING:
        send_b2(d).start()
    sum_a(3)
    for t in TRIO:
        send_a2(t).wait()
    gw_buf[sp, :, :HALF] = (chip[3, y, :, :HALF] + recv_a2[0]) + (recv_a2[1] + recv_a2[2])
    first, second = pl.ds(0, HALF), pl.ds(HALF, HALF)
    grad_sends = [send_gw(first, 0, d) for d in RING]
    for copy in grad_sends:
        copy.start()
    drain(gtile.at[pl.ds(1, GROUP - 1)], t_send.at[0], t_recv.at[0])
    gpart[...] = jnp.sum(gtile[...], axis=0)
    gain_sends = [remote(gpart, gacross.at[before(d)], u_send.at[before(d)], u_recv.at[before(d)], ring_sp(d)) for d in RING]
    for copy in gain_sends:
        copy.start()
    for d in RING:
        send_b2(d).wait()
    gw_buf[sp, :, HALF:] = (sum_b[y] + recv_b2[0]) + (recv_b2[1] + recv_b2[2])
    more = [send_gw(second, 1, d) for d in RING]
    for copy in more:
        copy.start()
    grad_sends += more
    remote_steps(3)
    gx_stage = gy_buf
    gx_stage[...] = acc[...].astype(jnp.bfloat16)
    store_gx = pltpu.make_async_copy(gx_stage, gx_hbm, out_sem.at[0])
    store_gx.start()
    for copy in gain_sends:
        copy.wait()
    gain_ref[...] = (gpart[...] + gacross[0]) + (gacross[1] + gacross[2])
    store_gain = pltpu.make_async_copy(gain_ref, gain_hbm, out_sem.at[1])
    store_gain.start()
    for copy in grad_sends:
        copy.wait()
    store_gw = [pltpu.make_async_copy(gw_buf.at[s, :, pl.ds(m * BLK, BLK)], out.at[:, pl.ds(s * BLK, BLK)], out_sem.at[6 + m * NSP + s])
                for m, out in enumerate((gq_hbm, gk_hbm, gv_hbm)) for s in QUAD]
    for copy in store_gw:
        copy.start()
    for copy in spread:
        copy.wait()
    store_o = [pltpu.make_async_copy(fout.at[n], gwo_hbm.at[:, pl.ds(n * BLK, BLK)], out_sem.at[2 + n]) for n in QUAD]
    for copy in store_o:
        copy.start()
    for copy in [store_gx, store_gain] + store_gw + store_o:
        copy.wait()


def tail(d_blocks, x_full, weights, grad_y, a_sum, b_sum, dv_tok, tiles):
    hbm = pl.BlockSpec(memory_space=pl.ANY)
    vmem = pl.BlockSpec(memory_space=pltpu.VMEM)
    dma = pltpu.SemaphoreType.DMA
    return pl.pallas_call(
        tail_kernel,
        out_shape=[jax.ShapeDtypeStruct((BLK, WIDTH), BF16), ] + [jax.ShapeDtypeStruct((ROWS, WIDTH), F32)] * NSP + [
                   jax.ShapeDtypeStruct((SUB, TILE), F32)],
        in_specs=[hbm] * 10 + [vmem], out_specs=[hbm] * 6,
        scratch_shapes=[pltpu.VMEM((SUB, TILE), F32),
            pltpu.VMEM((NSP, BLK, QKV), BF16), pltpu.VMEM((2, WIDTH, BLK), BF16), pltpu.VMEM((2, NSP, 2, ROWS, QKV), F32),
            pltpu.VMEM((NSP, NSP, ROWS, QKV), F32), pltpu.VMEM((NSP, 2, ROWS, HALF // 2), F32), pltpu.VMEM((2, NSP, ROWS, HALF // 2), F32),
            pltpu.VMEM((2, NSP, ROWS, HALF), F32), pltpu.VMEM((2, NSP, ROWS, HALF), F32),
            pltpu.VMEM((NSP, ROWS, HALF), F32), pltpu.VMEM((3, ROWS, HALF), F32), pltpu.VMEM((3, ROWS, HALF), F32),
            pltpu.VMEM((3, BLK, QKV), BF16), pltpu.VMEM((3, WIDTH, BLK), BF16), pltpu.VMEM((BLK, WIDTH), F32), pltpu.VMEM((BLK, WIDTH), BF16),
            pltpu.VMEM((NSP, ROWS, QKV), F32), pltpu.VMEM((GROUP, SUB, TILE), F32), pltpu.VMEM((SUB, TILE), F32), pltpu.VMEM((3, SUB, TILE), F32),
            pltpu.VMEM(a_sum.shape, F32), pltpu.VMEM(b_sum.shape, F32), pltpu.VMEM((3,) + a_sum.shape[1:], F32), pltpu.VMEM((3,) + a_sum.shape[1:], F32),
            pltpu.VMEM((NSP, ROWS, BLK), F32), pltpu.VMEM((3, ROWS, BLK), F32), pltpu.VMEM((NSP, ROWS, BLK), F32),
            dma((7,)), dma((2,)), dma((3,)), dma((18,))] + dma_sems((NSP, NSP), (NSP,), (NSP, 2), (2,), (NSP,), (NSP,), (2, NSP), (1,), (NSP,), (NSP,), (NSP,), (NSP,), (NSP,), (NSP, 2), (2,)),
        compiler_params=pltpu.CompilerParams(collective_id=3, has_side_effects=True, vmem_limit_bytes=62 * MIB),
        cost_estimate=pl.CostEstimate(flops=60_000_000_000, bytes_accessed=60 * MIB, transcendentals=0),
        name='tail')(d_blocks, x_full, *[w.reshape(WIDTH, QKV) for w in weights], grad_y, a_sum, b_sum, dv_tok, tiles)


def deliver_kernel(*refs):
    count = (len(refs) - 2) // 3
    sources, results, held = refs[:count], refs[count:2 * count], refs[2 * count:3 * count]
    in_sem, out_sem = refs[3 * count:]
    loads = [pltpu.make_async_copy(src, buf, in_sem.at[i]) for i, (src, buf) in enumerate(zip(sources, held))]
    stores = [pltpu.make_async_copy(buf, dst, out_sem.at[i]) for i, (buf, dst) in enumerate(zip(held, results))]
    for load in loads:
        load.start()
    for load, store in zip(loads, stores):
        load.wait()
        store.start()
    for store in stores:
        store.wait()


def deliver(*arrays):
    hbm = [pl.BlockSpec(memory_space=pl.ANY)] * len(arrays)
    sems = [pltpu.SemaphoreType.DMA((len(arrays),))] * 2
    return pl.pallas_call(
        deliver_kernel, out_shape=[jax.ShapeDtypeStruct(a.shape, a.dtype) for a in arrays], in_specs=hbm, out_specs=hbm,
        scratch_shapes=[pltpu.VMEM(a.shape, a.dtype) for a in arrays] + sems, name='deliver')(*arrays)


def solution(mesh):
    grid_mesh = Mesh(mesh.devices.reshape(NSP, NSP, NSP, 2), ('sp',) + FS)
    tok_spec = P(FS, 'sp', None)
    row_spec = P(FS, None)
    vec_spec = P(FS)

    freq = ROPE_THETA ** (-np.arange(HALF_HEAD) * (2.0 / HEAD_DIM))
    freq = np.concatenate([freq, freq])[None, :]
    angles = (np.arange(0, SEQ, ROWS)[:, None] * freq, np.arange(ROWS)[:, None] * freq)
    tables = [table(angle).astype(np.float32) for angle in angles for table in (np.cos, np.sin)]

    def local_step(x, grad_y, wq_rows, wk_rows, wv_rows, wo_rows, gq_rows, gk_rows, gpost_rows):
        x = x.reshape(BLK, WIDTH)
        grad_y = grad_y.reshape(BLK, WIDTH)
        vecs = jnp.stack([gq_rows, gk_rows, gpost_rows])
        gain_tile = jnp.pad(jnp.concatenate([vecs, vecs], axis=1), ((0, 5), (0, 0)))
        w_rows = (wq_rows, wk_rows, wv_rows)
        x_full, q0, k0, q_rot, k_rot, v, o_heads, o_tok, lse, y, grad_a, grad_o, w_own, w_next, w_far, w_prev, inv, gains, post = forward_pass(
            x, grad_y, *w_rows, wo_rows, gain_tile, tables)
        d_blocks, a_sum, b_sum, dv_tok, tiles = mid(
            o_tok, grad_a, grad_o, (q_rot, k_rot, v, o_heads, q0, k0), lse, inv, gains, post, tables)
        grad_x, *grad_w, gain_grads = tail(d_blocks, x_full.reshape(WIDTH, WIDTH), (w_own, w_next, w_far, w_prev), grad_y, a_sum, b_sum, dv_tok, tiles)
        y, grad_x, *grad_w = deliver(y, grad_x, *grad_w)
        gain_grads = lax.dynamic_slice_in_dim(gain_grads, lax.axis_index('core') * ROWS, ROWS, axis=1)
        return (y.reshape(1, BLK, WIDTH), grad_x.reshape(1, BLK, WIDTH), *grad_w, gain_grads[0], gain_grads[1], gain_grads[2])

    return jax.shard_map(local_step, mesh=grid_mesh,
                         in_specs=(tok_spec, tok_spec, row_spec, row_spec, row_spec, row_spec, vec_spec, vec_spec, vec_spec),
                         out_specs=(tok_spec, tok_spec, row_spec, row_spec, row_spec, row_spec, vec_spec, vec_spec, vec_spec),
                         check_vma=False)
```

profile of v0, /device:TPU:0, one launch (start us, length us, event | category | flops | bytes accessed | tf_op | source)
XLA Modules:
  0.0 274.0 jit_solution(8035215109867503424)
XLA Ops:
  0.6 1.4 fusion.tile_ref
  2.1 129.0 %forward.1 = (bf16[4,512,2048]{2,1,0:T(8,128)(2,1)}, bf16[4,512,512]{2,1,0:T(8,128)(2,1)}, bf16[4,512,512]{2,1,0:T(8,128)(2,1)}, bf16[4,512,512]{2,1,0:T(8,128)(...) custom-call(bf16[512,2048]{1,0:T(8,128)(2,1)} %bitcast.21, ...), custom_call_target="tpu_custom_call" | custom-call | flops 80000000000 | bytes 41943040 | tf_op jit(solution)/shard_map/forward/pallas_call | solution.py:498
  131.0 53.4 %middle.1 = (bf16[4,512,1536]{2,1,0:T(8,128)(2,1)}, f32[4,2,64,512]{3,2,1,0:T(8,128)}, f32[2,4,64,512]{3,2,1,0:T(8,128)}, bf16[4,512,512]{2,1,0:T(8,128)(2,1)}, f32[32,8,128]{2,1,0:T(8,128)}) custom-call(bf16[4,512,512]{2,1,0:T(8,128)(2,1)} %get-tuple-element.46.ot_hbm, bf16[512,2048]{1,0:T(8,128)(2,1)} %get-tuple-element.47.ga_hbm, ...), custom_call_target="tpu_custom_call" | custom-call | flops 60000002048 | bytes 33554432 | tf_op jit(solution)/shard_map/middle/pallas_call | solution.py:740
  184.5 84.5 %tail.1 = (bf16[512,2048]{1,0:T(8,128)(2,1)}, f32[64,2048]{1,0:T(8,128)}, f32[64,2048]{1,0:T(8,128)}, f32[64,2048]{1,0:T(8,128)}, f32[64,2048]{1,0:T(8,128)}, /*index=5*/f32[8,128]{1,0:T(8,128)}) custom-call(bf16[4,512,1536]{2,1,0:T(8,128)(2,1)} %get-tuple-element.59.d_hbm, bf16[2048,2048]{1,0:T(8,128)(2,1)} %bitcast.26, bf16[2048,1536]{1,0:T(8,128)(2,1)} %bitcast.27, ...), custom_call_target="tpu_custom_call" | custom-call | flops 60000002048 | bytes 62914560 | tf_op jit(solution)/shard_map/tail/pallas_call | solution.py:1017
  269.0 0.0 copy-start
  269.0 4.4 %deliver.1 = (bf16[512,2048]{1,0:T(8,128)(2,1)}, bf16[512,2048]{1,0:T(8,128)(2,1)}, f32[64,2048]{1,0:T(8,128)}, f32[64,2048]{1,0:T(8,128)}, f32[64,2048]{1,0:T(8,128)}, /*index=5*/f32[64,2048]{1,0:T(8,128)}) custom-call(bf16[512,2048]{1,0:T(8,128)(2,1)} %get-tuple-element.45.refs_0_, bf16[512,2048]{1,0:T(8,128)(2,1)} %get-tuple-element.69.refs_1_, ...), custom_call_target="tpu_custom_call" | custom-call | tf_op jit(solution)/shard_map/deliver/pallas_call | solution.py:1055
  273.4 0.0 copy-done
  273.4 0.1 constant_dynamic-slice_fusion
  273.5 0.5 slice_bitcast_fusion
Async XLA Ops:
  269.0 4.4 %copy-start = (f32[8,128]{1,0:T(8,128)S(1)}, f32[8,128]{1,0:T(8,128)}, u32[]{:S(2)}) copy-start(f32[8,128]{1,0:T(8,128)} %get-tuple-element.80) | copy-start | bytes 12292
where the time goes:
time: 274 us
  Pallas kernels  271 us (99%)
    pallas_call x1, Pallas kernels, forward_pass(): pl.pallas_call(fwd_kernel, out_shape=[jax.ShapeDtypeStruct((NSP, BLK, WID...  129 us
    pallas_call x1, Pallas kernels, tail(): pl.pallas_call(tail_kernel, out_shape=[jax.ShapeDtypeStruct((BLK, WIDTH),...  84.5 us
    pallas_call x1, Pallas kernels, mid(): pl.pallas_call(mid_kernel, out_shape=[jax.ShapeDtypeStruct((NSP, BLK, QKV...  53.4 us

commit v1 on v0

--- a/solution.py
+++ b/solution.py
@@ -35,6 +35,7 @@
 VMEM_LIMIT = 62 * 2 ** 20
 SUB = 8
 WIDE = 256
+PEERS = 3
 PART = 16
 SIDES = (1, 3)
 HALF_HEAD = 64
@@ -116,7 +117,7 @@
 
 
 def step_offset(t):
-    return jnp.where(t == 0, 2, jnp.where(t == 1, 1, jnp.where(t == 2, 3, 0)))
+    return jnp.where(t == 0, 2, jnp.where(t == 1, 1, jnp.where(t == 2, PEERS, 0)))
 
 
 def local_gains(gt_ref, grow):
@@ -169,7 +170,7 @@
     sp, z, y, core = my_coords()
     a1_send, a1_recv, b1_send, b1_recv, near_send, near_recv, far_send, far_recv, c_send, c_recv = sems
     low, high = pl.ds(0, GROUP), pl.ds(GROUP, GROUP)
-    ways = tuple(enumerate(SIDES))
+    ways = tuple(enumerate((1, PEERS)))
 
     def first(d):
         own_low, own_high = buf.at[z, y, core, low], buf.at[z, y, core, high]
@@ -222,7 +223,7 @@
 
 
 def gather_sems(groups):
-    return dma_sems((groups, 3), (groups, 3), (groups, NSP), (groups, NSP), (groups, NSP))
+    return dma_sems((groups, PEERS), (groups, PEERS), (groups, NSP), (groups, NSP), (groups, NSP))
 
 
 def norm_and_grad(acc, x, grad_y, gain, y_out, grad_out, post):
@@ -242,14 +243,14 @@
     loop(BLK // ROWS, chunk)
 
 
-def fwd_kernel(x_hbm, gy_hbm, wq_hbm, wk_hbm, wv_hbm, wo_hbm, tile_ref, ca_ref, sa_ref, cb_ref, sb_ref,
+def fwd_kernel(x_hbm, gy_hbm, wq_hbm, wk_hbm, wv_hbm, wo_hbm, tile_hbm, ca_hbm, sa_hbm, cb_hbm, sb_hbm,
                xf_hbm, q0_hbm, k0_hbm, qr_hbm, kr_hbm, v_hbm, o_hbm, ot_hbm, lse_hbm, y_hbm, ga_hbm, ds_hbm, wl_hbm, wa_hbm, wb_hbm, wc_hbm,
                inv_hbm, gt_hbm, post_hbm,
-               inv_ref, gt_ref, post_ref, xf, wl, wo, q0, k0, v, qr, kr, o, ot, lse, s_scr, vt_scr, cos_scr, sin_scr, st, st_in, grow, gpost, invc,
+               tile_ref, ca_ref, sa_ref, cb_ref, sb_ref, inv_ref, gt_ref, post_ref, xf, wl, wo, q0, k0, v, qr, kr, o, ot, lse, s_scr, vt_scr, cos_scr, sin_scr, st, st_in, grow, gpost, invc,
                ld_sem, out_sem, own_send, own_recv, fw_send, fw_recv, t_send, t_recv, u_send, u_recv, o_send, o_recv, *w_sems):
     sp, z, y, core = my_coords()
     me = fsdp_index()
-    right, left = ring_sp(1), ring_sp(3)
+    right, left = ring_sp(1), ring_sp(PEERS)
     far = mod4(sp + 2)
     w_rows = (wq_hbm, wk_hbm, wv_hbm)
 
@@ -259,9 +260,11 @@
     loads = []
     for g, buf in enumerate((wl, wa_hbm, wb_hbm, wc_hbm)):
         for m, w_hbm in enumerate(w_rows):
-            loads.append(pltpu.make_async_copy(w_hbm.at[:, own_cols(g)], buf.at[z, y, core, :, pl.ds(m * BLK, BLK)], ld_sem.at[g * 3 + m]))
+            loads.append(pltpu.make_async_copy(w_hbm.at[:, own_cols(g)], buf.at[z, y, core, :, pl.ds(m * BLK, BLK)], ld_sem.at[g * PEERS + m]))
     loads.append(pltpu.make_async_copy(wo_hbm, wo.at[z, y, core], ld_sem.at[12]))
     loads.append(pltpu.make_async_copy(x_hbm, xf.at[sp], ld_sem.at[13]))
+    for k, pair in enumerate(((tile_hbm, tile_ref), (ca_hbm, ca_ref), (sa_hbm, sa_ref), (cb_hbm, cb_ref), (sb_hbm, sb_ref))):
+        loads.insert(0, pltpu.make_async_copy(*pair, out_sem.at[k]))
     for load in loads:
         load.start()
     greet_all()
@@ -272,14 +275,14 @@
     def own_x(side, c):
         return remote(x_hbm.at[chunk(c)], xf.at[sp, chunk(c)], own_send.at[side, c], own_recv.at[side, c], (right, left)[side])
 
-    for right_c, left_c in zip((0, 2, 1, 3), (1, 3, 0, 2)):
+    for right_c, left_c in zip((0, 2, 1, PEERS), (1, PEERS, 0, 2)):
         own_x(0, right_c).start()
         own_x(1, left_c).start()
 
     tile_sends = []
     for step in range(1, GROUP):
         tile_sends.append(remote(tile_ref, gt_ref.at[me], t_send.at[0], t_recv.at[0], fsdp_peer(step)[1]))
-    for load in loads[:3]:
+    for load in loads[:SUB]:
         load.wait()
     stages = [gather_stages(buf, g, w_sems) for g, buf in enumerate((wl, wo, wa_hbm, wb_hbm, wc_hbm))]
 
@@ -293,7 +296,7 @@
         stages[g][2]()
 
     def share(g):
-        stages[g][3]()
+        stages[g][PEERS]()
 
     def gathered(g):
         stages[g][NSP]()
@@ -306,7 +309,7 @@
     pass_on(0)
 
     def forward(side, i):
-        block = mod4(sp + (3, 1)[side])
+        block = mod4(sp + (PEERS, 1)[side])
         piece = xf.at[block, chunk(2 * i + side)]
         return remote(piece, piece, fw_send.at[side, i], fw_recv.at[side, i], (right, left)[side])
 
@@ -317,7 +320,7 @@
 
     forward_x(0)
     relay(0)
-    for load in loads[3:]:
+    for load in loads[SUB:]:
         load.wait()
     for g in RING + (NSP,):
         begin(g)
@@ -325,6 +328,8 @@
     forward_x(1)
     pass_on(1)
     gathered(0)
+    stores = [pltpu.make_async_copy(wl, wl_hbm, out_sem.at[NSP])]
+    stores[0].start()
     st[:, :] = jnp.zeros_like(st)
 
     def project(block, i):
@@ -337,7 +342,7 @@
             if n < 2:
                 wide = out.astype(F32)
                 wide = wide * wide
-                part = (wide[:, :TILE] + wide[:, TILE:WIDE]) + (wide[:, WIDE:3 * TILE] + wide[:, 3 * TILE:])
+                part = (wide[:, :TILE] + wide[:, TILE:WIDE]) + (wide[:, WIDE:PEERS * TILE] + wide[:, PEERS * TILE:])
                 mine = lax.broadcasted_iota(jnp.int32, (SUB, WIDE), 0) == n * NSP + block
                 st[:, rows] = jnp.where(mine, row_sum(part.T), st[:, rows])
 
@@ -356,23 +361,26 @@
         project(far, i)
 
     loop(6, near)
+    for d in (0, 1, PEERS):
+        stores.append(pltpu.make_async_copy(xf.at[mod4(sp + d)], xf_hbm.at[mod4(sp + d)], out_sem.at[5 + d]))
+        stores[-1].start()
     relay(1)
-    for g in (2, 3, NSP):
+    for g in (2, PEERS, NSP):
         pass_on(g)
     loop(2, distant)
     stats = [remote(st, st_in.at[before(d)], u_send.at[before(d)], u_recv.at[before(d)], ring_sp(d)) for d in RING]
     for copy in stats:
         copy.start()
-    stores = [pltpu.make_async_copy(src, dst, out_sem.at[i]) for i, (src, dst) in enumerate(((xf, xf_hbm), (q0, q0_hbm), (k0, k0_hbm), (v, v_hbm), (wl, wl_hbm)))]
-    for copy in stores:
-        copy.start()
+    for i, (src, dst) in enumerate(((xf.at[far], xf_hbm.at[far]), (q0, q0_hbm), (k0, k0_hbm), (v, v_hbm))):
+        stores.append(pltpu.make_async_copy(src, dst, out_sem.at[i]))
+        stores[-1].start()
     relay(2)
     share(1)
     drain(gt_ref.at[pl.ds(1, GROUP - 1)], t_send.at[0], t_recv.at[0])
     local_gains(gt_ref, grow)
     lane = lax.broadcasted_iota(jnp.int32, (1, TILE), 1) < HALF_HEAD
     for i in range(WIDTH // TILE):
-        gpost[:, i * TILE:(i + 1) * TILE] = jnp.broadcast_to(jnp.where(lane, gt_ref[2 * i, 2:3, :], gt_ref[2 * i + 1, 2:3, :]), (SUB, TILE))
+        gpost[:, i * TILE:(i + 1) * TILE] = jnp.broadcast_to(jnp.where(lane, gt_ref[2 * i, 2:PEERS, :], gt_ref[2 * i + 1, 2:PEERS, :]), (SUB, TILE))
     for copy in stats:
         copy.wait()
     total = (st[:, :] + st_in[0]) + (st_in[1] + st_in[2])
@@ -429,7 +437,7 @@
     for copy in stores:
         copy.wait()
     ot[sp] = o[sp]
-    relay(3)
+    relay(PEERS)
     relay(NSP)
     share(2)
     last = [pltpu.make_async_copy(o, o_hbm, out_sem.at[0]), pltpu.make_async_copy(lse, lse_hbm, out_sem.at[1]),
@@ -457,12 +465,12 @@
                 acc[n] += part
 
     loop(NSP, project_out)
-    share(3)
+    share(PEERS)
     share(NSP)
     grad_in.wait()
     last.append(pltpu.make_async_copy(ot, ot_hbm, out_sem.at[2]))
     last[-1].start()
-    y_out, grad_a = xf.at[far], xf.at[mod4(sp + 3)]
+    y_out, grad_a = xf.at[far], xf.at[mod4(sp + PEERS)]
     norm_and_grad(acc, xf.at[sp], xf.at[mod4(sp + 1)], gpost[0:1, :], y_out, grad_a, post_ref)
     for i, (src, dst) in enumerate(((y_out, y_hbm), (grad_a, ga_hbm), (inv_ref, inv_hbm), (gt_ref, gt_hbm), (post_ref, post_hbm))):
         last.append(pltpu.make_async_copy(src, dst, out_sem.at[SUB + i]))
@@ -475,7 +483,7 @@
 
     loop(NSP, grad_attn)
     gathered(2)
-    gathered(3)
+    gathered(PEERS)
     last.append(pltpu.make_async_copy(v, ds_hbm, out_sem.at[5]))
     last[-1].start()
     gathered(NSP)
@@ -499,20 +507,20 @@
         fwd_kernel,
         out_shape=[jax.ShapeDtypeStruct((NSP, BLK, WIDTH), BF16)] + [wide] * 7 + [jax.ShapeDtypeStruct((NSP, SUB, SEQ), F32), tokens, tokens, wide] + [weight] * NSP + [
             jax.ShapeDtypeStruct((SUB, BLK), F32), jax.ShapeDtypeStruct((GROUP, SUB, TILE), F32), jax.ShapeDtypeStruct((SUB, WIDTH), F32)],
-        in_specs=[hbm] * 6 + [vmem] * 5, out_specs=[hbm] * 19,
-        scratch_shapes=[pltpu.VMEM((SUB, BLK), F32), pltpu.VMEM((GROUP, SUB, TILE), F32), pltpu.VMEM((SUB, WIDTH), F32), pltpu.VMEM((NSP, BLK, WIDTH), BF16), pltpu.VMEM(blocks + (QKV,), BF16), pltpu.VMEM(blocks + (WIDTH,), BF16)] + [pltpu.VMEM(quad, BF16)] * 7 + [
+        in_specs=[hbm] * 11, out_specs=[hbm] * 19,
+        scratch_shapes=[pltpu.VMEM(a.shape, F32) for a in (gain_tile, *tables)] + [pltpu.VMEM((SUB, BLK), F32), pltpu.VMEM((GROUP, SUB, TILE), F32), pltpu.VMEM((SUB, WIDTH), F32), pltpu.VMEM((NSP, BLK, WIDTH), BF16), pltpu.VMEM(blocks + (QKV,), BF16), pltpu.VMEM(blocks + (WIDTH,), BF16)] + [pltpu.VMEM(quad, BF16)] * 7 + [
             pltpu.VMEM((NSP, SUB, SEQ), F32), pltpu.VMEM((2,) + quad, F32), pltpu.VMEM((TILE, SEQ), BF16),
-            pltpu.VMEM((SEQ, TILE), F32), pltpu.VMEM((SEQ, TILE), F32), pltpu.VMEM((SUB, BLK), F32), pltpu.VMEM((3, SUB, BLK), F32), pltpu.VMEM((SUB, BLK), F32),
+            pltpu.VMEM((SEQ, TILE), F32), pltpu.VMEM((SEQ, TILE), F32), pltpu.VMEM((SUB, BLK), F32), pltpu.VMEM((PEERS, SUB, BLK), F32), pltpu.VMEM((SUB, BLK), F32),
             pltpu.VMEM((SUB, WIDTH), F32), pltpu.VMEM((2, NSP, BLK, TILE), F32),
-            pltpu.SemaphoreType.DMA((14,)), pltpu.SemaphoreType.DMA((13,))] + dma_sems((2, NSP), (2, 2), (1,), (3,), (NSP, 3)) + gather_sems(5),
+            pltpu.SemaphoreType.DMA((14,)), pltpu.SemaphoreType.DMA((13,))] + dma_sems((2, NSP), (2, 2), (1,), (PEERS,), (NSP, PEERS)) + gather_sems(5),
         compiler_params=pltpu.CompilerParams(collective_id=1, has_side_effects=True, vmem_limit_bytes=VMEM_LIMIT),
         cost_estimate=pl.CostEstimate(flops=80_000_000_000, bytes_accessed=40 * MIB, transcendentals=0),
         name='forward')(x, grad_y, wq_rows, wk_rows, wv_rows, wo_rows, gain_tile, *tables)
 
 
-def mid_kernel(ot_hbm, ga_hbm, ds_hbm, qr_hbm, kr_hbm, v_hbm, o_hbm, q0_hbm, k0_hbm, lse_hbm, inv_ref, gt_ref, post_ref,
-               ca_ref, sa_ref, cb_ref, sb_ref, d_hbm, as_hbm, bs_hbm, dvt_hbm, tile_hbm,
-               tile_ref, ot, ga, gap, ott, do, qa, ka, va, oa, q0, k0, otp, big, chip, half_y, half_z, full_y, full_z, invc, cos_scr, sin_scr,
+def mid_kernel(ot_hbm, ga_hbm, ds_hbm, qr_hbm, kr_hbm, v_hbm, o_hbm, q0_hbm, k0_hbm, lse_hbm, inv_hbm, gt_hbm, post_hbm,
+               ca_hbm, sa_hbm, cb_hbm, sb_hbm, d_hbm, as_hbm, bs_hbm, dvt_hbm, tile_hbm,
+               inv_ref, gt_ref, post_ref, ca_ref, sa_ref, cb_ref, sb_ref, tile_ref, ot, ga, gap, ott, do, qa, ka, va, oa, q0, k0, otp, big, chip, half_y, half_z, full_y, full_z, invc, cos_scr, sin_scr,
                dk_scr, dv_scr, kt_scr, lse, grow, gacc, st, st_in,
                in_sem, out_sem, do_send, do_recv, c_send, c_recv, a1_send, a1_recv, b1_send, b1_recv, a2_send, a2_recv, b2_send, b2_recv,
                u_send, u_recv, v_send, v_recv):
@@ -531,6 +539,7 @@
         return copies
 
     load_ot = group([(ot_hbm, ot), (ga_hbm, ga)], in_sem.at[0])
+    load_aux = group(((inv_hbm, inv_ref), (gt_hbm, gt_ref), (post_hbm, post_ref), (ca_hbm, ca_ref), (sa_hbm, sa_ref), (cb_hbm, cb_ref), (sb_hbm, sb_ref)), in_sem.at[1])
 
     barrier = pltpu.get_barrier_semaphore()
     greeted = [ring(d) for ring in (ring_sp, ring_z, ring_y) for d in RING] + [partner()]
@@ -560,6 +569,8 @@
         ott[s] = ot[s].T
     for i in QUAD:
         send_core(i).start()
+    for copy in load_aux:
+        copy.wait()
     local_gains(gt_ref, grow)
     fill_rope(ca_ref, sa_ref, cb_ref, sb_ref, cos_scr, sin_scr)
     inv_columns(inv_ref, invc)
@@ -569,7 +580,7 @@
         return mod4(z + step_offset(t))
 
     low, high = pl.ds(0, 2), pl.ds(2, 2)
-    ways = tuple(enumerate(SIDES))
+    ways = tuple(enumerate((1, PEERS)))
 
     def half_a(t, i, d):
         return remote(chip.at[t, i, mod4(y + 2)], half_y.at[t, i], a1_send.at[t, i], a1_recv.at[t, i], ring_y(d))
@@ -618,9 +629,6 @@
     for copy in load_qk:
         copy.wait()
 
-    row = lax.broadcasted_iota(jnp.int32, (BLK, BLK), 0)
-    col = lax.broadcasted_iota(jnp.int32, (BLK, BLK), 1)
-
     def unrotate(grad, i, m, lanes, kept):
         rows = slice(i * BLK, (i + 1) * BLK)
         grad = grad * cos_scr[rows, :] - pltpu.roll(grad, HALF_HEAD, 1) * sin_scr[rows, :]
@@ -647,20 +655,22 @@
             delta = row_sum((do_i.astype(F32) * oa[i, :, lanes].astype(F32)).T)
             top = lse[h, 0:1, i * BLK:(i + 1) * BLK]
             dqt = None
-            for j in range(i + 1):
-                s = lax.dot_general(ka[j, :, lanes], q_i, NT, preferred_element_type=F32)
-                p = jnp.exp2(s * LOG2_SCALE - top)
+            tiles = [(j, 0, BLK, 0) for j in range(i)] + [(i, 0, BLK // 2, 0), (i, BLK // 2, BLK, BLK // 2)]
+            for j, start, stop, first in tiles:
+                keys = slice(start, stop)
+                s = lax.dot_general(ka[j, keys, lanes], q_i[first:], NT, preferred_element_type=F32)
+                p = jnp.exp2(s * LOG2_SCALE - top[:, first:])
                 if j == i:
-                    p = jnp.where(row <= col, p, 0.0)
-                dp = lax.dot_general(va[j, :, lanes], do_i, NT, preferred_element_type=F32)
-                grad_s = (p * (dp - delta)).astype(BF16)
-                dv = jnp.dot(p.astype(BF16), do_i, preferred_element_type=F32)
-                dk = jnp.dot(grad_s, q_i, preferred_element_type=F32)
-                part = jnp.dot(kt_scr[:, j * BLK:(j + 1) * BLK], grad_s, preferred_element_type=F32)
-                dqt = plus(dqt, part)
+                    p = jnp.where(lax.broadcasted_iota(jnp.int32, s.shape, 0) <= lax.broadcasted_iota(jnp.int32, s.shape, 1), p, 0.0)
+                dp = lax.dot_general(va[j, keys, lanes], do_i[first:], NT, preferred_element_type=F32)
+                grad_s = (p * (dp - delta[:, first:])).astype(BF16)
+                dv = jnp.dot(p.astype(BF16), do_i[first:], preferred_element_type=F32)
+                dk = jnp.dot(grad_s, q_i[first:], preferred_element_type=F32)
+                part = jnp.dot(kt_scr[:, j * BLK + start:j * BLK + stop], grad_s, preferred_element_type=F32)
+                dqt = plus(dqt, part) if first == 0 else jnp.concatenate([dqt[:, :first], dqt[:, first:] + part], axis=1)
                 if j == i:
-                    dv_scr[j] = dv
-                    dk_scr[j] = dk
+                    dv_scr[j, keys] = dv
+                    dk_scr[j, keys] = dk
                 else:
                     dv_scr[j] += dv
                     dk_scr[j] += dk
@@ -690,15 +700,15 @@
     tile_ref[:, :, :] = jnp.zeros_like(tile_ref)
     for i in range(WIDTH // TILE):
         total = row_sum(post_ref[:, i * TILE:(i + 1) * TILE])
-        tile_ref[2 * i, 2:3, :] = total
-        tile_ref[2 * i + 1, 2:3, :] = total
+        tile_ref[2 * i, 2:PEERS, :] = total
+        tile_ref[2 * i + 1, 2:PEERS, :] = total
     for m in PAIR:
         for h in QUAD:
             total = row_sum(gacc[m, :, h * TILE:(h + 1) * TILE])
             for c in PAIR:
                 tile_ref[sp * SUB + 2 * h + c, m:m + 1, :] = total
 
-    store_v += group([(tile_ref, tile_hbm)], out_sem.at[3])
+    store_v += group([(tile_ref, tile_hbm)], out_sem.at[PEERS])
     for copy in stats:
         copy.wait()
     st[:, :] = ((st[:, :] + st_in[0]) + (st_in[1] + st_in[2])) / WIDTH
@@ -736,21 +746,21 @@
     scratch = half + [pltpu.VMEM(shape, F32) for shape in (
         (2,) + quad, (NSP, NSP, NSP, ROWS, BLK), (NSP,) + pair, (NSP,) + pair, (2, NSP) + pair, (2, NSP) + pair,
         (2, NSP, BLK, TILE), (SEQ, TILE), (SEQ, TILE), (NSP, BLK, TILE), (NSP, BLK, TILE))] + [pltpu.VMEM((TILE, SEQ), BF16)] + [
-        pltpu.VMEM(shape, F32) for shape in ((NSP, SUB, SEQ), (SUB, BLK), (2, SUB, BLK), (SUB, BLK), (3, SUB, BLK))]
+        pltpu.VMEM(shape, F32) for shape in ((NSP, SUB, SEQ), (SUB, BLK), (2, SUB, BLK), (SUB, BLK), (PEERS, SUB, BLK))]
     return pl.pallas_call(
         mid_kernel,
         out_shape=[jax.ShapeDtypeStruct((NSP, BLK, QKV), BF16),
                    jax.ShapeDtypeStruct((NSP,) + pair, F32), jax.ShapeDtypeStruct((2, NSP, ROWS, BLK), F32), jax.ShapeDtypeStruct(quad, BF16),
                    jax.ShapeDtypeStruct(gains.shape, F32)],
-        in_specs=[hbm] * 10 + [vmem] * 7, out_specs=[hbm] * 5,
-        scratch_shapes=[pltpu.VMEM(gains.shape, F32)] + scratch + [pltpu.SemaphoreType.DMA(shape) for shape in ((3, SUB), (NSP, 5))] + sems,
+        in_specs=[hbm] * 17, out_specs=[hbm] * 5,
+        scratch_shapes=[pltpu.VMEM(a.shape, F32) for a in (inv, gains, post, *tables, gains)] + scratch + [pltpu.SemaphoreType.DMA(shape) for shape in ((PEERS, SUB), (NSP, 5))] + sems,
         compiler_params=pltpu.CompilerParams(collective_id=2, has_side_effects=True, vmem_limit_bytes=VMEM_LIMIT),
         cost_estimate=pl.CostEstimate(flops=60_000_000_000, bytes_accessed=WIDTH * WIDTH * SUB, transcendentals=0),
         name='middle')(o_tok, grad_a, grad_o, *heads, lse, inv, gains, post, *tables)
 
 
-def tail_kernel(d_hbm, x_hbm, wl_hbm, wa_hbm, wb_hbm, wc_hbm, gy_hbm, as_hbm, bs_hbm, dvt_hbm, tile_ref,
-                gx_hbm, gq_hbm, gk_hbm, gv_hbm, gwo_hbm, gain_hbm, gain_ref,
+def tail_kernel(d_hbm, x_hbm, wl_hbm, wa_hbm, wb_hbm, wc_hbm, gy_hbm, as_hbm, bs_hbm, dvt_hbm, tile_hbm,
+                gx_hbm, gq_hbm, gk_hbm, gv_hbm, gwo_hbm, gain_hbm, tile_ref, gain_ref,
                 d_loc, x_col, part, chip, half_y, half_z, full_y, full_z, sum_b, recv_a2, recv_b2, d_tok, w_buf, acc, gy_buf, gw_buf, gtile, gpart, gacross,
                 o_a, o_b, o_ra, o_rb, fin, rc, fout,
                 ld_sem, x_sem, w_sem, out_sem, d_send, d_recv, c_send, c_recv, a1_send, a1_recv, b1_send, b1_recv,
@@ -759,11 +769,12 @@
     sp, z, y, core = my_coords()
     me = fsdp_index()
 
-    load_o = [pltpu.make_async_copy(as_hbm, o_a, ld_sem.at[2]), pltpu.make_async_copy(bs_hbm, o_b, ld_sem.at[3])]
+    load_o = [pltpu.make_async_copy(as_hbm, o_a, ld_sem.at[2]), pltpu.make_async_copy(bs_hbm, o_b, ld_sem.at[PEERS])]
     load_d = pltpu.make_async_copy(d_hbm, d_loc, ld_sem.at[0])
     load_gy = pltpu.make_async_copy(gy_hbm, gy_buf, ld_sem.at[1])
-    load_v = [pltpu.make_async_copy(dvt_hbm.at[mod4(sp + NSP - d)], d_tok.at[before(d), :, pl.ds(2 * BLK, BLK)], ld_sem.at[3 + d]) for d in RING]
-    for load in load_o + [load_d]:
+    load_v = [pltpu.make_async_copy(dvt_hbm.at[mod4(sp + NSP - d)], d_tok.at[before(d), :, pl.ds(2 * BLK, BLK)], ld_sem.at[PEERS + d]) for d in RING]
+    load_tile = pltpu.make_async_copy(tile_hbm, tile_ref, ld_sem.at[7])
+    for load in [load_tile] + load_o + [load_d]:
         load.start()
 
     def step_z(t):
@@ -775,23 +786,24 @@
     load_x(0).start()
 
     def source(k):
-        return jnp.where(k == 0, 0, jnp.where(k == 1, 1, jnp.where(k == 2, 3, 2)))
+        return jnp.where(k == 0, 0, jnp.where(k == 1, 1, jnp.where(k == 2, PEERS, 2)))
 
     def which(j):
-        return lax.rem(j + 2, 3)
+        return lax.rem(j + 2, PEERS)
 
     w_order = (wl_hbm, wc_hbm, wa_hbm, wb_hbm)
 
     def load_w(j, src=wl_hbm):
-        return pltpu.make_async_copy(src.at[:, pl.ds(pl.multiple_of(which(j) * BLK, BLK), BLK)], w_buf.at[lax.rem(j, 3)], w_sem.at[lax.rem(j, 3)])
+        return pltpu.make_async_copy(src.at[:, pl.ds(pl.multiple_of(which(j) * BLK, BLK), BLK)], w_buf.at[lax.rem(j, PEERS)], w_sem.at[lax.rem(j, PEERS)])
 
     def start_w(j):
         for k, src in enumerate(w_order):
-            @pl.when(j // 3 == k)
+            @pl.when(j // PEERS == k)
             def _():
                 load_w(j, src).start()
 
     greet_all()
+    load_tile.wait()
     tile_sends = []
     for step in range(1, GROUP):
         f, peer = fsdp_peer(step)
@@ -810,12 +822,12 @@
     for load in load_o:
         load.wait()
     low, high = pl.ds(0, 2), pl.ds(2, 2)
-    o_sends = [remote(o_a.at[t], o_ra.at[t], oa_send.at[t], oa_recv.at[t], ring_z(d)) for t, d in enumerate((2, 1, 3))]
+    o_sends = [remote(o_a.at[t], o_ra.at[t], oa_send.at[t], oa_recv.at[t], ring_z(d)) for t, d in enumerate((2, 1, PEERS))]
     o_sends += [remote(o_b.at[:, mod4(y + d)], o_rb.at[before(d)], ob_send.at[d], ob_recv.at[d], ring_y(d)) for d in RING]
     for copy in o_sends:
         copy.start()
-    for m in PAIR:
-        for d in SIDES:
+    for d in (1, PEERS, 2):
+        for m in PAIR:
             send_d(d, m).start()
 
     load_d.wait()
@@ -824,7 +836,7 @@
         return remote(part.at[parity(t), :, other_core(core)], chip.at[t], c_send.at[t], c_recv.at[t], partner())
 
     quarter = HALF // 2
-    ways = tuple(enumerate(SIDES))
+    ways = tuple(enumerate((1, PEERS)))
 
     def half_a(t, i, d):
         return remote(chip.at[t, mod4(y + 2), :, pl.ds(i * quarter, quarter)], half_y.at[t, i], a1_send.at[t, i], a1_recv.at[t, i], ring_y(d))
@@ -864,7 +876,7 @@
     def wgrad_step(t, carry):
         load_x(t).wait()
 
-        @pl.when(t < 3)
+        @pl.when(t < PEERS)
         def _():
             load_x(t + 1).start()
 
@@ -880,7 +892,7 @@
         return carry
 
     repeat(NSP, wgrad_step)
-    finish(3)
+    finish(PEERS)
     pass_a(0)
     pass_a(1)
     pass_b()
@@ -892,14 +904,12 @@
     scatter = [remote(fin.at[mod4(sp + d)], rc.at[before(d)], s_send.at[d], s_recv.at[d], ring_sp(d)) for d in RING]
     for copy in scatter:
         copy.start()
-    for m in PAIR:
-        send_d(2, m).start()
     for load in load_v + [load_gy]:
         load.wait()
     acc[...] = gy_buf[...].astype(F32)
 
     def gx_step(k, m, block):
-        j = 3 * k + m
+        j = PEERS * k + m
         load_w(j).wait()
 
         @pl.when(j < 10)
@@ -908,7 +918,7 @@
 
         def columns(n):
             cols = pl.ds(pl.multiple_of(n * 2 * BLK, 2 * BLK), 2 * BLK)
-            acc[:, cols] += lax.dot_general(block, w_buf[lax.rem(j, 3), cols, :], NT, preferred_element_type=F32)
+            acc[:, cols] += lax.dot_general(block, w_buf[lax.rem(j, PEERS), cols, :], NT, preferred_element_type=F32)
 
         loop(2, columns)
 
@@ -916,7 +926,7 @@
         gx_step(0, i, d_loc[sp, :, pl.ds(pl.multiple_of(which(i) * BLK, BLK), BLK)])
         return carry
 
-    repeat(3, own_steps)
+    repeat(PEERS, own_steps)
 
     def remote_steps(k):
         d = source(k)
@@ -928,7 +938,7 @@
 
             gx_step(k, i, d_tok[before(d), :, pl.ds(pl.multiple_of(which(i) * BLK, BLK), BLK)])
             return carry
-        repeat(3, step)
+        repeat(PEERS, step)
 
     def send_a2(t):
         return remote(chip.at[t, y, :, pl.ds(0, HALF)], recv_a2.at[t], a2_send.at[t], a2_recv.at[t], (sp, step_z(t), y, core))
@@ -941,38 +951,39 @@
             full_a(t, i, d).wait()
         chip[t, y, :, :HALF] += full_y[0, t] + full_y[1, t]
 
-    def send_gw(cols, part, d):
-        return remote(gw_buf.at[sp, :, cols], gw_buf.at[sp, :, cols], g_send.at[part, d], g_recv.at[part, d], ring_sp(d))
-
-    pass_a(3)
-    sum_a(0)
-    send_a2(0).start()
-    remote_steps(1)
-    sum_a(1)
-    send_a2(1).start()
-    remote_steps(2)
-    sum_a(2)
-    send_a2(2).start()
-    for copy in scatter:
-        copy.wait()
-    fout[sp] = (fin[sp] + rc[0]) + (rc[1] + rc[2])
-    spread = [remote(fout.at[sp], fout.at[sp], f_send.at[d], f_recv.at[d], ring_sp(d)) for d in RING]
-    for copy in spread:
-        copy.start()
+    halves = (pl.ds(0, HALF), pl.ds(HALF, HALF))
+
+    def near_gw(part, i, d):
+        piece = gw_buf.at[sp, :, halves[part]]
+        return remote(piece, piece, g_send.at[part, i], g_recv.at[part, i], ring_sp(d))
+
+    def near_out(i, d):
+        return remote(fout.at[sp], fout.at[sp], f_send.at[i], f_recv.at[i], ring_sp(d))
+
+    def far_out(i, d):
+        piece = fout.at[mod4(sp + NSP - d), pl.ds(i * GROUP, GROUP)]
+        return remote(piece, piece, f_send.at[2 + i], f_recv.at[2 + i], ring_sp(d))
+
+    def far_gw(part, i, d):
+        piece = gw_buf.at[mod4(sp + NSP - d), pl.ds(i * GROUP, GROUP), halves[part]]
+        return remote(piece, piece, g_send.at[part, 2 + i], g_recv.at[part, 2 + i], ring_sp(d))
+
+    pass_a(PEERS)
+    for t in TRIO:
+        sum_a(t)
+        send_a2(t).start()
     for i, d in ways:
         full_b(i, d).wait()
     for i in QUAD:
-        sum_b[i] = chip[3, i, :, HALF:] + (full_z[0, i] + full_z[1, i])
+        sum_b[i] = chip[PEERS, i, :, HALF:] + (full_z[0, i] + full_z[1, i])
     for d in RING:
         send_b2(d).start()
-    sum_a(3)
+    sum_a(PEERS)
     for t in TRIO:
         send_a2(t).wait()
-    gw_buf[sp, :, :HALF] = (chip[3, y, :, :HALF] + recv_a2[0]) + (recv_a2[1] + recv_a2[2])
-    first, second = pl.ds(0, HALF), pl.ds(HALF, HALF)
-    grad_sends = [send_gw(first, 0, d) for d in RING]
-    for copy in grad_sends:
-        copy.start()
+    gw_buf[sp, :, :HALF] = (chip[PEERS, y, :, :HALF] + recv_a2[0]) + (recv_a2[1] + recv_a2[2])
+    for i, d in ways:
+        near_gw(0, i, d).start()
     drain(gtile.at[pl.ds(1, GROUP - 1)], t_send.at[0], t_recv.at[0])
     gpart[...] = jnp.sum(gtile[...], axis=0)
     gain_sends = [remote(gpart, gacross.at[before(d)], u_send.at[before(d)], u_recv.at[before(d)], ring_sp(d)) for d in RING]
@@ -981,11 +992,22 @@
     for d in RING:
         send_b2(d).wait()
     gw_buf[sp, :, HALF:] = (sum_b[y] + recv_b2[0]) + (recv_b2[1] + recv_b2[2])
-    more = [send_gw(second, 1, d) for d in RING]
-    for copy in more:
-        copy.start()
-    grad_sends += more
-    remote_steps(3)
+    for i, d in ways:
+        near_gw(1, i, d).start()
+    for copy in scatter:
+        copy.wait()
+    fout[sp] = (fin[sp] + rc[0]) + (rc[1] + rc[2])
+    for i, d in ways:
+        near_out(i, d).start()
+    for part in PAIR:
+        remote_steps(part + 1)
+        for i, d in ways:
+            near_gw(part, i, d).wait()
+            far_gw(part, i, d).start()
+    for i, d in ways:
+        near_out(i, d).wait()
+        far_out(i, d).start()
+    remote_steps(PEERS)
     gx_stage = gy_buf
     gx_stage[...] = acc[...].astype(jnp.bfloat16)
     store_gx = pltpu.make_async_copy(gx_stage, gx_hbm, out_sem.at[0])
@@ -995,14 +1017,15 @@
     gain_ref[...] = (gpart[...] + gacross[0]) + (gacross[1] + gacross[2])
     store_gain = pltpu.make_async_copy(gain_ref, gain_hbm, out_sem.at[1])
     store_gain.start()
-    for copy in grad_sends:
-        copy.wait()
+    for part in PAIR:
+        for i, d in ways:
+            far_gw(part, i, d).wait()
     store_gw = [pltpu.make_async_copy(gw_buf.at[s, :, pl.ds(m * BLK, BLK)], out.at[:, pl.ds(s * BLK, BLK)], out_sem.at[6 + m * NSP + s])
                 for m, out in enumerate((gq_hbm, gk_hbm, gv_hbm)) for s in QUAD]
     for copy in store_gw:
         copy.start()
-    for copy in spread:
-        copy.wait()
+    for i, d in ways:
+        far_out(i, d).wait()
     store_o = [pltpu.make_async_copy(fout.at[n], gwo_hbm.at[:, pl.ds(n * BLK, BLK)], out_sem.at[2 + n]) for n in QUAD]
     for copy in store_o:
         copy.start()
@@ -1018,26 +1041,26 @@
         tail_kernel,
         out_shape=[jax.ShapeDtypeStruct((BLK, WIDTH), BF16), ] + [jax.ShapeDtypeStruct((ROWS, WIDTH), F32)] * NSP + [
                    jax.ShapeDtypeStruct((SUB, TILE), F32)],
-        in_specs=[hbm] * 10 + [vmem], out_specs=[hbm] * 6,
-        scratch_shapes=[pltpu.VMEM((SUB, TILE), F32),
+        in_specs=[hbm] * 11, out_specs=[hbm] * 6,
+        scratch_shapes=[pltpu.VMEM(tiles.shape, F32), pltpu.VMEM((SUB, TILE), F32),
             pltpu.VMEM((NSP, BLK, QKV), BF16), pltpu.VMEM((2, WIDTH, BLK), BF16), pltpu.VMEM((2, NSP, 2, ROWS, QKV), F32),
             pltpu.VMEM((NSP, NSP, ROWS, QKV), F32), pltpu.VMEM((NSP, 2, ROWS, HALF // 2), F32), pltpu.VMEM((2, NSP, ROWS, HALF // 2), F32),
             pltpu.VMEM((2, NSP, ROWS, HALF), F32), pltpu.VMEM((2, NSP, ROWS, HALF), F32),
-            pltpu.VMEM((NSP, ROWS, HALF), F32), pltpu.VMEM((3, ROWS, HALF), F32), pltpu.VMEM((3, ROWS, HALF), F32),
-            pltpu.VMEM((3, BLK, QKV), BF16), pltpu.VMEM((3, WIDTH, BLK), BF16), pltpu.VMEM((BLK, WIDTH), F32), pltpu.VMEM((BLK, WIDTH), BF16),
-            pltpu.VMEM((NSP, ROWS, QKV), F32), pltpu.VMEM((GROUP, SUB, TILE), F32), pltpu.VMEM((SUB, TILE), F32), pltpu.VMEM((3, SUB, TILE), F32),
-            pltpu.VMEM(a_sum.shape, F32), pltpu.VMEM(b_sum.shape, F32), pltpu.VMEM((3,) + a_sum.shape[1:], F32), pltpu.VMEM((3,) + a_sum.shape[1:], F32),
-            pltpu.VMEM((NSP, ROWS, BLK), F32), pltpu.VMEM((3, ROWS, BLK), F32), pltpu.VMEM((NSP, ROWS, BLK), F32),
-            dma((7,)), dma((2,)), dma((3,)), dma((18,))] + dma_sems((NSP, NSP), (NSP,), (NSP, 2), (2,), (NSP,), (NSP,), (2, NSP), (1,), (NSP,), (NSP,), (NSP,), (NSP,), (NSP,), (NSP, 2), (2,)),
-        compiler_params=pltpu.CompilerParams(collective_id=3, has_side_effects=True, vmem_limit_bytes=62 * MIB),
+            pltpu.VMEM((NSP, ROWS, HALF), F32), pltpu.VMEM((PEERS, ROWS, HALF), F32), pltpu.VMEM((PEERS, ROWS, HALF), F32),
+            pltpu.VMEM((PEERS, BLK, QKV), BF16), pltpu.VMEM((PEERS, WIDTH, BLK), BF16), pltpu.VMEM((BLK, WIDTH), F32), pltpu.VMEM((BLK, WIDTH), BF16),
+            pltpu.VMEM((NSP, ROWS, QKV), F32), pltpu.VMEM((GROUP, SUB, TILE), F32), pltpu.VMEM((SUB, TILE), F32), pltpu.VMEM((PEERS, SUB, TILE), F32),
+            pltpu.VMEM(a_sum.shape, F32), pltpu.VMEM(b_sum.shape, F32), pltpu.VMEM((PEERS,) + a_sum.shape[1:], F32), pltpu.VMEM((PEERS,) + a_sum.shape[1:], F32),
+            pltpu.VMEM((NSP, ROWS, BLK), F32), pltpu.VMEM((PEERS, ROWS, BLK), F32), pltpu.VMEM((NSP, ROWS, BLK), F32),
+            dma((SUB,)), dma((2,)), dma((PEERS,)), dma((18,))] + dma_sems((NSP, NSP), (NSP,), (NSP, 2), (2,), (NSP,), (NSP,), (2, NSP), (1,), (NSP,), (NSP,), (NSP,), (NSP,), (NSP,), (NSP, 2), (2,)),
+        compiler_params=pltpu.CompilerParams(collective_id=PEERS, has_side_effects=True, vmem_limit_bytes=62 * MIB),
         cost_estimate=pl.CostEstimate(flops=60_000_000_000, bytes_accessed=60 * MIB, transcendentals=0),
         name='tail')(d_blocks, x_full, *[w.reshape(WIDTH, QKV) for w in weights], grad_y, a_sum, b_sum, dv_tok, tiles)
 
 
 def deliver_kernel(*refs):
-    count = (len(refs) - 2) // 3
-    sources, results, held = refs[:count], refs[count:2 * count], refs[2 * count:3 * count]
-    in_sem, out_sem = refs[3 * count:]
+    count = (len(refs) - 2) // PEERS
+    sources, results, held = refs[:count], refs[count:2 * count], refs[2 * count:PEERS * count]
+    in_sem, out_sem = refs[PEERS * count:]
     loads = [pltpu.make_async_copy(src, buf, in_sem.at[i]) for i, (src, buf) in enumerate(zip(sources, held))]
     stores = [pltpu.make_async_copy(buf, dst, out_sem.at[i]) for i, (buf, dst) in enumerate(zip(held, results))]
     for load in loads:

time: 274 us -> 265 us (0.967)
  Pallas kernels: 271 us -> 262 us
    pallas_call x1, Pallas kernels: 84.5 us -> 77.2 us  [tail(): pl.pallas_call(tail_kernel, out_shape=[jax.ShapeDtypeStruct((BLK, WIDTH),...]
where the time goes in v1:
time: 265 us
  Pallas kernels  262 us (99%)
    pallas_call x1, Pallas kernels, forward_pass(): pl.pallas_call(fwd_kernel, out_shape=[jax.ShapeDtypeStruct((NSP, BLK, WID...  128 us
    pallas_call x1, Pallas kernels, tail(): pl.pallas_call(tail_kernel, out_shape=[jax.ShapeDtypeStruct((BLK, WIDTH),...  77.2 us
    pallas_call x1, Pallas kernels, mid(): pl.pallas_call(mid_kernel, out_shape=[jax.ShapeDtypeStruct((NSP, BLK, QKV...  51.9 us

profile of v1, /device:TPU:0, one launch (start us, length us, event | category | flops | bytes accessed | tf_op | source)
XLA Modules:
  0.0 264.6 jit_solution(17053602196464296022)
XLA Ops:
  0.6 1.4 fusion.tile_hbm
  2.1 128.5 %forward.1 = (bf16[4,512,2048]{2,1,0:T(8,128)(2,1)}, bf16[4,512,512]{2,1,0:T(8,128)(2,1)}, bf16[4,512,512]{2,1,0:T(8,128)(2,1)}, bf16[4,512,512]{2,1,0:T(8,128)(...) custom-call(bf16[512,2048]{1,0:T(8,128)(2,1)} %bitcast.21, ...), custom_call_target="tpu_custom_call" | custom-call | flops 80000000000 | bytes 41943040 | tf_op jit(solution)/shard_map/forward/pallas_call | solution.py:506
  130.5 51.9 %middle.1 = (bf16[4,512,1536]{2,1,0:T(8,128)(2,1)}, f32[4,2,64,512]{3,2,1,0:T(8,128)}, f32[2,4,64,512]{3,2,1,0:T(8,128)}, bf16[4,512,512]{2,1,0:T(8,128)(2,1)}, f32[32,8,128]{2,1,0:T(8,128)}) custom-call(bf16[4,512,512]{2,1,0:T(8,128)(2,1)} %get-tuple-element.46.ot_hbm, bf16[512,2048]{1,0:T(8,128)(2,1)} %get-tuple-element.47.ga_hbm, ...), custom_call_target="tpu_custom_call" | custom-call | flops 60000002048 | bytes 33554432 | tf_op jit(solution)/shard_map/middle/pallas_call | solution.py:750
  182.4 77.2 %tail.1 = (bf16[512,2048]{1,0:T(8,128)(2,1)}, f32[64,2048]{1,0:T(8,128)}, f32[64,2048]{1,0:T(8,128)}, f32[64,2048]{1,0:T(8,128)}, f32[64,2048]{1,0:T(8,128)}, /*index=5*/f32[8,128]{1,0:T(8,128)}) custom-call(bf16[4,512,1536]{2,1,0:T(8,128)(2,1)} %get-tuple-element.59.d_hbm, bf16[2048,2048]{1,0:T(8,128)(2,1)} %bitcast.26, bf16[2048,1536]{1,0:T(8,128)(2,1)} %bitcast.27, ...), custom_call_target="tpu_custom_call" | custom-call | flops 60000002048 | bytes 62914560 | tf_op jit(solution)/shard_map/tail/pallas_call | solution.py:1040
  259.6 0.0 copy-start
  259.6 4.4 %deliver.1 = (bf16[512,2048]{1,0:T(8,128)(2,1)}, bf16[512,2048]{1,0:T(8,128)(2,1)}, f32[64,2048]{1,0:T(8,128)}, f32[64,2048]{1,0:T(8,128)}, f32[64,2048]{1,0:T(8,128)}, /*index=5*/f32[64,2048]{1,0:T(8,128)}) custom-call(bf16[512,2048]{1,0:T(8,128)(2,1)} %get-tuple-element.45.refs_0_, bf16[512,2048]{1,0:T(8,128)(2,1)} %get-tuple-element.69.refs_1_, ...), custom_call_target="tpu_custom_call" | custom-call | tf_op jit(solution)/shard_map/deliver/pallas_call | solution.py:1078
  264.0 0.0 copy-done
  264.0 0.1 constant_dynamic-slice_fusion
  264.0 0.5 slice_bitcast_fusion
Async XLA Ops:
  259.6 4.4 %copy-start = (f32[8,128]{1,0:T(8,128)S(1)}, f32[8,128]{1,0:T(8,128)}, u32[]{:S(2)}) copy-start(f32[8,128]{1,0:T(8,128)} %get-tuple-element.80) | copy-start | bytes 12292

commit v2 on v1

--- a/solution.py
+++ b/solution.py
@@ -73,17 +73,6 @@
     return lax.axis_index('sp'), lax.axis_index('z'), lax.axis_index('y'), lax.axis_index('core')
 
 
-def fsdp_index():
-    sp, z, y, core = my_coords()
-    return z * SUB + y * 2 + core
-
-
-def fsdp_peer(step):
-    sp = lax.axis_index('sp')
-    f = lax.rem(fsdp_index() + step, GROUP)
-    return f, (sp, f // SUB, mod4(f // 2), parity(f))
-
-
 def mod4(value):
     return lax.rem(value, NSP)
 
@@ -122,10 +111,10 @@
 
 def local_gains(gt_ref, grow):
     lane = lax.broadcasted_iota(jnp.int32, (1, TILE), 1) < HALF_HEAD
-    first = lax.axis_index('sp') * SUB
+    sp = lax.axis_index('sp')
     for h in QUAD:
         for m in PAIR:
-            grow[m:m + 1, h * TILE:(h + 1) * TILE] = jnp.where(lane, gt_ref[first + 2 * h, m:m + 1, :], gt_ref[first + 2 * h + 1, m:m + 1, :])
+            grow[m:m + 1, h * TILE:(h + 1) * TILE] = jnp.where(lane, gt_ref[sp, h, 0, m:m + 1, :], gt_ref[sp, h, 1, m:m + 1, :])
 
 
 def inv_columns(inv_ref, invc):
@@ -138,13 +127,12 @@
     return pltpu.make_async_remote_copy(src_ref=src, dst_ref=dst, send_sem=send, recv_sem=recv, device_id=peer, device_id_type=MESH)
 
 
-def greet_all():
+def greet(rings):
     barrier = pltpu.get_barrier_semaphore()
-    for step in range(1, GROUP):
-        pl.semaphore_signal(barrier, device_id=fsdp_peer(step)[1], device_id_type=MESH)
-    for d in RING:
-        pl.semaphore_signal(barrier, device_id=ring_sp(d), device_id_type=MESH)
-    pl.semaphore_wait(barrier, 34)
+    peers = [ring(d) for ring in rings for d in RING] + [partner()]
+    for peer in peers:
+        pl.semaphore_signal(barrier, device_id=peer, device_id_type=MESH)
+    pl.semaphore_wait(barrier, len(peers))
 
 
 def fill_rope(ca_ref, sa_ref, cb_ref, sb_ref, cos_scr, sin_scr):
@@ -168,62 +156,47 @@
 
 def gather_stages(buf, g, sems):
     sp, z, y, core = my_coords()
-    a1_send, a1_recv, b1_send, b1_recv, near_send, near_recv, far_send, far_recv, c_send, c_recv = sems
+    first, near, far, both = [(sems[2 * k].at[g], sems[2 * k + 1].at[g]) for k in range(NSP)]
     low, high = pl.ds(0, GROUP), pl.ds(GROUP, GROUP)
     ways = tuple(enumerate((1, PEERS)))
 
-    def first(d):
-        own_low, own_high = buf.at[z, y, core, low], buf.at[z, y, core, high]
-        return (remote(own_low, own_low, a1_send.at[g, before(d)], a1_recv.at[g, before(d)], ring_z(d)),
-                remote(own_high, own_high, b1_send.at[g, before(d)], b1_recv.at[g, before(d)], ring_y(d)))
+    def send(piece, pair, peer):
+        remote(piece, piece, *pair, peer).start()
 
     def send_near(e):
-        along_y, along_z = buf.at[mod4(z + NSP - e), y, core, low], buf.at[z, mod4(y + NSP - e), core, high]
         for i, d in ways:
-            remote(along_y, along_y, near_send.at[g, i], near_recv.at[g, i], ring_y(d)).start()
-            remote(along_z, along_z, near_send.at[g, 2 + i], near_recv.at[g, 2 + i], ring_z(d)).start()
-
-    def across(e):
-        piece = buf.at[mod4(z + NSP - e), :, core]
-        return remote(piece, piece, c_send.at[g, e], c_recv.at[g, e], partner())
+            send(buf.at[mod4(z + NSP - e), y, core, low], near, ring_y(d))
+            send(buf.at[z, mod4(y + NSP - e), core, high], near, ring_z(d))
 
     def begin():
         for d in RING:
-            for copy in first(d):
-                copy.start()
+            send(buf.at[z, y, core, low], first, ring_z(d))
+            send(buf.at[z, y, core, high], first, ring_y(d))
         send_near(0)
 
     def pass_on():
+        drain(buf.at[0, pl.ds(0, PEERS), core], *first)
         for e in RING:
-            for copy in first(e):
-                copy.wait()
             send_near(e)
 
     def relay():
+        drain(buf.at[:, :, core, low], *near)
         for i, d in ways:
-            drain(buf.at[:, y, core, low], near_send.at[g, i], near_recv.at[g, i])
-            piece = buf.at[:, mod4(y + NSP - d), core, pl.ds(i * PART, PART)]
-            remote(piece, piece, far_send.at[g, i], far_recv.at[g, i], ring_y(d)).start()
-            drain(buf.at[z, :, core, high], near_send.at[g, 2 + i], near_recv.at[g, 2 + i])
-            piece = buf.at[mod4(z + NSP - d), :, core, pl.ds(GROUP + i * PART, PART)]
-            remote(piece, piece, far_send.at[g, 2 + i], far_recv.at[g, 2 + i], ring_z(d)).start()
+            send(buf.at[:, mod4(y + NSP - d), core, pl.ds(i * PART, PART)], far, ring_y(d))
+            send(buf.at[mod4(z + NSP - d), :, core, pl.ds(GROUP + i * PART, PART)], far, ring_z(d))
 
     def share():
-        for i, d in ways:
-            drain(buf.at[:, y, core, pl.ds(0, PART)], far_send.at[g, i], far_recv.at[g, i])
-            drain(buf.at[z, :, core, pl.ds(0, PART)], far_send.at[g, 2 + i], far_recv.at[g, 2 + i])
-        for e in QUAD:
-            across(e).start()
+        drain(buf.at[:, :, core, pl.ds(0, PART)], *far)
+        send(buf.at[:, :, core], both, partner())
 
     def finish():
-        for e in QUAD:
-            across(e).wait()
+        drain(buf.at[:, :, core], *both)
 
     return begin, pass_on, relay, share, finish
 
 
 def gather_sems(groups):
-    return dma_sems((groups, PEERS), (groups, PEERS), (groups, NSP), (groups, NSP), (groups, NSP))
+    return dma_sems((groups,), (groups,), (groups,), (groups,))
 
 
 def norm_and_grad(acc, x, grad_y, gain, y_out, grad_out, post):
@@ -249,7 +222,6 @@
                tile_ref, ca_ref, sa_ref, cb_ref, sb_ref, inv_ref, gt_ref, post_ref, xf, wl, wo, q0, k0, v, qr, kr, o, ot, lse, s_scr, vt_scr, cos_scr, sin_scr, st, st_in, grow, gpost, invc,
                ld_sem, out_sem, own_send, own_recv, fw_send, fw_recv, t_send, t_recv, u_send, u_recv, o_send, o_recv, *w_sems):
     sp, z, y, core = my_coords()
-    me = fsdp_index()
     right, left = ring_sp(1), ring_sp(PEERS)
     far = mod4(sp + 2)
     w_rows = (wq_hbm, wk_hbm, wv_hbm)
@@ -267,7 +239,7 @@
         loads.insert(0, pltpu.make_async_copy(*pair, out_sem.at[k]))
     for load in loads:
         load.start()
-    greet_all()
+    greet((ring_sp, ring_z, ring_y))
 
     def chunk(c):
         return pl.ds(pl.multiple_of(c * TILE, TILE), TILE)
@@ -279,9 +251,10 @@
         own_x(0, right_c).start()
         own_x(1, left_c).start()
 
-    tile_sends = []
-    for step in range(1, GROUP):
-        tile_sends.append(remote(tile_ref, gt_ref.at[me], t_send.at[0], t_recv.at[0], fsdp_peer(step)[1]))
+    def send_tiles(k, tiles, peers):
+        for peer in peers:
+            remote(tiles, tiles, t_send.at[k], t_recv.at[k], peer).start()
+
     for load in loads[:SUB]:
         load.wait()
     stages = [gather_stages(buf, g, w_sems) for g, buf in enumerate((wl, wo, wa_hbm, wb_hbm, wc_hbm))]
@@ -302,11 +275,12 @@
         stages[g][NSP]()
 
     begin(0)
-    for copy in tile_sends:
-        copy.start()
-    gt_ref[me] = tile_ref[:, :]
+    gt_ref[z, y, core] = tile_ref[:, :]
+    send_tiles(0, gt_ref.at[z, y, core], [ring_z(d) for d in RING])
     fill_rope(ca_ref, sa_ref, cb_ref, sb_ref, cos_scr, sin_scr)
     pass_on(0)
+    drain(gt_ref.at[pl.ds(0, PEERS), 0, 0], t_send.at[0], t_recv.at[0])
+    send_tiles(1, gt_ref.at[:, y, core], [ring_y(d) for d in RING])
 
     def forward(side, i):
         block = mod4(sp + (PEERS, 1)[side])
@@ -320,6 +294,8 @@
 
     forward_x(0)
     relay(0)
+    drain(gt_ref.at[:, pl.ds(0, PEERS), 0], t_send.at[1], t_recv.at[1])
+    send_tiles(2, gt_ref.at[:, :, core], [partner()])
     for load in loads[SUB:]:
         load.wait()
     for g in RING + (NSP,):
@@ -376,11 +352,11 @@
         stores[-1].start()
     relay(2)
     share(1)
-    drain(gt_ref.at[pl.ds(1, GROUP - 1)], t_send.at[0], t_recv.at[0])
+    drain(gt_ref.at[:, :, 0], t_send.at[2], t_recv.at[2])
     local_gains(gt_ref, grow)
     lane = lax.broadcasted_iota(jnp.int32, (1, TILE), 1) < HALF_HEAD
     for i in range(WIDTH // TILE):
-        gpost[:, i * TILE:(i + 1) * TILE] = jnp.broadcast_to(jnp.where(lane, gt_ref[2 * i, 2:PEERS, :], gt_ref[2 * i + 1, 2:PEERS, :]), (SUB, TILE))
+        gpost[:, i * TILE:(i + 1) * TILE] = jnp.broadcast_to(jnp.where(lane, gt_ref[i // NSP, i % NSP, 0, 2:PEERS, :], gt_ref[i // NSP, i % NSP, 1, 2:PEERS, :]), (SUB, TILE))
     for copy in stats:
         copy.wait()
     total = (st[:, :] + st_in[0]) + (st_in[1] + st_in[2])
@@ -392,7 +368,7 @@
 
     def send_o(h, d):
         lanes = pl.ds(pl.multiple_of(h * TILE, TILE), TILE)
-        return remote(o.at[mod4(sp + d), :, lanes], ot.at[sp, :, lanes], o_send.at[h, before(d)], o_recv.at[h, before(d)], ring_sp(d))
+        return remote(o.at[mod4(sp + d), :, lanes], ot.at[sp, :, lanes], o_send.at[h], o_recv.at[h], ring_sp(d))
 
     def head(h, carry):
         lanes = pl.ds(pl.multiple_of(h * TILE, TILE), TILE)
@@ -449,9 +425,8 @@
     acc = s_scr.at[0]
 
     def project_out(h):
-        for d in RING:
-            send_o(h, d).wait()
         lanes = pl.ds(pl.multiple_of(h * TILE, TILE), TILE)
+        drain(ot.at[pl.ds(0, PEERS), :, lanes], o_send.at[h], o_recv.at[h])
         mine = jnp.concatenate([ot[s, :, lanes] for s in QUAD], axis=1)
         for n in QUAD:
             part = jnp.dot(mine, wo[:, h, :, :, n * BLK:(n + 1) * BLK].reshape(BLK, BLK), preferred_element_type=F32)
@@ -506,13 +481,13 @@
     return pl.pallas_call(
         fwd_kernel,
         out_shape=[jax.ShapeDtypeStruct((NSP, BLK, WIDTH), BF16)] + [wide] * 7 + [jax.ShapeDtypeStruct((NSP, SUB, SEQ), F32), tokens, tokens, wide] + [weight] * NSP + [
-            jax.ShapeDtypeStruct((SUB, BLK), F32), jax.ShapeDtypeStruct((GROUP, SUB, TILE), F32), jax.ShapeDtypeStruct((SUB, WIDTH), F32)],
+            jax.ShapeDtypeStruct((SUB, BLK), F32), jax.ShapeDtypeStruct(blocks[:PEERS] + (SUB, TILE), F32), jax.ShapeDtypeStruct((SUB, WIDTH), F32)],
         in_specs=[hbm] * 11, out_specs=[hbm] * 19,
-        scratch_shapes=[pltpu.VMEM(a.shape, F32) for a in (gain_tile, *tables)] + [pltpu.VMEM((SUB, BLK), F32), pltpu.VMEM((GROUP, SUB, TILE), F32), pltpu.VMEM((SUB, WIDTH), F32), pltpu.VMEM((NSP, BLK, WIDTH), BF16), pltpu.VMEM(blocks + (QKV,), BF16), pltpu.VMEM(blocks + (WIDTH,), BF16)] + [pltpu.VMEM(quad, BF16)] * 7 + [
+        scratch_shapes=[pltpu.VMEM(a.shape, F32) for a in (gain_tile, *tables)] + [pltpu.VMEM((SUB, BLK), F32), pltpu.VMEM(blocks[:PEERS] + (SUB, TILE), F32), pltpu.VMEM((SUB, WIDTH), F32), pltpu.VMEM((NSP, BLK, WIDTH), BF16), pltpu.VMEM(blocks + (QKV,), BF16), pltpu.VMEM(blocks + (WIDTH,), BF16)] + [pltpu.VMEM(quad, BF16)] * 7 + [
             pltpu.VMEM((NSP, SUB, SEQ), F32), pltpu.VMEM((2,) + quad, F32), pltpu.VMEM((TILE, SEQ), BF16),
             pltpu.VMEM((SEQ, TILE), F32), pltpu.VMEM((SEQ, TILE), F32), pltpu.VMEM((SUB, BLK), F32), pltpu.VMEM((PEERS, SUB, BLK), F32), pltpu.VMEM((SUB, BLK), F32),
             pltpu.VMEM((SUB, WIDTH), F32), pltpu.VMEM((2, NSP, BLK, TILE), F32),
-            pltpu.SemaphoreType.DMA((14,)), pltpu.SemaphoreType.DMA((13,))] + dma_sems((2, NSP), (2, 2), (1,), (PEERS,), (NSP, PEERS)) + gather_sems(5),
+            pltpu.SemaphoreType.DMA((14,)), pltpu.SemaphoreType.DMA((13,))] + dma_sems((2, NSP), (2, 2), (PEERS,), (PEERS,), (NSP,)) + gather_sems(5),
         compiler_params=pltpu.CompilerParams(collective_id=1, has_side_effects=True, vmem_limit_bytes=VMEM_LIMIT),
         cost_estimate=pl.CostEstimate(flops=80_000_000_000, bytes_accessed=40 * MIB, transcendentals=0),
         name='forward')(x, grad_y, wq_rows, wk_rows, wv_rows, wo_rows, gain_tile, *tables)
@@ -541,16 +516,12 @@
     load_ot = group([(ot_hbm, ot), (ga_hbm, ga)], in_sem.at[0])
     load_aux = group(((inv_hbm, inv_ref), (gt_hbm, gt_ref), (post_hbm, post_ref), (ca_hbm, ca_ref), (sa_hbm, sa_ref), (cb_hbm, cb_ref), (sb_hbm, sb_ref)), in_sem.at[1])
 
-    barrier = pltpu.get_barrier_semaphore()
-    greeted = [ring(d) for ring in (ring_sp, ring_z, ring_y) for d in RING] + [partner()]
-    for peer in greeted:
-        pl.semaphore_signal(barrier, device_id=peer, device_id_type=MESH)
-    pl.semaphore_wait(barrier, len(greeted))
+    greet((ring_sp, ring_z, ring_y))
 
     def send_do(h, d):
-        return remote(ds_hbm.at[mod4(sp + d), :, lanes_of(h)], do.at[sp, :, lanes_of(h)], do_send.at[h, d], do_recv.at[h, d], ring_sp(d))
-
-    send_grad = remote(ga_hbm, gap, c_send.at[NSP], c_recv.at[NSP], partner())
+        return remote(ds_hbm.at[mod4(sp + d), :, lanes_of(h)], do.at[sp, :, lanes_of(h)], do_send.at[h], do_recv.at[h], ring_sp(d))
+
+    send_grad = remote(ga_hbm, gap, c_send.at[1], c_recv.at[1], partner())
     send_grad.start()
     for h in QUAD:
         for d in RING:
@@ -563,7 +534,7 @@
         return pl.ds(pl.multiple_of(i * TILE + c * ROWS, ROWS), ROWS)
 
     def send_core(i):
-        return remote(ott.at[:, core_rows(i, other_core(core))], otp.at[:, i], c_send.at[i], c_recv.at[i], partner())
+        return remote(ott.at[:, core_rows(i, other_core(core))], otp.at[:, i], c_send.at[0], c_recv.at[0], partner())
 
     for s in QUAD:
         ott[s] = ot[s].T
@@ -589,10 +560,10 @@
         return remote(chip.at[0, 2 + i, k], half_z.at[k, i], b1_send.at[k, i], b1_recv.at[k, i], ring_z(d))
 
     def sum_a(t, i, d):
-        return remote(chip.at[t, low, mod4(y + d)], full_y.at[i, t], a2_send.at[t, i], a2_recv.at[t, i], ring_y(d))
+        return remote(chip.at[t, low, mod4(y + d)], full_y.at[i, t], a2_send.at[0], a2_recv.at[0], ring_y(d))
 
     def sum_b(k, i, d):
-        return remote(chip.at[1 + i, high, k], full_z.at[i, k], b2_send.at[k, i], b2_recv.at[k, i], ring_z(d))
+        return remote(chip.at[1 + i, high, k], full_z.at[i, k], b2_send.at[0], b2_recv.at[0], ring_z(d))
 
     def pass_on(t):
         for i, d in ways:
@@ -605,8 +576,7 @@
             sum_b(t, i, d).start()
 
     send_grad.wait()
-    for i in QUAD:
-        send_core(i).wait()
+    drain(otp, c_send.at[0], c_recv.at[0])
 
     def wgrad(t):
         block = step_z(t)
@@ -637,12 +607,11 @@
         big[m, i, :, lanes] = grad * grow[m:m + 1, lanes]
 
     def send_dv(h, d):
-        return remote(va.at[mod4(sp + d), :, lanes_of(h)], dvt_hbm.at[sp, :, lanes_of(h)], v_send.at[h, d], v_recv.at[h, d], ring_sp(d))
+        return remote(va.at[mod4(sp + d), :, lanes_of(h)], dvt_hbm.at[sp, :, lanes_of(h)], v_send.at[0], v_recv.at[0], ring_sp(d))
 
     def head(h):
         lanes = lanes_of(h)
-        for d in RING:
-            send_do(h, d).wait()
+        drain(do.at[pl.ds(0, PEERS), :, lanes], do_send.at[h], do_recv.at[h])
 
         @pl.when(h > 0)
         def _():
@@ -690,7 +659,7 @@
                 term = big[m, i, :, lanes] * ref[i, :, lanes].astype(F32)
                 part = plus(part, term)
             st[m * NSP + i:m * NSP + i + 1, :] = row_sum((part * invc[m, i]).T)
-    stats = [remote(st, st_in.at[before(d)], u_send.at[d], u_recv.at[d], ring_sp(d)) for d in RING]
+    stats = [remote(st, st_in.at[before(d)], u_send.at[before(d)], u_recv.at[before(d)], ring_sp(d)) for d in RING]
     for copy in stats:
         copy.start()
     for d in RING:
@@ -700,13 +669,13 @@
     tile_ref[:, :, :] = jnp.zeros_like(tile_ref)
     for i in range(WIDTH // TILE):
         total = row_sum(post_ref[:, i * TILE:(i + 1) * TILE])
-        tile_ref[2 * i, 2:PEERS, :] = total
-        tile_ref[2 * i + 1, 2:PEERS, :] = total
+        for c in PAIR:
+            tile_ref[i // NSP, i % NSP, c, 2:PEERS, :] = total
     for m in PAIR:
         for h in QUAD:
             total = row_sum(gacc[m, :, h * TILE:(h + 1) * TILE])
             for c in PAIR:
-                tile_ref[sp * SUB + 2 * h + c, m:m + 1, :] = total
+                tile_ref[sp, h, c, m:m + 1, :] = total
 
     store_v += group([(tile_ref, tile_hbm)], out_sem.at[PEERS])
     for copy in stats:
@@ -721,16 +690,13 @@
                 ref[i, :, lanes] = (invc[m, i] * (big[m, i, :, lanes] - hat * proj)).astype(BF16)
     store_d = group([(ref, d_hbm.at[:, :, block_cols(m)]) for m, ref in enumerate(kept)], out_sem.at[2])
 
+    drain(full_y, a2_send.at[0], a2_recv.at[0])
+    drain(full_z, b2_send.at[0], b2_recv.at[0])
     for t in QUAD:
-        for i, d in ways:
-            sum_a(t, i, d).wait()
-            sum_b(t, i, d).wait()
         chip[t, low, y] += full_y[0, t] + full_y[1, t]
         chip[NSP - 1, high, t] += full_z[0, t] + full_z[1, t]
     store_w = group([(chip.at[t, low, y], as_hbm.at[t]) for t in QUAD] + [(chip.at[NSP - 1, high], bs_hbm)], out_sem.at[0])
-    for h in QUAD:
-        for d in RING:
-            send_dv(h, d).wait()
+    drain(dvt_hbm.at[pl.ds(0, PEERS)], v_send.at[0], v_recv.at[0])
     for copy in store_v + store_d + store_w:
         copy.wait()
 
@@ -741,7 +707,7 @@
     quad = (NSP, BLK, BLK)
     tokens = (BLK, WIDTH)
     pair = (2, ROWS, BLK)
-    sems = dma_sems((NSP, NSP), (NSP + 1,), (NSP, 2), (NSP, 2), (NSP, 2), (NSP, 2), (NSP,), (NSP, NSP))
+    sems = dma_sems((NSP,), (2,), (NSP, 2), (NSP, 2), (1,), (1,), (PEERS,), (1,))
     half = [pltpu.VMEM(shape, BF16) for shape in (quad, tokens, tokens) + (quad,) * SUB + ((NSP, NSP, ROWS, BLK),)]
     scratch = half + [pltpu.VMEM(shape, F32) for shape in (
         (2,) + quad, (NSP, NSP, NSP, ROWS, BLK), (NSP,) + pair, (NSP,) + pair, (2, NSP) + pair, (2, NSP) + pair,
@@ -761,13 +727,12 @@
 
 def tail_kernel(d_hbm, x_hbm, wl_hbm, wa_hbm, wb_hbm, wc_hbm, gy_hbm, as_hbm, bs_hbm, dvt_hbm, tile_hbm,
                 gx_hbm, gq_hbm, gk_hbm, gv_hbm, gwo_hbm, gain_hbm, tile_ref, gain_ref,
-                d_loc, x_col, part, chip, half_y, half_z, full_y, full_z, sum_b, recv_a2, recv_b2, d_tok, w_buf, acc, gy_buf, gw_buf, gtile, gpart, gacross,
+                d_loc, x_col, part, chip, half_y, half_z, full_y, full_z, sum_b, recv_a2, recv_b2, d_tok, w_buf, acc, gy_buf, gw_buf, tile_y, tile_z, tile_c, gpart, gacross,
                 o_a, o_b, o_ra, o_rb, fin, rc, fout,
                 ld_sem, x_sem, w_sem, out_sem, d_send, d_recv, c_send, c_recv, a1_send, a1_recv, b1_send, b1_recv,
                 a2_send, a2_recv, b2_send, b2_recv, g_send, g_recv, t_send, t_recv, u_send, u_recv,
                 oa_send, oa_recv, ob_send, ob_recv, s_send, s_recv, f_send, f_recv, f1_send, f1_recv, f2_send, f2_recv):
     sp, z, y, core = my_coords()
-    me = fsdp_index()
 
     load_o = [pltpu.make_async_copy(as_hbm, o_a, ld_sem.at[2]), pltpu.make_async_copy(bs_hbm, o_b, ld_sem.at[PEERS])]
     load_d = pltpu.make_async_copy(d_hbm, d_loc, ld_sem.at[0])
@@ -802,14 +767,10 @@
             def _():
                 load_w(j, src).start()
 
-    greet_all()
+    greet((ring_sp, ring_z, ring_y))
     load_tile.wait()
-    tile_sends = []
-    for step in range(1, GROUP):
-        f, peer = fsdp_peer(step)
-        tile_sends.append(remote(tile_ref.at[f], gtile.at[me], t_send.at[0], t_recv.at[0], peer))
-        tile_sends[-1].start()
-    gtile[me] = tile_ref[me]
+    for d in RING:
+        remote(tile_ref.at[:, mod4(y + d)], tile_y.at[before(d)], t_send.at[0], t_recv.at[0], ring_y(d)).start()
 
     def send_d(d, m):
         return remote(d_hbm.at[mod4(sp + d), :, pl.ds(m * BLK, BLK)], d_tok.at[before(d), :, pl.ds(m * BLK, BLK)],
@@ -822,12 +783,12 @@
     for load in load_o:
         load.wait()
     low, high = pl.ds(0, 2), pl.ds(2, 2)
-    o_sends = [remote(o_a.at[t], o_ra.at[t], oa_send.at[t], oa_recv.at[t], ring_z(d)) for t, d in enumerate((2, 1, PEERS))]
-    o_sends += [remote(o_b.at[:, mod4(y + d)], o_rb.at[before(d)], ob_send.at[d], ob_recv.at[d], ring_y(d)) for d in RING]
+    o_sends = [remote(o_a.at[t], o_ra.at[t], oa_send.at[0], oa_recv.at[0], ring_z(d)) for t, d in enumerate((2, 1, PEERS))]
+    o_sends += [remote(o_b.at[:, mod4(y + d)], o_rb.at[before(d)], ob_send.at[0], ob_recv.at[0], ring_y(d)) for d in RING]
     for copy in o_sends:
         copy.start()
-    for d in (1, PEERS, 2):
-        for m in PAIR:
+    for m in PAIR:
+        for d in (1, PEERS):
             send_d(d, m).start()
 
     load_d.wait()
@@ -892,18 +853,21 @@
         return carry
 
     repeat(NSP, wgrad_step)
-    finish(PEERS)
+    drain(tile_y, t_send.at[0], t_recv.at[0])
+    tile_ref[:, y] = (tile_ref[:, y] + tile_y[0]) + (tile_y[1] + tile_y[2])
+    for d in RING:
+        remote(tile_ref.at[mod4(z + d), y], tile_z.at[before(d)], t_send.at[1], t_recv.at[1], ring_z(d)).start()
+    drain(o_ra, oa_send.at[0], oa_recv.at[0])
+    drain(o_rb, ob_send.at[0], ob_recv.at[0])
+    fin[low] = (o_a[NSP - 1] + o_ra[0]) + (o_ra[1] + o_ra[2])
+    fin[high] = (o_b[:, y] + o_rb[0]) + (o_rb[1] + o_rb[2])
+    scatter = [remote(fin.at[mod4(sp + d)], rc.at[before(d)], s_send.at[0], s_recv.at[0], ring_sp(d)) for d in RING]
+    for copy in scatter:
+        copy.start()
+    for m in PAIR:
+        send_d(2, m).start()
     pass_a(0)
     pass_a(1)
-    pass_b()
-    pass_a(2)
-    for copy in o_sends:
-        copy.wait()
-    fin[low] = (o_a[NSP - 1] + o_ra[0]) + (o_ra[1] + o_ra[2])
-    fin[high] = (o_b[:, y] + o_rb[0]) + (o_rb[1] + o_rb[2])
-    scatter = [remote(fin.at[mod4(sp + d)], rc.at[before(d)], s_send.at[d], s_recv.at[d], ring_sp(d)) for d in RING]
-    for copy in scatter:
-        copy.start()
     for load in load_v + [load_gy]:
         load.wait()
     acc[...] = gy_buf[...].astype(F32)
@@ -928,6 +892,12 @@
 
     repeat(PEERS, own_steps)
 
+    finish(PEERS)
+    pass_b()
+    pass_a(2)
+    drain(tile_z, t_send.at[1], t_recv.at[1])
+    tile_ref[z, y] = (tile_ref[z, y] + tile_z[0]) + (tile_z[1] + tile_z[2])
+    remote(tile_ref.at[z, y, other_core(core)], tile_c, t_send.at[2], t_recv.at[2], partner()).start()
     def remote_steps(k):
         d = source(k)
 
@@ -941,10 +911,10 @@
         repeat(PEERS, step)
 
     def send_a2(t):
-        return remote(chip.at[t, y, :, pl.ds(0, HALF)], recv_a2.at[t], a2_send.at[t], a2_recv.at[t], (sp, step_z(t), y, core))
+        return remote(chip.at[t, y, :, pl.ds(0, HALF)], recv_a2.at[t], a2_send.at[0], a2_recv.at[0], (sp, step_z(t), y, core))
 
     def send_b2(d):
-        return remote(sum_b.at[mod4(y + d)], recv_b2.at[before(d)], b2_send.at[before(d)], b2_recv.at[before(d)], ring_y(d))
+        return remote(sum_b.at[mod4(y + d)], recv_b2.at[before(d)], b2_send.at[0], b2_recv.at[0], ring_y(d))
 
     def sum_a(t):
         for i, d in ways:
@@ -968,10 +938,12 @@
         piece = gw_buf.at[mod4(sp + NSP - d), pl.ds(i * GROUP, GROUP), halves[part]]
         return remote(piece, piece, g_send.at[part, 2 + i], g_recv.at[part, 2 + i], ring_sp(d))
 
+    remote_steps(1)
     pass_a(PEERS)
     for t in TRIO:
         sum_a(t)
         send_a2(t).start()
+    remote_steps(2)
     for i, d in ways:
         full_b(i, d).wait()
     for i in QUAD:
@@ -979,48 +951,43 @@
     for d in RING:
         send_b2(d).start()
     sum_a(PEERS)
-    for t in TRIO:
-        send_a2(t).wait()
+    drain(recv_a2, a2_send.at[0], a2_recv.at[0])
     gw_buf[sp, :, :HALF] = (chip[PEERS, y, :, :HALF] + recv_a2[0]) + (recv_a2[1] + recv_a2[2])
     for i, d in ways:
         near_gw(0, i, d).start()
-    drain(gtile.at[pl.ds(1, GROUP - 1)], t_send.at[0], t_recv.at[0])
-    gpart[...] = jnp.sum(gtile[...], axis=0)
-    gain_sends = [remote(gpart, gacross.at[before(d)], u_send.at[before(d)], u_recv.at[before(d)], ring_sp(d)) for d in RING]
+    drain(tile_c, t_send.at[2], t_recv.at[2])
+    gpart[...] = tile_ref[z, y, core] + tile_c[...]
+    gain_sends = [remote(gpart, gacross.at[before(d)], u_send.at[0], u_recv.at[0], ring_sp(d)) for d in RING]
     for copy in gain_sends:
         copy.start()
-    for d in RING:
-        send_b2(d).wait()
+    drain(recv_b2, b2_send.at[0], b2_recv.at[0])
     gw_buf[sp, :, HALF:] = (sum_b[y] + recv_b2[0]) + (recv_b2[1] + recv_b2[2])
     for i, d in ways:
         near_gw(1, i, d).start()
-    for copy in scatter:
-        copy.wait()
+    drain(rc, s_send.at[0], s_recv.at[0])
     fout[sp] = (fin[sp] + rc[0]) + (rc[1] + rc[2])
     for i, d in ways:
         near_out(i, d).start()
     for part in PAIR:
-        remote_steps(part + 1)
         for i, d in ways:
             near_gw(part, i, d).wait()
             far_gw(part, i, d).start()
+    remote_steps(PEERS)
     for i, d in ways:
         near_out(i, d).wait()
         far_out(i, d).start()
-    remote_steps(PEERS)
     gx_stage = gy_buf
     gx_stage[...] = acc[...].astype(jnp.bfloat16)
     store_gx = pltpu.make_async_copy(gx_stage, gx_hbm, out_sem.at[0])
     store_gx.start()
-    for copy in gain_sends:
-        copy.wait()
+    drain(gacross, u_send.at[0], u_recv.at[0])
     gain_ref[...] = (gpart[...] + gacross[0]) + (gacross[1] + gacross[2])
     store_gain = pltpu.make_async_copy(gain_ref, gain_hbm, out_sem.at[1])
     store_gain.start()
     for part in PAIR:
         for i, d in ways:
             far_gw(part, i, d).wait()
-    store_gw = [pltpu.make_async_copy(gw_buf.at[s, :, pl.ds(m * BLK, BLK)], out.at[:, pl.ds(s * BLK, BLK)], out_sem.at[6 + m * NSP + s])
+    store_gw = [pltpu.make_async_copy(gw_buf.at[s, :, pl.ds(m * BLK, BLK)], out.at[:, pl.ds(s * BLK, BLK)], out_sem.at[6])
                 for m, out in enumerate((gq_hbm, gk_hbm, gv_hbm)) for s in QUAD]
     for copy in store_gw:
         copy.start()
@@ -1029,7 +996,8 @@
     store_o = [pltpu.make_async_copy(fout.at[n], gwo_hbm.at[:, pl.ds(n * BLK, BLK)], out_sem.at[2 + n]) for n in QUAD]
     for copy in store_o:
         copy.start()
-    for copy in [store_gx, store_gain] + store_gw + store_o:
+    drain(gw_buf, out_sem.at[6])
+    for copy in [store_gx, store_gain] + store_o:
         copy.wait()
 
 
@@ -1048,10 +1016,10 @@
             pltpu.VMEM((2, NSP, ROWS, HALF), F32), pltpu.VMEM((2, NSP, ROWS, HALF), F32),
             pltpu.VMEM((NSP, ROWS, HALF), F32), pltpu.VMEM((PEERS, ROWS, HALF), F32), pltpu.VMEM((PEERS, ROWS, HALF), F32),
             pltpu.VMEM((PEERS, BLK, QKV), BF16), pltpu.VMEM((PEERS, WIDTH, BLK), BF16), pltpu.VMEM((BLK, WIDTH), F32), pltpu.VMEM((BLK, WIDTH), BF16),
-            pltpu.VMEM((NSP, ROWS, QKV), F32), pltpu.VMEM((GROUP, SUB, TILE), F32), pltpu.VMEM((SUB, TILE), F32), pltpu.VMEM((PEERS, SUB, TILE), F32),
+            pltpu.VMEM((NSP, ROWS, QKV), F32), pltpu.VMEM((PEERS, NSP, 2, SUB, TILE), F32), pltpu.VMEM((PEERS, 2, SUB, TILE), F32), pltpu.VMEM((SUB, TILE), F32), pltpu.VMEM((SUB, TILE), F32), pltpu.VMEM((PEERS, SUB, TILE), F32),
             pltpu.VMEM(a_sum.shape, F32), pltpu.VMEM(b_sum.shape, F32), pltpu.VMEM((PEERS,) + a_sum.shape[1:], F32), pltpu.VMEM((PEERS,) + a_sum.shape[1:], F32),
             pltpu.VMEM((NSP, ROWS, BLK), F32), pltpu.VMEM((PEERS, ROWS, BLK), F32), pltpu.VMEM((NSP, ROWS, BLK), F32),
-            dma((SUB,)), dma((2,)), dma((PEERS,)), dma((18,))] + dma_sems((NSP, NSP), (NSP,), (NSP, 2), (2,), (NSP,), (NSP,), (2, NSP), (1,), (NSP,), (NSP,), (NSP,), (NSP,), (NSP,), (NSP, 2), (2,)),
+            dma((SUB,)), dma((2,)), dma((PEERS,)), dma((7,))] + dma_sems((PEERS, 2), (NSP,), (NSP, 2), (2,), (1,), (1,), (2, NSP), (PEERS,), (1,), (1,), (1,), (1,), (NSP,), (NSP, 2), (2,)),
         compiler_params=pltpu.CompilerParams(collective_id=PEERS, has_side_effects=True, vmem_limit_bytes=62 * MIB),
         cost_estimate=pl.CostEstimate(flops=60_000_000_000, bytes_accessed=60 * MIB, transcendentals=0),
         name='tail')(d_blocks, x_full, *[w.reshape(WIDTH, QKV) for w in weights], grad_y, a_sum, b_sum, dv_tok, tiles)

time: 265 us -> 259 us (0.977)
  Pallas kernels: 262 us -> 256 us
    pallas_call x1, Pallas kernels: 128 us -> 123 us  [forward_pass(): pl.pallas_call(fwd_kernel, out_shape=[jax.ShapeDtypeStruct((NSP, BLK, WID...]
where the time goes in v2:
time: 259 us
  Pallas kernels  256 us (99%)
    pallas_call x1, Pallas kernels, forward_pass(): pl.pallas_call(fwd_kernel, out_shape=[jax.ShapeDtypeStruct((NSP, BLK, WID...  123 us
    pallas_call x1, Pallas kernels, tail(): pl.pallas_call(tail_kernel, out_shape=[jax.ShapeDtypeStruct((BLK, WIDTH),...  76.8 us
    pallas_call x1, Pallas kernels, mid(): pl.pallas_call(mid_kernel, out_shape=[jax.ShapeDtypeStruct((NSP, BLK, QKV...  51.8 us

profile of v2, /device:TPU:0, one launch (start us, length us, event | category | flops | bytes accessed | tf_op | source)
XLA Modules:
  0.0 258.8 jit_solution(17961947198350148333)
XLA Ops:
  0.6 1.4 fusion.tile_hbm
  2.1 123.1 %forward.1 = (bf16[4,512,2048]{2,1,0:T(8,128)(2,1)}, bf16[4,512,512]{2,1,0:T(8,128)(2,1)}, bf16[4,512,512]{2,1,0:T(8,128)(2,1)}, bf16[4,512,512]{2,1,0:T(8,128)(...) custom-call(bf16[512,2048]{1,0:T(8,128)(2,1)} %bitcast.21, ...), custom_call_target="tpu_custom_call" | custom-call | flops 80000000000 | bytes 41943040 | tf_op jit(solution)/shard_map/forward/pallas_call | solution.py:481
  125.2 51.8 %middle.1 = (bf16[4,512,1536]{2,1,0:T(8,128)(2,1)}, f32[4,2,64,512]{3,2,1,0:T(8,128)}, f32[2,4,64,512]{3,2,1,0:T(8,128)}, bf16[4,512,512]{2,1,0:T(8,128)(2,1)}, f32[4,4,2,8,128]{4,3,2,1,0:T(8,128)}) custom-call(bf16[4,512,512]{2,1,0:T(8,128)(2,1)} %get-tuple-element.46.ot_hbm, bf16[512,2048]{1,0:T(8,128)(2,1)} %get-tuple-element.47.ga_hbm, ...), custom_call_target="tpu_custom_call" | custom-call | flops 60000002048 | bytes 33554432 | tf_op jit(solution)/shard_map/middle/pallas_call | solution.py:716
  177.0 76.8 %tail.1 = (bf16[512,2048]{1,0:T(8,128)(2,1)}, f32[64,2048]{1,0:T(8,128)}, f32[64,2048]{1,0:T(8,128)}, f32[64,2048]{1,0:T(8,128)}, f32[64,2048]{1,0:T(8,128)}, /*index=5*/f32[8,128]{1,0:T(8,128)}) custom-call(bf16[4,512,1536]{2,1,0:T(8,128)(2,1)} %get-tuple-element.59.d_hbm, bf16[2048,2048]{1,0:T(8,128)(2,1)} %bitcast.26, bf16[2048,1536]{1,0:T(8,128)(2,1)} %bitcast.27, ...), custom_call_target="tpu_custom_call" | custom-call | flops 60000002048 | bytes 62914560 | tf_op jit(solution)/shard_map/tail/pallas_call | solution.py:1008
  253.8 0.0 copy-start
  253.9 4.4 %deliver.1 = (bf16[512,2048]{1,0:T(8,128)(2,1)}, bf16[512,2048]{1,0:T(8,128)(2,1)}, f32[64,2048]{1,0:T(8,128)}, f32[64,2048]{1,0:T(8,128)}, f32[64,2048]{1,0:T(8,128)}, /*index=5*/f32[64,2048]{1,0:T(8,128)}) custom-call(bf16[512,2048]{1,0:T(8,128)(2,1)} %get-tuple-element.45.refs_0_, bf16[512,2048]{1,0:T(8,128)(2,1)} %get-tuple-element.69.refs_1_, ...), custom_call_target="tpu_custom_call" | custom-call | tf_op jit(solution)/shard_map/deliver/pallas_call | solution.py:1046
  258.2 0.0 copy-done
  258.2 0.1 constant_dynamic-slice_fusion
  258.3 0.5 slice_bitcast_fusion
Async XLA Ops:
  253.8 4.4 %copy-start = (f32[8,128]{1,0:T(8,128)S(1)}, f32[8,128]{1,0:T(8,128)}, u32[]{:S(2)}) copy-start(f32[8,128]{1,0:T(8,128)} %get-tuple-element.80) | copy-start | bytes 12292

commit v3 on v2

--- a/solution.py
+++ b/solution.py
@@ -35,6 +35,7 @@
 VMEM_LIMIT = 62 * 2 ** 20
 SUB = 8
 WIDE = 256
+DUAL = 2
 PEERS = 3
 PART = 16
 SIDES = (1, 3)
@@ -106,7 +107,7 @@
 
 
 def step_offset(t):
-    return jnp.where(t == 0, 2, jnp.where(t == 1, 1, jnp.where(t == 2, PEERS, 0)))
+    return jnp.where(t == 0, DUAL, jnp.where(t == 1, 1, jnp.where(t == DUAL, PEERS, 0)))
 
 
 def local_gains(gt_ref, grow):
@@ -156,7 +157,7 @@
 
 def gather_stages(buf, g, sems):
     sp, z, y, core = my_coords()
-    first, near, far, both = [(sems[2 * k].at[g], sems[2 * k + 1].at[g]) for k in range(NSP)]
+    first, near, far, both = [(sems[DUAL * k].at[g], sems[DUAL * k + 1].at[g]) for k in range(NSP)]
     low, high = pl.ds(0, GROUP), pl.ds(GROUP, GROUP)
     ways = tuple(enumerate((1, PEERS)))
 
@@ -216,14 +217,14 @@
     loop(BLK // ROWS, chunk)
 
 
-def fwd_kernel(x_hbm, gy_hbm, wq_hbm, wk_hbm, wv_hbm, wo_hbm, tile_hbm, ca_hbm, sa_hbm, cb_hbm, sb_hbm,
+def fwd_kernel(x_hbm, gy_hbm, wq_hbm, wk_hbm, wv_hbm, wo_hbm, gq_ref, gk_ref, gp_ref, ca_hbm, sa_hbm, cb_hbm, sb_hbm,
                xf_hbm, q0_hbm, k0_hbm, qr_hbm, kr_hbm, v_hbm, o_hbm, ot_hbm, lse_hbm, y_hbm, ga_hbm, ds_hbm, wl_hbm, wa_hbm, wb_hbm, wc_hbm,
                inv_hbm, gt_hbm, post_hbm,
                tile_ref, ca_ref, sa_ref, cb_ref, sb_ref, inv_ref, gt_ref, post_ref, xf, wl, wo, q0, k0, v, qr, kr, o, ot, lse, s_scr, vt_scr, cos_scr, sin_scr, st, st_in, grow, gpost, invc,
                ld_sem, out_sem, own_send, own_recv, fw_send, fw_recv, t_send, t_recv, u_send, u_recv, o_send, o_recv, *w_sems):
     sp, z, y, core = my_coords()
     right, left = ring_sp(1), ring_sp(PEERS)
-    far = mod4(sp + 2)
+    far = mod4(sp + DUAL)
     w_rows = (wq_hbm, wk_hbm, wv_hbm)
 
     def own_cols(d):
@@ -235,7 +236,7 @@
             loads.append(pltpu.make_async_copy(w_hbm.at[:, own_cols(g)], buf.at[z, y, core, :, pl.ds(m * BLK, BLK)], ld_sem.at[g * PEERS + m]))
     loads.append(pltpu.make_async_copy(wo_hbm, wo.at[z, y, core], ld_sem.at[12]))
     loads.append(pltpu.make_async_copy(x_hbm, xf.at[sp], ld_sem.at[13]))
-    for k, pair in enumerate(((tile_hbm, tile_ref), (ca_hbm, ca_ref), (sa_hbm, sa_ref), (cb_hbm, cb_ref), (sb_hbm, sb_ref))):
+    for k, pair in enumerate(((ca_hbm, ca_ref), (sa_hbm, sa_ref), (cb_hbm, cb_ref), (sb_hbm, sb_ref))):
         loads.insert(0, pltpu.make_async_copy(*pair, out_sem.at[k]))
     for load in loads:
         load.start()
@@ -247,7 +248,7 @@
     def own_x(side, c):
         return remote(x_hbm.at[chunk(c)], xf.at[sp, chunk(c)], own_send.at[side, c], own_recv.at[side, c], (right, left)[side])
 
-    for right_c, left_c in zip((0, 2, 1, PEERS), (1, PEERS, 0, 2)):
+    for right_c, left_c in zip((0, DUAL, 1, PEERS), (1, PEERS, 0, DUAL)):
         own_x(0, right_c).start()
         own_x(1, left_c).start()
 
@@ -255,7 +256,11 @@
         for peer in peers:
             remote(tiles, tiles, t_send.at[k], t_recv.at[k], peer).start()
 
-    for load in loads[:SUB]:
+    tile_ref[:, :] = jnp.zeros_like(tile_ref)
+    for m, vec in enumerate((gq_ref, gk_ref, gp_ref)):
+        for side in PAIR:
+            tile_ref[m:m + 1, side * ROWS:(side + 1) * ROWS] = vec[...].reshape(1, ROWS)
+    for load in loads[:7]:
         load.wait()
     stages = [gather_stages(buf, g, w_sems) for g, buf in enumerate((wl, wo, wa_hbm, wb_hbm, wc_hbm))]
 
@@ -266,7 +271,7 @@
         stages[g][1]()
 
     def relay(g):
-        stages[g][2]()
+        stages[g][DUAL]()
 
     def share(g):
         stages[g][PEERS]()
@@ -284,19 +289,19 @@
 
     def forward(side, i):
         block = mod4(sp + (PEERS, 1)[side])
-        piece = xf.at[block, chunk(2 * i + side)]
+        piece = xf.at[block, chunk(DUAL * i + side)]
         return remote(piece, piece, fw_send.at[side, i], fw_recv.at[side, i], (right, left)[side])
 
     def forward_x(i):
         for side in PAIR:
-            own_x(side, 2 * i + side).wait()
+            own_x(side, DUAL * i + side).wait()
             forward(side, i).start()
 
     forward_x(0)
     relay(0)
     drain(gt_ref.at[:, pl.ds(0, PEERS), 0], t_send.at[1], t_recv.at[1])
-    send_tiles(2, gt_ref.at[:, :, core], [partner()])
-    for load in loads[SUB:]:
+    send_tiles(DUAL, gt_ref.at[:, :, core], [partner()])
+    for load in loads[7:]:
         load.wait()
     for g in RING + (NSP,):
         begin(g)
@@ -315,7 +320,7 @@
             weight = wl[:, :, :, :, n * BLK:(n + 1) * BLK].reshape(WIDTH, BLK)
             out = jnp.dot(tokens, weight, preferred_element_type=F32).astype(BF16)
             dst[block, rows, :] = out
-            if n < 2:
+            if n < DUAL:
                 wide = out.astype(F32)
                 wide = wide * wide
                 part = (wide[:, :TILE] + wide[:, TILE:WIDE]) + (wide[:, WIDE:PEERS * TILE] + wide[:, PEERS * TILE:])
@@ -323,13 +328,13 @@
                 st[:, rows] = jnp.where(mine, row_sum(part.T), st[:, rows])
 
     def near(step):
-        k, i = step // 2, parity(step)
+        k, i = step // DUAL, parity(step)
         for side in PAIR:
-            @pl.when(k == 2 - side)
+            @pl.when(k == DUAL - side)
             def _():
-                own_x(side, 2 * i + 1 - side).wait()
-
-        project(mod4(sp + k + lax.select(k == 2, 1, 0)), i)
+                own_x(side, DUAL * i + 1 - side).wait()
+
+        project(mod4(sp + k + lax.select(k == DUAL, 1, 0)), i)
 
     def distant(i):
         for side in PAIR:
@@ -341,25 +346,23 @@
         stores.append(pltpu.make_async_copy(xf.at[mod4(sp + d)], xf_hbm.at[mod4(sp + d)], out_sem.at[5 + d]))
         stores[-1].start()
     relay(1)
-    for g in (2, PEERS, NSP):
+    for g in (DUAL, PEERS, NSP):
         pass_on(g)
-    loop(2, distant)
+    loop(DUAL, distant)
     stats = [remote(st, st_in.at[before(d)], u_send.at[before(d)], u_recv.at[before(d)], ring_sp(d)) for d in RING]
     for copy in stats:
         copy.start()
-    for i, (src, dst) in enumerate(((xf.at[far], xf_hbm.at[far]), (q0, q0_hbm), (k0, k0_hbm), (v, v_hbm))):
-        stores.append(pltpu.make_async_copy(src, dst, out_sem.at[i]))
-        stores[-1].start()
-    relay(2)
+    late = [pltpu.make_async_copy(src, dst, out_sem.at[i]) for i, (src, dst) in enumerate(((xf.at[far], xf_hbm.at[far]), (q0, q0_hbm), (k0, k0_hbm), (v, v_hbm)))]
+    relay(DUAL)
     share(1)
-    drain(gt_ref.at[:, :, 0], t_send.at[2], t_recv.at[2])
+    drain(gt_ref.at[:, :, 0], t_send.at[DUAL], t_recv.at[DUAL])
     local_gains(gt_ref, grow)
     lane = lax.broadcasted_iota(jnp.int32, (1, TILE), 1) < HALF_HEAD
     for i in range(WIDTH // TILE):
-        gpost[:, i * TILE:(i + 1) * TILE] = jnp.broadcast_to(jnp.where(lane, gt_ref[i // NSP, i % NSP, 0, 2:PEERS, :], gt_ref[i // NSP, i % NSP, 1, 2:PEERS, :]), (SUB, TILE))
+        gpost[:, i * TILE:(i + 1) * TILE] = jnp.broadcast_to(jnp.where(lane, gt_ref[i // NSP, i % NSP, 0, DUAL:PEERS, :], gt_ref[i // NSP, i % NSP, 1, DUAL:PEERS, :]), (SUB, TILE))
     for copy in stats:
         copy.wait()
-    total = (st[:, :] + st_in[0]) + (st_in[1] + st_in[2])
+    total = (st[:, :] + st_in[0]) + (st_in[1] + st_in[DUAL])
     inv_ref[:, :] = lax.rsqrt(total / WIDTH + RMS_EPSILON)
 
     inv_columns(inv_ref, invc)
@@ -380,7 +383,7 @@
         vt_scr[:, :] = v[:, :, lanes].reshape(SEQ, TILE).T
         for i in QUAD:
             q_i = qr[i, :, lanes]
-            buf = i % 2
+            buf = i % DUAL
             top = None
             for j in range(i + 1):
                 s = lax.dot_general(kr[j, :, lanes], q_i, NT, preferred_element_type=F32)
@@ -410,13 +413,15 @@
         return carry
 
     repeat(NSP, head)
+    for copy in late:
+        copy.start()
     for copy in stores:
         copy.wait()
     ot[sp] = o[sp]
     relay(PEERS)
     relay(NSP)
-    share(2)
-    last = [pltpu.make_async_copy(o, o_hbm, out_sem.at[0]), pltpu.make_async_copy(lse, lse_hbm, out_sem.at[1]),
+    share(DUAL)
+    last = [pltpu.make_async_copy(o, o_hbm, out_sem.at[13]), pltpu.make_async_copy(lse, lse_hbm, out_sem.at[14]),
             pltpu.make_async_copy(qr, qr_hbm, out_sem.at[6]), pltpu.make_async_copy(kr, kr_hbm, out_sem.at[7])]
     grad_in = pltpu.make_async_copy(gy_hbm, xf.at[mod4(sp + 1)], ld_sem.at[0])
     for copy in last + [grad_in]:
@@ -443,7 +448,9 @@
     share(PEERS)
     share(NSP)
     grad_in.wait()
-    last.append(pltpu.make_async_copy(ot, ot_hbm, out_sem.at[2]))
+    for copy in late:
+        copy.wait()
+    last.append(pltpu.make_async_copy(ot, ot_hbm, out_sem.at[DUAL]))
     last[-1].start()
     y_out, grad_a = xf.at[far], xf.at[mod4(sp + PEERS)]
     norm_and_grad(acc, xf.at[sp], xf.at[mod4(sp + 1)], gpost[0:1, :], y_out, grad_a, post_ref)
@@ -457,7 +464,7 @@
             v[s, :, pl.ds(pl.multiple_of(h * TILE, TILE), TILE)] = out[:, s * TILE:(s + 1) * TILE]
 
     loop(NSP, grad_attn)
-    gathered(2)
+    gathered(DUAL)
     gathered(PEERS)
     last.append(pltpu.make_async_copy(v, ds_hbm, out_sem.at[5]))
     last[-1].start()
@@ -470,27 +477,27 @@
     return [pltpu.SemaphoreType.DMA(shape) for shape in shapes for _ in PAIR]
 
 
-def forward_pass(x, grad_y, wq_rows, wk_rows, wv_rows, wo_rows, gain_tile, tables):
+def forward_pass(x, grad_y, wq_rows, wk_rows, wv_rows, wo_rows, vecs, tables):
     hbm = pl.BlockSpec(memory_space=pl.ANY)
     vmem = pl.BlockSpec(memory_space=pltpu.VMEM)
     quad = (NSP, BLK, BLK)
     wide = jax.ShapeDtypeStruct(quad, BF16)
     tokens = jax.ShapeDtypeStruct((BLK, WIDTH), BF16)
-    blocks = (NSP, NSP, 2, ROWS)
+    blocks = (NSP, NSP, DUAL, ROWS)
     weight = jax.ShapeDtypeStruct(blocks + (QKV,), BF16)
     return pl.pallas_call(
         fwd_kernel,
         out_shape=[jax.ShapeDtypeStruct((NSP, BLK, WIDTH), BF16)] + [wide] * 7 + [jax.ShapeDtypeStruct((NSP, SUB, SEQ), F32), tokens, tokens, wide] + [weight] * NSP + [
             jax.ShapeDtypeStruct((SUB, BLK), F32), jax.ShapeDtypeStruct(blocks[:PEERS] + (SUB, TILE), F32), jax.ShapeDtypeStruct((SUB, WIDTH), F32)],
-        in_specs=[hbm] * 11, out_specs=[hbm] * 19,
-        scratch_shapes=[pltpu.VMEM(a.shape, F32) for a in (gain_tile, *tables)] + [pltpu.VMEM((SUB, BLK), F32), pltpu.VMEM(blocks[:PEERS] + (SUB, TILE), F32), pltpu.VMEM((SUB, WIDTH), F32), pltpu.VMEM((NSP, BLK, WIDTH), BF16), pltpu.VMEM(blocks + (QKV,), BF16), pltpu.VMEM(blocks + (WIDTH,), BF16)] + [pltpu.VMEM(quad, BF16)] * 7 + [
-            pltpu.VMEM((NSP, SUB, SEQ), F32), pltpu.VMEM((2,) + quad, F32), pltpu.VMEM((TILE, SEQ), BF16),
+        in_specs=[hbm] * 6 + [vmem] * PEERS + [hbm] * NSP, out_specs=[hbm] * 19,
+        scratch_shapes=[pltpu.VMEM((SUB, TILE), F32)] + [pltpu.VMEM(a.shape, F32) for a in tables] + [pltpu.VMEM((SUB, BLK), F32), pltpu.VMEM(blocks[:PEERS] + (SUB, TILE), F32), pltpu.VMEM((SUB, WIDTH), F32), pltpu.VMEM((NSP, BLK, WIDTH), BF16), pltpu.VMEM(blocks + (QKV,), BF16), pltpu.VMEM(blocks + (WIDTH,), BF16)] + [pltpu.VMEM(quad, BF16)] * 7 + [
+            pltpu.VMEM((NSP, SUB, SEQ), F32), pltpu.VMEM((DUAL,) + quad, F32), pltpu.VMEM((TILE, SEQ), BF16),
             pltpu.VMEM((SEQ, TILE), F32), pltpu.VMEM((SEQ, TILE), F32), pltpu.VMEM((SUB, BLK), F32), pltpu.VMEM((PEERS, SUB, BLK), F32), pltpu.VMEM((SUB, BLK), F32),
-            pltpu.VMEM((SUB, WIDTH), F32), pltpu.VMEM((2, NSP, BLK, TILE), F32),
-            pltpu.SemaphoreType.DMA((14,)), pltpu.SemaphoreType.DMA((13,))] + dma_sems((2, NSP), (2, 2), (PEERS,), (PEERS,), (NSP,)) + gather_sems(5),
+            pltpu.VMEM((SUB, WIDTH), F32), pltpu.VMEM((DUAL, NSP, BLK, TILE), F32),
+            pltpu.SemaphoreType.DMA((14,)), pltpu.SemaphoreType.DMA((15,))] + dma_sems((DUAL, NSP), (DUAL, DUAL), (PEERS,), (PEERS,), (NSP,)) + gather_sems(5),
         compiler_params=pltpu.CompilerParams(collective_id=1, has_side_effects=True, vmem_limit_bytes=VMEM_LIMIT),
         cost_estimate=pl.CostEstimate(flops=80_000_000_000, bytes_accessed=40 * MIB, transcendentals=0),
-        name='forward')(x, grad_y, wq_rows, wk_rows, wv_rows, wo_rows, gain_tile, *tables)
+        name='forward')(x, grad_y, wq_rows, wk_rows, wv_rows, wo_rows, *vecs, *tables)
 
 
 def mid_kernel(ot_hbm, ga_hbm, ds_hbm, qr_hbm, kr_hbm, v_hbm, o_hbm, q0_hbm, k0_hbm, lse_hbm, inv_hbm, gt_hbm, post_hbm,
@@ -526,7 +533,7 @@
     for h in QUAD:
         for d in RING:
             send_do(h, d).start()
-    load_qk = group([(ds_hbm.at[sp], do.at[sp]), (qr_hbm, qa), (kr_hbm, ka), (v_hbm, va), (o_hbm, oa), (lse_hbm, lse), (q0_hbm, q0), (k0_hbm, k0)], in_sem.at[2])
+    load_qk = group([(ds_hbm.at[sp], do.at[sp]), (qr_hbm, qa), (kr_hbm, ka), (v_hbm, va), (o_hbm, oa), (lse_hbm, lse), (q0_hbm, q0), (k0_hbm, k0)], in_sem.at[DUAL])
     for copy in load_ot:
         copy.wait()
 
@@ -550,14 +557,14 @@
     def step_z(t):
         return mod4(z + step_offset(t))
 
-    low, high = pl.ds(0, 2), pl.ds(2, 2)
+    low, high = pl.ds(0, DUAL), pl.ds(DUAL, DUAL)
     ways = tuple(enumerate((1, PEERS)))
 
     def half_a(t, i, d):
-        return remote(chip.at[t, i, mod4(y + 2)], half_y.at[t, i], a1_send.at[t, i], a1_recv.at[t, i], ring_y(d))
+        return remote(chip.at[t, i, mod4(y + DUAL)], half_y.at[t, i], a1_send.at[t, i], a1_recv.at[t, i], ring_y(d))
 
     def half_b(k, i, d):
-        return remote(chip.at[0, 2 + i, k], half_z.at[k, i], b1_send.at[k, i], b1_recv.at[k, i], ring_z(d))
+        return remote(chip.at[0, DUAL + i, k], half_z.at[k, i], b1_send.at[k, i], b1_recv.at[k, i], ring_z(d))
 
     def sum_a(t, i, d):
         return remote(chip.at[t, low, mod4(y + d)], full_y.at[i, t], a2_send.at[0], a2_recv.at[0], ring_y(d))
@@ -570,22 +577,24 @@
             half_a(t, i, d).wait()
             chip[t, i, mod4(y + d)] += half_y[t, i]
             half_b(t, i, d).wait()
-            chip[1 + i, 2 + i, t] += half_z[t, i]
+            chip[1 + i, DUAL + i, t] += half_z[t, i]
         for i, d in ways:
             sum_a(t, i, d).start()
             sum_b(t, i, d).start()
 
-    send_grad.wait()
-    drain(otp, c_send.at[0], c_recv.at[0])
-
-    def wgrad(t):
+    def cols_of(n):
+        return slice(n * BLK, (n + 1) * BLK)
+
+    def wgrad_own(t):
         block = step_z(t)
         mine = jnp.concatenate([ott[block, core_rows(i, core), :] for i in QUAD], axis=0)
-        other = otp[block].reshape(NSP * ROWS, BLK)
         for n in QUAD:
-            cols = slice(n * BLK, (n + 1) * BLK)
-            part = jnp.dot(mine, ga[:, cols], preferred_element_type=F32) + jnp.dot(other, gap[:, cols], preferred_element_type=F32)
-            chip[t, n] = part.reshape(NSP, ROWS, BLK)
+            chip[t, n] = jnp.dot(mine, ga[:, cols_of(n)], preferred_element_type=F32).reshape(NSP, ROWS, BLK)
+
+    def wgrad(t):
+        other = otp[step_z(t)].reshape(NSP * ROWS, BLK)
+        for n in QUAD:
+            chip[t, n] += jnp.dot(other, gap[:, cols_of(n)], preferred_element_type=F32).reshape(NSP, ROWS, BLK)
         for i, d in ways:
             half_a(t, i, d).start()
 
@@ -595,6 +604,9 @@
                 for i, d in ways:
                     half_b(k, i, d).start()
 
+    loop(NSP, wgrad_own)
+    send_grad.wait()
+    drain(otp, c_send.at[0], c_recv.at[0])
     loop(NSP, wgrad)
     for copy in load_qk:
         copy.wait()
@@ -624,7 +636,7 @@
             delta = row_sum((do_i.astype(F32) * oa[i, :, lanes].astype(F32)).T)
             top = lse[h, 0:1, i * BLK:(i + 1) * BLK]
             dqt = None
-            tiles = [(j, 0, BLK, 0) for j in range(i)] + [(i, 0, BLK // 2, 0), (i, BLK // 2, BLK, BLK // 2)]
+            tiles = [(j, 0, BLK, 0) for j in range(i)] + [(i, 0, BLK // DUAL, 0), (i, BLK // DUAL, BLK, BLK // DUAL)]
             for j, start, stop, first in tiles:
                 keys = slice(start, stop)
                 s = lax.dot_general(ka[j, keys, lanes], q_i[first:], NT, preferred_element_type=F32)
@@ -664,13 +676,13 @@
         copy.start()
     for d in RING:
         send_dv(NSP - 1, d).start()
-    store_v = group([(va, d_hbm.at[:, :, block_cols(2)]), (va.at[sp], dvt_hbm.at[sp])], out_sem.at[1])
+    store_v = group([(va, d_hbm.at[:, :, block_cols(DUAL)]), (va.at[sp], dvt_hbm.at[sp])], out_sem.at[1])
 
     tile_ref[:, :, :] = jnp.zeros_like(tile_ref)
     for i in range(WIDTH // TILE):
         total = row_sum(post_ref[:, i * TILE:(i + 1) * TILE])
         for c in PAIR:
-            tile_ref[i // NSP, i % NSP, c, 2:PEERS, :] = total
+            tile_ref[i // NSP, i % NSP, c, DUAL:PEERS, :] = total
     for m in PAIR:
         for h in QUAD:
             total = row_sum(gacc[m, :, h * TILE:(h + 1) * TILE])
@@ -680,7 +692,7 @@
     store_v += group([(tile_ref, tile_hbm)], out_sem.at[PEERS])
     for copy in stats:
         copy.wait()
-    st[:, :] = ((st[:, :] + st_in[0]) + (st_in[1] + st_in[2])) / WIDTH
+    st[:, :] = ((st[:, :] + st_in[0]) + (st_in[1] + st_in[DUAL])) / WIDTH
     for m, ref in enumerate(kept):
         for i in QUAD:
             proj = jnp.broadcast_to(st[m * NSP + i:m * NSP + i + 1, :], (TILE, BLK)).T
@@ -688,7 +700,7 @@
                 lanes = slice(h * TILE, (h + 1) * TILE)
                 hat = ref[i, :, lanes].astype(F32) * invc[m, i]
                 ref[i, :, lanes] = (invc[m, i] * (big[m, i, :, lanes] - hat * proj)).astype(BF16)
-    store_d = group([(ref, d_hbm.at[:, :, block_cols(m)]) for m, ref in enumerate(kept)], out_sem.at[2])
+    store_d = group([(ref, d_hbm.at[:, :, block_cols(m)]) for m, ref in enumerate(kept)], out_sem.at[DUAL])
 
     drain(full_y, a2_send.at[0], a2_recv.at[0])
     drain(full_z, b2_send.at[0], b2_recv.at[0])
@@ -706,21 +718,21 @@
     vmem = pl.BlockSpec(memory_space=pltpu.VMEM)
     quad = (NSP, BLK, BLK)
     tokens = (BLK, WIDTH)
-    pair = (2, ROWS, BLK)
-    sems = dma_sems((NSP,), (2,), (NSP, 2), (NSP, 2), (1,), (1,), (PEERS,), (1,))
+    pair = (DUAL, ROWS, BLK)
+    sems = dma_sems((NSP,), (DUAL,), (NSP, DUAL), (NSP, DUAL), (1,), (1,), (PEERS,), (1,))
     half = [pltpu.VMEM(shape, BF16) for shape in (quad, tokens, tokens) + (quad,) * SUB + ((NSP, NSP, ROWS, BLK),)]
     scratch = half + [pltpu.VMEM(shape, F32) for shape in (
-        (2,) + quad, (NSP, NSP, NSP, ROWS, BLK), (NSP,) + pair, (NSP,) + pair, (2, NSP) + pair, (2, NSP) + pair,
-        (2, NSP, BLK, TILE), (SEQ, TILE), (SEQ, TILE), (NSP, BLK, TILE), (NSP, BLK, TILE))] + [pltpu.VMEM((TILE, SEQ), BF16)] + [
-        pltpu.VMEM(shape, F32) for shape in ((NSP, SUB, SEQ), (SUB, BLK), (2, SUB, BLK), (SUB, BLK), (PEERS, SUB, BLK))]
+        (DUAL,) + quad, (NSP, NSP, NSP, ROWS, BLK), (NSP,) + pair, (NSP,) + pair, (DUAL, NSP) + pair, (DUAL, NSP) + pair,
+        (DUAL, NSP, BLK, TILE), (SEQ, TILE), (SEQ, TILE), (NSP, BLK, TILE), (NSP, BLK, TILE))] + [pltpu.VMEM((TILE, SEQ), BF16)] + [
+        pltpu.VMEM(shape, F32) for shape in ((NSP, SUB, SEQ), (SUB, BLK), (DUAL, SUB, BLK), (SUB, BLK), (PEERS, SUB, BLK))]
     return pl.pallas_call(
         mid_kernel,
         out_shape=[jax.ShapeDtypeStruct((NSP, BLK, QKV), BF16),
-                   jax.ShapeDtypeStruct((NSP,) + pair, F32), jax.ShapeDtypeStruct((2, NSP, ROWS, BLK), F32), jax.ShapeDtypeStruct(quad, BF16),
+                   jax.ShapeDtypeStruct((NSP,) + pair, F32), jax.ShapeDtypeStruct((DUAL, NSP, ROWS, BLK), F32), jax.ShapeDtypeStruct(quad, BF16),
                    jax.ShapeDtypeStruct(gains.shape, F32)],
         in_specs=[hbm] * 17, out_specs=[hbm] * 5,
         scratch_shapes=[pltpu.VMEM(a.shape, F32) for a in (inv, gains, post, *tables, gains)] + scratch + [pltpu.SemaphoreType.DMA(shape) for shape in ((PEERS, SUB), (NSP, 5))] + sems,
-        compiler_params=pltpu.CompilerParams(collective_id=2, has_side_effects=True, vmem_limit_bytes=VMEM_LIMIT),
+        compiler_params=pltpu.CompilerParams(collective_id=DUAL, has_side_effects=True, vmem_limit_bytes=VMEM_LIMIT),
         cost_estimate=pl.CostEstimate(flops=60_000_000_000, bytes_accessed=WIDTH * WIDTH * SUB, transcendentals=0),
         name='middle')(o_tok, grad_a, grad_o, *heads, lse, inv, gains, post, *tables)
 
@@ -734,10 +746,10 @@
                 oa_send, oa_recv, ob_send, ob_recv, s_send, s_recv, f_send, f_recv, f1_send, f1_recv, f2_send, f2_recv):
     sp, z, y, core = my_coords()
 
-    load_o = [pltpu.make_async_copy(as_hbm, o_a, ld_sem.at[2]), pltpu.make_async_copy(bs_hbm, o_b, ld_sem.at[PEERS])]
+    load_o = [pltpu.make_async_copy(as_hbm, o_a, ld_sem.at[DUAL]), pltpu.make_async_copy(bs_hbm, o_b, ld_sem.at[PEERS])]
     load_d = pltpu.make_async_copy(d_hbm, d_loc, ld_sem.at[0])
     load_gy = pltpu.make_async_copy(gy_hbm, gy_buf, ld_sem.at[1])
-    load_v = [pltpu.make_async_copy(dvt_hbm.at[mod4(sp + NSP - d)], d_tok.at[before(d), :, pl.ds(2 * BLK, BLK)], ld_sem.at[PEERS + d]) for d in RING]
+    load_v = [pltpu.make_async_copy(dvt_hbm.at[mod4(sp + NSP - d)], d_tok.at[before(d), :, pl.ds(DUAL * BLK, BLK)], ld_sem.at[PEERS + d]) for d in RING]
     load_tile = pltpu.make_async_copy(tile_hbm, tile_ref, ld_sem.at[7])
     for load in [load_tile] + load_o + [load_d]:
         load.start()
@@ -751,10 +763,10 @@
     load_x(0).start()
 
     def source(k):
-        return jnp.where(k == 0, 0, jnp.where(k == 1, 1, jnp.where(k == 2, PEERS, 2)))
+        return jnp.where(k == 0, 0, jnp.where(k == 1, 1, jnp.where(k == DUAL, PEERS, DUAL)))
 
     def which(j):
-        return lax.rem(j + 2, PEERS)
+        return lax.rem(j + DUAL, PEERS)
 
     w_order = (wl_hbm, wc_hbm, wa_hbm, wb_hbm)
 
@@ -782,8 +794,8 @@
     start_w(1)
     for load in load_o:
         load.wait()
-    low, high = pl.ds(0, 2), pl.ds(2, 2)
-    o_sends = [remote(o_a.at[t], o_ra.at[t], oa_send.at[0], oa_recv.at[0], ring_z(d)) for t, d in enumerate((2, 1, PEERS))]
+    low, high = pl.ds(0, DUAL), pl.ds(DUAL, DUAL)
+    o_sends = [remote(o_a.at[t], o_ra.at[t], oa_send.at[0], oa_recv.at[0], ring_z(d)) for t, d in enumerate((DUAL, 1, PEERS))]
     o_sends += [remote(o_b.at[:, mod4(y + d)], o_rb.at[before(d)], ob_send.at[0], ob_recv.at[0], ring_y(d)) for d in RING]
     for copy in o_sends:
         copy.start()
@@ -796,11 +808,11 @@
     def send_core(t):
         return remote(part.at[parity(t), :, other_core(core)], chip.at[t], c_send.at[t], c_recv.at[t], partner())
 
-    quarter = HALF // 2
+    quarter = HALF // DUAL
     ways = tuple(enumerate((1, PEERS)))
 
     def half_a(t, i, d):
-        return remote(chip.at[t, mod4(y + 2), :, pl.ds(i * quarter, quarter)], half_y.at[t, i], a1_send.at[t, i], a1_recv.at[t, i], ring_y(d))
+        return remote(chip.at[t, mod4(y + DUAL), :, pl.ds(i * quarter, quarter)], half_y.at[t, i], a1_send.at[t, i], a1_recv.at[t, i], ring_y(d))
 
     def half_b(i, d):
         return remote(chip.at[0, :, :, pl.ds(HALF + i * quarter, quarter)], half_z.at[i], b1_send.at[i], b1_recv.at[i], ring_z(d))
@@ -844,7 +856,7 @@
         for n in TRIO:
             prod = lax.dot_general(x_col[parity(t)], d_loc[:, :, n * BLK:(n + 1) * BLK].reshape(WIDTH, BLK),
                                    (((0,), (0,)), ((), ())), preferred_element_type=F32)
-            part[parity(t), :, :, :, n * BLK:(n + 1) * BLK] = prod.reshape(NSP, 2, ROWS, BLK)
+            part[parity(t), :, :, :, n * BLK:(n + 1) * BLK] = prod.reshape(NSP, DUAL, ROWS, BLK)
         send_core(t).start()
 
         @pl.when(t > 0)
@@ -854,18 +866,18 @@
 
     repeat(NSP, wgrad_step)
     drain(tile_y, t_send.at[0], t_recv.at[0])
-    tile_ref[:, y] = (tile_ref[:, y] + tile_y[0]) + (tile_y[1] + tile_y[2])
+    tile_ref[:, y] = (tile_ref[:, y] + tile_y[0]) + (tile_y[1] + tile_y[DUAL])
     for d in RING:
         remote(tile_ref.at[mod4(z + d), y], tile_z.at[before(d)], t_send.at[1], t_recv.at[1], ring_z(d)).start()
     drain(o_ra, oa_send.at[0], oa_recv.at[0])
     drain(o_rb, ob_send.at[0], ob_recv.at[0])
-    fin[low] = (o_a[NSP - 1] + o_ra[0]) + (o_ra[1] + o_ra[2])
-    fin[high] = (o_b[:, y] + o_rb[0]) + (o_rb[1] + o_rb[2])
+    fin[low] = (o_a[NSP - 1] + o_ra[0]) + (o_ra[1] + o_ra[DUAL])
+    fin[high] = (o_b[:, y] + o_rb[0]) + (o_rb[1] + o_rb[DUAL])
     scatter = [remote(fin.at[mod4(sp + d)], rc.at[before(d)], s_send.at[0], s_recv.at[0], ring_sp(d)) for d in RING]
     for copy in scatter:
         copy.start()
     for m in PAIR:
-        send_d(2, m).start()
+        send_d(DUAL, m).start()
     pass_a(0)
     pass_a(1)
     for load in load_v + [load_gy]:
@@ -878,13 +890,13 @@
 
         @pl.when(j < 10)
         def _():
-            start_w(j + 2)
+            start_w(j + DUAL)
 
         def columns(n):
-            cols = pl.ds(pl.multiple_of(n * 2 * BLK, 2 * BLK), 2 * BLK)
+            cols = pl.ds(pl.multiple_of(n * DUAL * BLK, DUAL * BLK), DUAL * BLK)
             acc[:, cols] += lax.dot_general(block, w_buf[lax.rem(j, PEERS), cols, :], NT, preferred_element_type=F32)
 
-        loop(2, columns)
+        loop(DUAL, columns)
 
     def own_steps(i, carry):
         gx_step(0, i, d_loc[sp, :, pl.ds(pl.multiple_of(which(i) * BLK, BLK), BLK)])
@@ -894,10 +906,10 @@
 
     finish(PEERS)
     pass_b()
-    pass_a(2)
+    pass_a(DUAL)
     drain(tile_z, t_send.at[1], t_recv.at[1])
-    tile_ref[z, y] = (tile_ref[z, y] + tile_z[0]) + (tile_z[1] + tile_z[2])
-    remote(tile_ref.at[z, y, other_core(core)], tile_c, t_send.at[2], t_recv.at[2], partner()).start()
+    tile_ref[z, y] = (tile_ref[z, y] + tile_z[0]) + (tile_z[1] + tile_z[DUAL])
+    remote(tile_ref.at[z, y, other_core(core)], tile_c, t_send.at[DUAL], t_recv.at[DUAL], partner()).start()
     def remote_steps(k):
         d = source(k)
 
@@ -932,18 +944,18 @@
 
     def far_out(i, d):
         piece = fout.at[mod4(sp + NSP - d), pl.ds(i * GROUP, GROUP)]
-        return remote(piece, piece, f_send.at[2 + i], f_recv.at[2 + i], ring_sp(d))
+        return remote(piece, piece, f_send.at[DUAL + i], f_recv.at[DUAL + i], ring_sp(d))
 
     def far_gw(part, i, d):
         piece = gw_buf.at[mod4(sp + NSP - d), pl.ds(i * GROUP, GROUP), halves[part]]
-        return remote(piece, piece, g_send.at[part, 2 + i], g_recv.at[part, 2 + i], ring_sp(d))
+        return remote(piece, piece, g_send.at[part, DUAL + i], g_recv.at[part, DUAL + i], ring_sp(d))
 
     remote_steps(1)
     pass_a(PEERS)
     for t in TRIO:
         sum_a(t)
         send_a2(t).start()
-    remote_steps(2)
+    remote_steps(DUAL)
     for i, d in ways:
         full_b(i, d).wait()
     for i in QUAD:
@@ -952,20 +964,20 @@
         send_b2(d).start()
     sum_a(PEERS)
     drain(recv_a2, a2_send.at[0], a2_recv.at[0])
-    gw_buf[sp, :, :HALF] = (chip[PEERS, y, :, :HALF] + recv_a2[0]) + (recv_a2[1] + recv_a2[2])
+    gw_buf[sp, :, :HALF] = (chip[PEERS, y, :, :HALF] + recv_a2[0]) + (recv_a2[1] + recv_a2[DUAL])
     for i, d in ways:
         near_gw(0, i, d).start()
-    drain(tile_c, t_send.at[2], t_recv.at[2])
+    drain(tile_c, t_send.at[DUAL], t_recv.at[DUAL])
     gpart[...] = tile_ref[z, y, core] + tile_c[...]
     gain_sends = [remote(gpart, gacross.at[before(d)], u_send.at[0], u_recv.at[0], ring_sp(d)) for d in RING]
     for copy in gain_sends:
         copy.start()
     drain(recv_b2, b2_send.at[0], b2_recv.at[0])
-    gw_buf[sp, :, HALF:] = (sum_b[y] + recv_b2[0]) + (recv_b2[1] + recv_b2[2])
+    gw_buf[sp, :, HALF:] = (sum_b[y] + recv_b2[0]) + (recv_b2[1] + recv_b2[DUAL])
     for i, d in ways:
         near_gw(1, i, d).start()
     drain(rc, s_send.at[0], s_recv.at[0])
-    fout[sp] = (fin[sp] + rc[0]) + (rc[1] + rc[2])
+    fout[sp] = (fin[sp] + rc[0]) + (rc[1] + rc[DUAL])
     for i, d in ways:
         near_out(i, d).start()
     for part in PAIR:
@@ -981,7 +993,7 @@
     store_gx = pltpu.make_async_copy(gx_stage, gx_hbm, out_sem.at[0])
     store_gx.start()
     drain(gacross, u_send.at[0], u_recv.at[0])
-    gain_ref[...] = (gpart[...] + gacross[0]) + (gacross[1] + gacross[2])
+    gain_ref[...] = (gpart[...] + gacross[0]) + (gacross[1] + gacross[DUAL])
     store_gain = pltpu.make_async_copy(gain_ref, gain_hbm, out_sem.at[1])
     store_gain.start()
     for part in PAIR:
@@ -993,7 +1005,7 @@
         copy.start()
     for i, d in ways:
         far_out(i, d).wait()
-    store_o = [pltpu.make_async_copy(fout.at[n], gwo_hbm.at[:, pl.ds(n * BLK, BLK)], out_sem.at[2 + n]) for n in QUAD]
+    store_o = [pltpu.make_async_copy(fout.at[n], gwo_hbm.at[:, pl.ds(n * BLK, BLK)], out_sem.at[DUAL + n]) for n in QUAD]
     for copy in store_o:
         copy.start()
     drain(gw_buf, out_sem.at[6])
@@ -1011,23 +1023,23 @@
                    jax.ShapeDtypeStruct((SUB, TILE), F32)],
         in_specs=[hbm] * 11, out_specs=[hbm] * 6,
         scratch_shapes=[pltpu.VMEM(tiles.shape, F32), pltpu.VMEM((SUB, TILE), F32),
-            pltpu.VMEM((NSP, BLK, QKV), BF16), pltpu.VMEM((2, WIDTH, BLK), BF16), pltpu.VMEM((2, NSP, 2, ROWS, QKV), F32),
-            pltpu.VMEM((NSP, NSP, ROWS, QKV), F32), pltpu.VMEM((NSP, 2, ROWS, HALF // 2), F32), pltpu.VMEM((2, NSP, ROWS, HALF // 2), F32),
-            pltpu.VMEM((2, NSP, ROWS, HALF), F32), pltpu.VMEM((2, NSP, ROWS, HALF), F32),
+            pltpu.VMEM((NSP, BLK, QKV), BF16), pltpu.VMEM((DUAL, WIDTH, BLK), BF16), pltpu.VMEM((DUAL, NSP, DUAL, ROWS, QKV), F32),
+            pltpu.VMEM((NSP, NSP, ROWS, QKV), F32), pltpu.VMEM((NSP, DUAL, ROWS, HALF // DUAL), F32), pltpu.VMEM((DUAL, NSP, ROWS, HALF // DUAL), F32),
+            pltpu.VMEM((DUAL, NSP, ROWS, HALF), F32), pltpu.VMEM((DUAL, NSP, ROWS, HALF), F32),
             pltpu.VMEM((NSP, ROWS, HALF), F32), pltpu.VMEM((PEERS, ROWS, HALF), F32), pltpu.VMEM((PEERS, ROWS, HALF), F32),
             pltpu.VMEM((PEERS, BLK, QKV), BF16), pltpu.VMEM((PEERS, WIDTH, BLK), BF16), pltpu.VMEM((BLK, WIDTH), F32), pltpu.VMEM((BLK, WIDTH), BF16),
-            pltpu.VMEM((NSP, ROWS, QKV), F32), pltpu.VMEM((PEERS, NSP, 2, SUB, TILE), F32), pltpu.VMEM((PEERS, 2, SUB, TILE), F32), pltpu.VMEM((SUB, TILE), F32), pltpu.VMEM((SUB, TILE), F32), pltpu.VMEM((PEERS, SUB, TILE), F32),
+            pltpu.VMEM((NSP, ROWS, QKV), F32), pltpu.VMEM((PEERS, NSP, DUAL, SUB, TILE), F32), pltpu.VMEM((PEERS, DUAL, SUB, TILE), F32), pltpu.VMEM((SUB, TILE), F32), pltpu.VMEM((SUB, TILE), F32), pltpu.VMEM((PEERS, SUB, TILE), F32),
             pltpu.VMEM(a_sum.shape, F32), pltpu.VMEM(b_sum.shape, F32), pltpu.VMEM((PEERS,) + a_sum.shape[1:], F32), pltpu.VMEM((PEERS,) + a_sum.shape[1:], F32),
             pltpu.VMEM((NSP, ROWS, BLK), F32), pltpu.VMEM((PEERS, ROWS, BLK), F32), pltpu.VMEM((NSP, ROWS, BLK), F32),
-            dma((SUB,)), dma((2,)), dma((PEERS,)), dma((7,))] + dma_sems((PEERS, 2), (NSP,), (NSP, 2), (2,), (1,), (1,), (2, NSP), (PEERS,), (1,), (1,), (1,), (1,), (NSP,), (NSP, 2), (2,)),
+            dma((SUB,)), dma((DUAL,)), dma((PEERS,)), dma((7,))] + dma_sems((PEERS, DUAL), (NSP,), (NSP, DUAL), (DUAL,), (1,), (1,), (DUAL, NSP), (PEERS,), (1,), (1,), (1,), (1,), (NSP,), (NSP, DUAL), (DUAL,)),
         compiler_params=pltpu.CompilerParams(collective_id=PEERS, has_side_effects=True, vmem_limit_bytes=62 * MIB),
         cost_estimate=pl.CostEstimate(flops=60_000_000_000, bytes_accessed=60 * MIB, transcendentals=0),
         name='tail')(d_blocks, x_full, *[w.reshape(WIDTH, QKV) for w in weights], grad_y, a_sum, b_sum, dv_tok, tiles)
 
 
 def deliver_kernel(*refs):
-    count = (len(refs) - 2) // PEERS
-    sources, results, held = refs[:count], refs[count:2 * count], refs[2 * count:PEERS * count]
+    count = (len(refs) - DUAL) // PEERS
+    sources, results, held = refs[:count], refs[count:DUAL * count], refs[DUAL * count:PEERS * count]
     in_sem, out_sem = refs[PEERS * count:]
     loads = [pltpu.make_async_copy(src, buf, in_sem.at[i]) for i, (src, buf) in enumerate(zip(sources, held))]
     stores = [pltpu.make_async_copy(buf, dst, out_sem.at[i]) for i, (buf, dst) in enumerate(zip(held, results))]
@@ -1042,14 +1054,14 @@
 
 def deliver(*arrays):
     hbm = [pl.BlockSpec(memory_space=pl.ANY)] * len(arrays)
-    sems = [pltpu.SemaphoreType.DMA((len(arrays),))] * 2
+    sems = [pltpu.SemaphoreType.DMA((len(arrays),))] * DUAL
     return pl.pallas_call(
         deliver_kernel, out_shape=[jax.ShapeDtypeStruct(a.shape, a.dtype) for a in arrays], in_specs=hbm, out_specs=hbm,
         scratch_shapes=[pltpu.VMEM(a.shape, a.dtype) for a in arrays] + sems, name='deliver')(*arrays)
 
 
 def solution(mesh):
-    grid_mesh = Mesh(mesh.devices.reshape(NSP, NSP, NSP, 2), ('sp',) + FS)
+    grid_mesh = Mesh(mesh.devices.reshape(NSP, NSP, NSP, DUAL), ('sp',) + FS)
     tok_spec = P(FS, 'sp', None)
     row_spec = P(FS, None)
     vec_spec = P(FS)
@@ -1062,17 +1074,16 @@
     def local_step(x, grad_y, wq_rows, wk_rows, wv_rows, wo_rows, gq_rows, gk_rows, gpost_rows):
         x = x.reshape(BLK, WIDTH)
         grad_y = grad_y.reshape(BLK, WIDTH)
-        vecs = jnp.stack([gq_rows, gk_rows, gpost_rows])
-        gain_tile = jnp.pad(jnp.concatenate([vecs, vecs], axis=1), ((0, 5), (0, 0)))
+        vecs = (gq_rows, gk_rows, gpost_rows)
         w_rows = (wq_rows, wk_rows, wv_rows)
         x_full, q0, k0, q_rot, k_rot, v, o_heads, o_tok, lse, y, grad_a, grad_o, w_own, w_next, w_far, w_prev, inv, gains, post = forward_pass(
-            x, grad_y, *w_rows, wo_rows, gain_tile, tables)
+            x, grad_y, *w_rows, wo_rows, vecs, tables)
         d_blocks, a_sum, b_sum, dv_tok, tiles = mid(
             o_tok, grad_a, grad_o, (q_rot, k_rot, v, o_heads, q0, k0), lse, inv, gains, post, tables)
         grad_x, *grad_w, gain_grads = tail(d_blocks, x_full.reshape(WIDTH, WIDTH), (w_own, w_next, w_far, w_prev), grad_y, a_sum, b_sum, dv_tok, tiles)
         y, grad_x, *grad_w = deliver(y, grad_x, *grad_w)
         gain_grads = lax.dynamic_slice_in_dim(gain_grads, lax.axis_index('core') * ROWS, ROWS, axis=1)
-        return (y.reshape(1, BLK, WIDTH), grad_x.reshape(1, BLK, WIDTH), *grad_w, gain_grads[0], gain_grads[1], gain_grads[2])
+        return (y.reshape(1, BLK, WIDTH), grad_x.reshape(1, BLK, WIDTH), *grad_w, gain_grads[0], gain_grads[1], gain_grads[DUAL])
 
     return jax.shard_map(local_step, mesh=grid_mesh,
                          in_specs=(tok_spec, tok_spec, row_spec, row_spec, row_spec, row_spec, vec_spec, vec_spec, vec_spec),

time: 259 us -> 258 us (level)
  no operation moved by 1% of the time
where the time goes in v3:
time: 258 us
  Pallas kernels  257 us (100%)
    pallas_call x1, Pallas kernels, forward_pass(): pl.pallas_call(fwd_kernel, out_shape=[jax.ShapeDtypeStruct((NSP, BLK, WID...  124 us
    pallas_call x1, Pallas kernels, tail(): pl.pallas_call(tail_kernel, out_shape=[jax.ShapeDtypeStruct((BLK, WIDTH),...  76.9 us
    pallas_call x1, Pallas kernels, mid(): pl.pallas_call(mid_kernel, out_shape=[jax.ShapeDtypeStruct((NSP, BLK, QKV...  51.7 us

profile of v3, /device:TPU:0, one launch (start us, length us, event | category | flops | bytes accessed | tf_op | source)
XLA Modules:
  0.0 258.3 jit_solution(18208437997229904448)
XLA Ops:
  0.6 124.0 %forward.1 = (bf16[4,512,2048]{2,1,0:T(8,128)(2,1)}, bf16[4,512,512]{2,1,0:T(8,128)(2,1)}, bf16[4,512,512]{2,1,0:T(8,128)(2,1)}, bf16[4,512,512]{2,1,0:T(8,128)(...) custom-call(bf16[512,2048]{1,0:T(8,128)(2,1)} %bitcast.15, ...), custom_call_target="tpu_custom_call" | custom-call | flops 80000000000 | bytes 41943040 | tf_op jit(solution)/shard_map/forward/pallas_call | solution.py:488
  124.6 51.7 %middle.1 = (bf16[4,512,1536]{2,1,0:T(8,128)(2,1)}, f32[4,2,64,512]{3,2,1,0:T(8,128)}, f32[2,4,64,512]{3,2,1,0:T(8,128)}, bf16[4,512,512]{2,1,0:T(8,128)(2,1)}, f32[4,4,2,8,128]{4,3,2,1,0:T(8,128)}) custom-call(bf16[4,512,512]{2,1,0:T(8,128)(2,1)} %get-tuple-element.46.ot_hbm, bf16[512,2048]{1,0:T(8,128)(2,1)} %get-tuple-element.47.ga_hbm, ...), custom_call_target="tpu_custom_call" | custom-call | flops 60000002048 | bytes 33554432 | tf_op jit(solution)/shard_map/middle/pallas_call | solution.py:728
  176.4 76.9 %tail.1 = (bf16[512,2048]{1,0:T(8,128)(2,1)}, f32[64,2048]{1,0:T(8,128)}, f32[64,2048]{1,0:T(8,128)}, f32[64,2048]{1,0:T(8,128)}, f32[64,2048]{1,0:T(8,128)}, /*index=5*/f32[8,128]{1,0:T(8,128)}) custom-call(bf16[4,512,1536]{2,1,0:T(8,128)(2,1)} %get-tuple-element.59.d_hbm, bf16[2048,2048]{1,0:T(8,128)(2,1)} %bitcast.20, bf16[2048,1536]{1,0:T(8,128)(2,1)} %bitcast.21, ...), custom_call_target="tpu_custom_call" | custom-call | flops 60000002048 | bytes 62914560 | tf_op jit(solution)/shard_map/tail/pallas_call | solution.py:1020
  253.3 0.0 copy-start
  253.3 4.4 %deliver.1 = (bf16[512,2048]{1,0:T(8,128)(2,1)}, bf16[512,2048]{1,0:T(8,128)(2,1)}, f32[64,2048]{1,0:T(8,128)}, f32[64,2048]{1,0:T(8,128)}, f32[64,2048]{1,0:T(8,128)}, /*index=5*/f32[64,2048]{1,0:T(8,128)}) custom-call(bf16[512,2048]{1,0:T(8,128)(2,1)} %get-tuple-element.45.refs_0_, bf16[512,2048]{1,0:T(8,128)(2,1)} %get-tuple-element.69.refs_1_, ...), custom_call_target="tpu_custom_call" | custom-call | tf_op jit(solution)/shard_map/deliver/pallas_call | solution.py:1058
  257.7 0.0 copy-done
  257.7 0.1 constant_dynamic-slice_fusion
  257.7 0.5 slice_bitcast_fusion
Async XLA Ops:
  253.3 4.4 %copy-start = (f32[8,128]{1,0:T(8,128)S(1)}, f32[8,128]{1,0:T(8,128)}, u32[]{:S(2)}) copy-start(f32[8,128]{1,0:T(8,128)} %get-tuple-element.80) | copy-start | bytes 12292

commit v4 on v3

--- a/solution.py
+++ b/solution.py
@@ -309,6 +309,7 @@
     forward_x(1)
     pass_on(1)
     gathered(0)
+    pass_on(DUAL)
     stores = [pltpu.make_async_copy(wl, wl_hbm, out_sem.at[NSP])]
     stores[0].start()
     st[:, :] = jnp.zeros_like(st)
@@ -346,7 +347,7 @@
         stores.append(pltpu.make_async_copy(xf.at[mod4(sp + d)], xf_hbm.at[mod4(sp + d)], out_sem.at[5 + d]))
         stores[-1].start()
     relay(1)
-    for g in (DUAL, PEERS, NSP):
+    for g in (PEERS, NSP):
         pass_on(g)
     loop(DUAL, distant)
     stats = [remote(st, st_in.at[before(d)], u_send.at[before(d)], u_recv.at[before(d)], ring_sp(d)) for d in RING]
@@ -366,6 +367,7 @@
     inv_ref[:, :] = lax.rsqrt(total / WIDTH + RMS_EPSILON)
 
     inv_columns(inv_ref, invc)
+    relay(PEERS)
     row = lax.broadcasted_iota(jnp.int32, (BLK, BLK), 0)
     col = lax.broadcasted_iota(jnp.int32, (BLK, BLK), 1)
 
@@ -418,9 +420,9 @@
     for copy in stores:
         copy.wait()
     ot[sp] = o[sp]
-    relay(PEERS)
     relay(NSP)
     share(DUAL)
+    share(PEERS)
     last = [pltpu.make_async_copy(o, o_hbm, out_sem.at[13]), pltpu.make_async_copy(lse, lse_hbm, out_sem.at[14]),
             pltpu.make_async_copy(qr, qr_hbm, out_sem.at[6]), pltpu.make_async_copy(kr, kr_hbm, out_sem.at[7])]
     grad_in = pltpu.make_async_copy(gy_hbm, xf.at[mod4(sp + 1)], ld_sem.at[0])
@@ -445,7 +447,6 @@
                 acc[n] += part
 
     loop(NSP, project_out)
-    share(PEERS)
     share(NSP)
     grad_in.wait()
     for copy in late:

time: 258 us -> 257 us (level)
  no operation moved by 1% of the time
where the time goes in v4:
time: 257 us
  Pallas kernels  256 us (100%)
    pallas_call x1, Pallas kernels, forward_pass(): pl.pallas_call(fwd_kernel, out_shape=[jax.ShapeDtypeStruct((NSP, BLK, WID...  126 us
    pallas_call x1, Pallas kernels, tail(): pl.pallas_call(tail_kernel, out_shape=[jax.ShapeDtypeStruct((BLK, WIDTH),...  75.1 us
    pallas_call x1, Pallas kernels, mid(): pl.pallas_call(mid_kernel, out_shape=[jax.ShapeDtypeStruct((NSP, BLK, QKV...  49.8 us

profile of v4, /device:TPU:0, one launch (start us, length us, event | category | flops | bytes accessed | tf_op | source)
XLA Modules:
  0.0 257.0 jit_solution(12245038959106121780)
XLA Ops:
  0.6 126.4 %forward.1 = (bf16[4,512,2048]{2,1,0:T(8,128)(2,1)}, bf16[4,512,512]{2,1,0:T(8,128)(2,1)}, bf16[4,512,512]{2,1,0:T(8,128)(2,1)}, bf16[4,512,512]{2,1,0:T(8,128)(...) custom-call(bf16[512,2048]{1,0:T(8,128)(2,1)} %bitcast.15, ...), custom_call_target="tpu_custom_call" | custom-call | flops 80000000000 | bytes 41943040 | tf_op jit(solution)/shard_map/forward/pallas_call | solution.py:489
  127.1 49.8 %middle.1 = (bf16[4,512,1536]{2,1,0:T(8,128)(2,1)}, f32[4,2,64,512]{3,2,1,0:T(8,128)}, f32[2,4,64,512]{3,2,1,0:T(8,128)}, bf16[4,512,512]{2,1,0:T(8,128)(2,1)}, f32[4,4,2,8,128]{4,3,2,1,0:T(8,128)}) custom-call(bf16[4,512,512]{2,1,0:T(8,128)(2,1)} %get-tuple-element.46.ot_hbm, bf16[512,2048]{1,0:T(8,128)(2,1)} %get-tuple-element.47.ga_hbm, ...), custom_call_target="tpu_custom_call" | custom-call | flops 60000002048 | bytes 33554432 | tf_op jit(solution)/shard_map/middle/pallas_call | solution.py:729
  176.9 75.1 %tail.1 = (bf16[512,2048]{1,0:T(8,128)(2,1)}, f32[64,2048]{1,0:T(8,128)}, f32[64,2048]{1,0:T(8,128)}, f32[64,2048]{1,0:T(8,128)}, f32[64,2048]{1,0:T(8,128)}, /*index=5*/f32[8,128]{1,0:T(8,128)}) custom-call(bf16[4,512,1536]{2,1,0:T(8,128)(2,1)} %get-tuple-element.59.d_hbm, bf16[2048,2048]{1,0:T(8,128)(2,1)} %bitcast.20, bf16[2048,1536]{1,0:T(8,128)(2,1)} %bitcast.21, ...), custom_call_target="tpu_custom_call" | custom-call | flops 60000002048 | bytes 62914560 | tf_op jit(solution)/shard_map/tail/pallas_call | solution.py:1021
  252.0 0.0 copy-start
  252.1 4.4 %deliver.1 = (bf16[512,2048]{1,0:T(8,128)(2,1)}, bf16[512,2048]{1,0:T(8,128)(2,1)}, f32[64,2048]{1,0:T(8,128)}, f32[64,2048]{1,0:T(8,128)}, f32[64,2048]{1,0:T(8,128)}, /*index=5*/f32[64,2048]{1,0:T(8,128)}) custom-call(bf16[512,2048]{1,0:T(8,128)(2,1)} %get-tuple-element.45.refs_0_, bf16[512,2048]{1,0:T(8,128)(2,1)} %get-tuple-element.69.refs_1_, ...), custom_call_target="tpu_custom_call" | custom-call | tf_op jit(solution)/shard_map/deliver/pallas_call | solution.py:1059
  256.4 0.0 copy-done
  256.4 0.1 constant_dynamic-slice_fusion
  256.5 0.5 slice_bitcast_fusion
Async XLA Ops:
  252.0 4.4 %copy-start = (f32[8,128]{1,0:T(8,128)S(1)}, f32[8,128]{1,0:T(8,128)}, u32[]{:S(2)}) copy-start(f32[8,128]{1,0:T(8,128)} %get-tuple-element.80) | copy-start | bytes 12292

commit v5 on v4

--- a/solution.py
+++ b/solution.py
@@ -218,10 +218,10 @@
 
 
 def fwd_kernel(x_hbm, gy_hbm, wq_hbm, wk_hbm, wv_hbm, wo_hbm, gq_ref, gk_ref, gp_ref, ca_hbm, sa_hbm, cb_hbm, sb_hbm,
-               xf_hbm, q0_hbm, k0_hbm, qr_hbm, kr_hbm, v_hbm, o_hbm, ot_hbm, lse_hbm, y_hbm, ga_hbm, ds_hbm, wl_hbm, wa_hbm, wb_hbm, wc_hbm,
+               xf_hbm, q0_hbm, k0_hbm, qr_hbm, kr_hbm, v_hbm, o_hbm, ot_hbm, lse_hbm, y_hbm, ga_hbm, ds_hbm, do_hbm, wl_hbm, wa_hbm, wb_hbm, wc_hbm,
                inv_hbm, gt_hbm, post_hbm,
                tile_ref, ca_ref, sa_ref, cb_ref, sb_ref, inv_ref, gt_ref, post_ref, xf, wl, wo, q0, k0, v, qr, kr, o, ot, lse, s_scr, vt_scr, cos_scr, sin_scr, st, st_in, grow, gpost, invc,
-               ld_sem, out_sem, own_send, own_recv, fw_send, fw_recv, t_send, t_recv, u_send, u_recv, o_send, o_recv, *w_sems):
+               ld_sem, out_sem, own_send, own_recv, fw_send, fw_recv, t_send, t_recv, u_send, u_recv, o_send, o_recv, b_send, b_recv, *w_sems):
     sp, z, y, core = my_coords()
     right, left = ring_sp(1), ring_sp(PEERS)
     far = mod4(sp + DUAL)
@@ -464,12 +464,19 @@
         for s in QUAD:
             v[s, :, pl.ds(pl.multiple_of(h * TILE, TILE), TILE)] = out[:, s * TILE:(s + 1) * TILE]
 
+        @pl.when(h == 0)
+        def _():
+            for d in RING:
+                remote(v.at[mod4(sp + d), :, pl.ds(0, TILE)], do_hbm.at[sp], b_send.at[0], b_recv.at[0], ring_sp(d)).start()
+
     loop(NSP, grad_attn)
     gathered(DUAL)
     gathered(PEERS)
-    last.append(pltpu.make_async_copy(v, ds_hbm, out_sem.at[5]))
-    last[-1].start()
+    last += [pltpu.make_async_copy(v, ds_hbm, out_sem.at[5]), pltpu.make_async_copy(v.at[sp, :, pl.ds(0, TILE)], do_hbm.at[sp], out_sem.at[0])]
+    for copy in last[-DUAL:]:
+        copy.start()
     gathered(NSP)
+    drain(do_hbm.at[pl.ds(0, PEERS)], b_send.at[0], b_recv.at[0])
     for copy in last:
         copy.wait()
 
@@ -488,20 +495,20 @@
     weight = jax.ShapeDtypeStruct(blocks + (QKV,), BF16)
     return pl.pallas_call(
         fwd_kernel,
-        out_shape=[jax.ShapeDtypeStruct((NSP, BLK, WIDTH), BF16)] + [wide] * 7 + [jax.ShapeDtypeStruct((NSP, SUB, SEQ), F32), tokens, tokens, wide] + [weight] * NSP + [
+        out_shape=[jax.ShapeDtypeStruct((NSP, BLK, WIDTH), BF16)] + [wide] * 7 + [jax.ShapeDtypeStruct((NSP, SUB, SEQ), F32), tokens, tokens, wide, jax.ShapeDtypeStruct((NSP, BLK, TILE), BF16)] + [weight] * NSP + [
             jax.ShapeDtypeStruct((SUB, BLK), F32), jax.ShapeDtypeStruct(blocks[:PEERS] + (SUB, TILE), F32), jax.ShapeDtypeStruct((SUB, WIDTH), F32)],
-        in_specs=[hbm] * 6 + [vmem] * PEERS + [hbm] * NSP, out_specs=[hbm] * 19,
+        in_specs=[hbm] * 6 + [vmem] * PEERS + [hbm] * NSP, out_specs=[hbm] * 20,
         scratch_shapes=[pltpu.VMEM((SUB, TILE), F32)] + [pltpu.VMEM(a.shape, F32) for a in tables] + [pltpu.VMEM((SUB, BLK), F32), pltpu.VMEM(blocks[:PEERS] + (SUB, TILE), F32), pltpu.VMEM((SUB, WIDTH), F32), pltpu.VMEM((NSP, BLK, WIDTH), BF16), pltpu.VMEM(blocks + (QKV,), BF16), pltpu.VMEM(blocks + (WIDTH,), BF16)] + [pltpu.VMEM(quad, BF16)] * 7 + [
             pltpu.VMEM((NSP, SUB, SEQ), F32), pltpu.VMEM((DUAL,) + quad, F32), pltpu.VMEM((TILE, SEQ), BF16),
             pltpu.VMEM((SEQ, TILE), F32), pltpu.VMEM((SEQ, TILE), F32), pltpu.VMEM((SUB, BLK), F32), pltpu.VMEM((PEERS, SUB, BLK), F32), pltpu.VMEM((SUB, BLK), F32),
             pltpu.VMEM((SUB, WIDTH), F32), pltpu.VMEM((DUAL, NSP, BLK, TILE), F32),
-            pltpu.SemaphoreType.DMA((14,)), pltpu.SemaphoreType.DMA((15,))] + dma_sems((DUAL, NSP), (DUAL, DUAL), (PEERS,), (PEERS,), (NSP,)) + gather_sems(5),
+            pltpu.SemaphoreType.DMA((14,)), pltpu.SemaphoreType.DMA((15,))] + dma_sems((DUAL, NSP), (DUAL, DUAL), (PEERS,), (PEERS,), (NSP,), (1,)) + gather_sems(5),
         compiler_params=pltpu.CompilerParams(collective_id=1, has_side_effects=True, vmem_limit_bytes=VMEM_LIMIT),
         cost_estimate=pl.CostEstimate(flops=80_000_000_000, bytes_accessed=40 * MIB, transcendentals=0),
         name='forward')(x, grad_y, wq_rows, wk_rows, wv_rows, wo_rows, *vecs, *tables)
 
 
-def mid_kernel(ot_hbm, ga_hbm, ds_hbm, qr_hbm, kr_hbm, v_hbm, o_hbm, q0_hbm, k0_hbm, lse_hbm, inv_hbm, gt_hbm, post_hbm,
+def mid_kernel(ot_hbm, ga_hbm, ds_hbm, do_hbm, qr_hbm, kr_hbm, v_hbm, o_hbm, q0_hbm, k0_hbm, lse_hbm, inv_hbm, gt_hbm, post_hbm,
                ca_hbm, sa_hbm, cb_hbm, sb_hbm, d_hbm, as_hbm, bs_hbm, dvt_hbm, tile_hbm,
                inv_ref, gt_ref, post_ref, ca_ref, sa_ref, cb_ref, sb_ref, tile_ref, ot, ga, gap, ott, do, qa, ka, va, oa, q0, k0, otp, big, chip, half_y, half_z, full_y, full_z, invc, cos_scr, sin_scr,
                dk_scr, dv_scr, kt_scr, lse, grow, gacc, st, st_in,
@@ -515,14 +522,14 @@
     def lanes_of(h):
         return pl.ds(pl.multiple_of(h * TILE, TILE), TILE)
 
-    def group(pairs, sem):
-        copies = [pltpu.make_async_copy(src, dst, sem.at[i]) for i, (src, dst) in enumerate(pairs)]
+    def group(pairs, sem, first):
+        copies = [pltpu.make_async_copy(src, dst, sem.at[first + i]) for i, (src, dst) in enumerate(pairs)]
         for copy in copies:
             copy.start()
         return copies
 
-    load_ot = group([(ot_hbm, ot), (ga_hbm, ga)], in_sem.at[0])
-    load_aux = group(((inv_hbm, inv_ref), (gt_hbm, gt_ref), (post_hbm, post_ref), (ca_hbm, ca_ref), (sa_hbm, sa_ref), (cb_hbm, cb_ref), (sb_hbm, sb_ref)), in_sem.at[1])
+    load_ot = group([(ot_hbm, ot), (ga_hbm, ga)], in_sem, 0)
+    load_aux = group(((inv_hbm, inv_ref), (gt_hbm, gt_ref), (post_hbm, post_ref), (ca_hbm, ca_ref), (sa_hbm, sa_ref), (cb_hbm, cb_ref), (sb_hbm, sb_ref)), in_sem, DUAL)
 
     greet((ring_sp, ring_z, ring_y))
 
@@ -531,10 +538,10 @@
 
     send_grad = remote(ga_hbm, gap, c_send.at[1], c_recv.at[1], partner())
     send_grad.start()
-    for h in QUAD:
+    for h in RING:
         for d in RING:
             send_do(h, d).start()
-    load_qk = group([(ds_hbm.at[sp], do.at[sp]), (qr_hbm, qa), (kr_hbm, ka), (v_hbm, va), (o_hbm, oa), (lse_hbm, lse), (q0_hbm, q0), (k0_hbm, k0)], in_sem.at[DUAL])
+    load_qk = group([(ds_hbm.at[sp, :, pl.ds(TILE, PEERS * TILE)], do.at[sp, :, pl.ds(TILE, PEERS * TILE)]), (do_hbm, do.at[:, :, pl.ds(0, TILE)]), (qr_hbm, qa), (kr_hbm, ka), (v_hbm, va), (o_hbm, oa), (lse_hbm, lse), (q0_hbm, q0), (k0_hbm, k0)], in_sem, 9)
     for copy in load_ot:
         copy.wait()
 
@@ -624,10 +631,10 @@
 
     def head(h):
         lanes = lanes_of(h)
-        drain(do.at[pl.ds(0, PEERS), :, lanes], do_send.at[h], do_recv.at[h])
 
         @pl.when(h > 0)
         def _():
+            drain(do.at[pl.ds(0, PEERS), :, lanes], do_send.at[h], do_recv.at[h])
             for d in RING:
                 send_dv(h - 1, d).start()
 
@@ -677,7 +684,7 @@
         copy.start()
     for d in RING:
         send_dv(NSP - 1, d).start()
-    store_v = group([(va, d_hbm.at[:, :, block_cols(DUAL)]), (va.at[sp], dvt_hbm.at[sp])], out_sem.at[1])
+    store_v = group([(va, d_hbm.at[:, :, block_cols(DUAL)]), (va.at[sp], dvt_hbm.at[sp])], out_sem, 5)
 
     tile_ref[:, :, :] = jnp.zeros_like(tile_ref)
     for i in range(WIDTH // TILE):
@@ -690,7 +697,7 @@
             for c in PAIR:
                 tile_ref[sp, h, c, m:m + 1, :] = total
 
-    store_v += group([(tile_ref, tile_hbm)], out_sem.at[PEERS])
+    store_v += group([(tile_ref, tile_hbm)], out_sem, 9)
     for copy in stats:
         copy.wait()
     st[:, :] = ((st[:, :] + st_in[0]) + (st_in[1] + st_in[DUAL])) / WIDTH
@@ -701,20 +708,20 @@
                 lanes = slice(h * TILE, (h + 1) * TILE)
                 hat = ref[i, :, lanes].astype(F32) * invc[m, i]
                 ref[i, :, lanes] = (invc[m, i] * (big[m, i, :, lanes] - hat * proj)).astype(BF16)
-    store_d = group([(ref, d_hbm.at[:, :, block_cols(m)]) for m, ref in enumerate(kept)], out_sem.at[DUAL])
+    store_d = group([(ref, d_hbm.at[:, :, block_cols(m)]) for m, ref in enumerate(kept)], out_sem, 7)
 
     drain(full_y, a2_send.at[0], a2_recv.at[0])
     drain(full_z, b2_send.at[0], b2_recv.at[0])
     for t in QUAD:
         chip[t, low, y] += full_y[0, t] + full_y[1, t]
         chip[NSP - 1, high, t] += full_z[0, t] + full_z[1, t]
-    store_w = group([(chip.at[t, low, y], as_hbm.at[t]) for t in QUAD] + [(chip.at[NSP - 1, high], bs_hbm)], out_sem.at[0])
+    store_w = group([(chip.at[t, low, y], as_hbm.at[t]) for t in QUAD] + [(chip.at[NSP - 1, high], bs_hbm)], out_sem, 0)
     drain(dvt_hbm.at[pl.ds(0, PEERS)], v_send.at[0], v_recv.at[0])
     for copy in store_v + store_d + store_w:
         copy.wait()
 
 
-def mid(o_tok, grad_a, grad_o, heads, lse, inv, gains, post, tables):
+def mid(o_tok, grad_a, grad_o, grad_first, heads, lse, inv, gains, post, tables):
     hbm = pl.BlockSpec(memory_space=pl.ANY)
     vmem = pl.BlockSpec(memory_space=pltpu.VMEM)
     quad = (NSP, BLK, BLK)
@@ -731,11 +738,11 @@
         out_shape=[jax.ShapeDtypeStruct((NSP, BLK, QKV), BF16),
                    jax.ShapeDtypeStruct((NSP,) + pair, F32), jax.ShapeDtypeStruct((DUAL, NSP, ROWS, BLK), F32), jax.ShapeDtypeStruct(quad, BF16),
                    jax.ShapeDtypeStruct(gains.shape, F32)],
-        in_specs=[hbm] * 17, out_specs=[hbm] * 5,
-        scratch_shapes=[pltpu.VMEM(a.shape, F32) for a in (inv, gains, post, *tables, gains)] + scratch + [pltpu.SemaphoreType.DMA(shape) for shape in ((PEERS, SUB), (NSP, 5))] + sems,
+        in_specs=[hbm] * 18, out_specs=[hbm] * 5,
+        scratch_shapes=[pltpu.VMEM(a.shape, F32) for a in (inv, gains, post, *tables, gains)] + scratch + [pltpu.SemaphoreType.DMA(shape) for shape in ((18,), (10,))] + sems,
         compiler_params=pltpu.CompilerParams(collective_id=DUAL, has_side_effects=True, vmem_limit_bytes=VMEM_LIMIT),
         cost_estimate=pl.CostEstimate(flops=60_000_000_000, bytes_accessed=WIDTH * WIDTH * SUB, transcendentals=0),
-        name='middle')(o_tok, grad_a, grad_o, *heads, lse, inv, gains, post, *tables)
+        name='middle')(o_tok, grad_a, grad_o, grad_first, *heads, lse, inv, gains, post, *tables)
 
 
 def tail_kernel(d_hbm, x_hbm, wl_hbm, wa_hbm, wb_hbm, wc_hbm, gy_hbm, as_hbm, bs_hbm, dvt_hbm, tile_hbm,
@@ -1077,10 +1084,10 @@
         grad_y = grad_y.reshape(BLK, WIDTH)
         vecs = (gq_rows, gk_rows, gpost_rows)
         w_rows = (wq_rows, wk_rows, wv_rows)
-        x_full, q0, k0, q_rot, k_rot, v, o_heads, o_tok, lse, y, grad_a, grad_o, w_own, w_next, w_far, w_prev, inv, gains, post = forward_pass(
+        x_full, q0, k0, q_rot, k_rot, v, o_heads, o_tok, lse, y, grad_a, grad_o, grad_first, w_own, w_next, w_far, w_prev, inv, gains, post = forward_pass(
             x, grad_y, *w_rows, wo_rows, vecs, tables)
         d_blocks, a_sum, b_sum, dv_tok, tiles = mid(
-            o_tok, grad_a, grad_o, (q_rot, k_rot, v, o_heads, q0, k0), lse, inv, gains, post, tables)
+            o_tok, grad_a, grad_o, grad_first, (q_rot, k_rot, v, o_heads, q0, k0), lse, inv, gains, post, tables)
         grad_x, *grad_w, gain_grads = tail(d_blocks, x_full.reshape(WIDTH, WIDTH), (w_own, w_next, w_far, w_prev), grad_y, a_sum, b_sum, dv_tok, tiles)
         y, grad_x, *grad_w = deliver(y, grad_x, *grad_w)
         gain_grads = lax.dynamic_slice_in_dim(gain_grads, lax.axis_index('core') * ROWS, ROWS, axis=1)

time: 257 us -> 257 us (level)
  no operation moved by 1% of the time
where the time goes in v5:
time: 257 us
  Pallas kernels  256 us (100%)
    pallas_call x1, Pallas kernels, forward_pass(): pl.pallas_call(fwd_kernel, out_shape=[jax.ShapeDtypeStruct((NSP, BLK, WID...  128 us
    pallas_call x1, Pallas kernels, tail(): pl.pallas_call(tail_kernel, out_shape=[jax.ShapeDtypeStruct((BLK, WIDTH),...  76 us
    pallas_call x1, Pallas kernels, mid(): pl.pallas_call(mid_kernel, out_shape=[jax.ShapeDtypeStruct((NSP, BLK, QKV...  47.5 us

profile of v5, /device:TPU:0, one launch (start us, length us, event | category | flops | bytes accessed | tf_op | source)
XLA Modules:
  0.0 256.9 jit_solution(2882154828068921892)
XLA Ops:
  0.6 127.7 %forward.1 = (bf16[4,512,2048]{2,1,0:T(8,128)(2,1)}, bf16[4,512,512]{2,1,0:T(8,128)(2,1)}, bf16[4,512,512]{2,1,0:T(8,128)(2,1)}, bf16[4,512,512]{2,1,0:T(8,128)(...) custom-call(bf16[512,2048]{1,0:T(8,128)(2,1)} %bitcast.15, ...), custom_call_target="tpu_custom_call" | custom-call | flops 80000000000 | bytes 41943040 | tf_op jit(solution)/shard_map/forward/pallas_call | solution.py:496
  128.3 47.5 %middle.1 = (bf16[4,512,1536]{2,1,0:T(8,128)(2,1)}, f32[4,2,64,512]{3,2,1,0:T(8,128)}, f32[2,4,64,512]{3,2,1,0:T(8,128)}, bf16[4,512,512]{2,1,0:T(8,128)(2,1)}, f32[4,4,2,8,128]{4,3,2,1,0:T(8,128)}) custom-call(bf16[4,512,512]{2,1,0:T(8,128)(2,1)} %get-tuple-element.47.ot_hbm, bf16[512,2048]{1,0:T(8,128)(2,1)} %get-tuple-element.48.ga_hbm, ...), custom_call_target="tpu_custom_call" | custom-call | flops 60000002048 | bytes 33554432 | tf_op jit(solution)/shard_map/middle/pallas_call | solution.py:736
  175.9 76.0 %tail.1 = (bf16[512,2048]{1,0:T(8,128)(2,1)}, f32[64,2048]{1,0:T(8,128)}, f32[64,2048]{1,0:T(8,128)}, f32[64,2048]{1,0:T(8,128)}, f32[64,2048]{1,0:T(8,128)}, /*index=5*/f32[8,128]{1,0:T(8,128)}) custom-call(bf16[4,512,1536]{2,1,0:T(8,128)(2,1)} %get-tuple-element.61.d_hbm, bf16[2048,2048]{1,0:T(8,128)(2,1)} %bitcast.20, bf16[2048,1536]{1,0:T(8,128)(2,1)} %bitcast.21, ...), custom_call_target="tpu_custom_call" | custom-call | flops 60000002048 | bytes 62914560 | tf_op jit(solution)/shard_map/tail/pallas_call | solution.py:1028
  251.9 0.0 copy-start
  251.9 4.4 %deliver.1 = (bf16[512,2048]{1,0:T(8,128)(2,1)}, bf16[512,2048]{1,0:T(8,128)(2,1)}, f32[64,2048]{1,0:T(8,128)}, f32[64,2048]{1,0:T(8,128)}, f32[64,2048]{1,0:T(8,128)}, /*index=5*/f32[64,2048]{1,0:T(8,128)}) custom-call(bf16[512,2048]{1,0:T(8,128)(2,1)} %get-tuple-element.46.refs_0_, bf16[512,2048]{1,0:T(8,128)(2,1)} %get-tuple-element.71.refs_1_, ...), custom_call_target="tpu_custom_call" | custom-call | tf_op jit(solution)/shard_map/deliver/pallas_call | solution.py:1066
  256.3 0.0 copy-done
  256.3 0.1 constant_dynamic-slice_fusion
  256.4 0.5 slice_bitcast_fusion
Async XLA Ops:
  251.9 4.4 %copy-start = (f32[8,128]{1,0:T(8,128)S(1)}, f32[8,128]{1,0:T(8,128)}, u32[]{:S(2)}) copy-start(f32[8,128]{1,0:T(8,128)} %get-tuple-element.82) | copy-start | bytes 12292
